TPU v7x, 8 devices: a whole 2x2x1 slice. The times are simulated.
8 devices in a mesh: data: 8 (over z, y, x, core).
Axes of the slice: x: 2, y: 2, z: 1, core: 2. Of those that a mesh axis runs over, the one named last changes fastest.
Arguments:
- feat_a: bfloat16 [8192, 2048], P('data')
- feat_b: bfloat16 [8192, 2048], P('data')
- w_in: bfloat16 [2048, 4096], replicated
- w_mid: bfloat16 [4096, 4096], replicated
- w_out: bfloat16 [4096, 4096], replicated
- t_in: bfloat16 [2048, 4096], replicated
- t_mid: bfloat16 [4096, 4096], replicated
- t_out: bfloat16 [4096, 4096], replicated
- gain_1: float32 [4096], replicated
- bias_1: float32 [4096], replicated
- gain_2: float32 [4096], replicated
- bias_2: float32 [4096], replicated
- off_weight: float32 [], replicated
Outputs:
- output 1: float32 [], replicated
- output 2: float32 [8192, 4096], P('data')
- output 3: float32 [2048, 4096], replicated
- output 4: float32 [4096, 4096], replicated
- output 5: float32 [4096, 4096], replicated
- output 6: float32 [4096], replicated
- output 7: float32 [4096], replicated
- output 8: float32 [4096], replicated
- output 9: float32 [4096], replicated
All inputs are finite; a program needn't handle non-finite values.
Results may differ from a plain program's by a relative error of at most 0.00515.
Values are sent between devices in bfloat16 or wider.
A program may use at most 1.5 GiB of HBM per device.

v0:
```python
import jax
import jax.numpy as jnp
from jax import lax
from jax.sharding import PartitionSpec as P

NORM_EPS = 1e-5
DATA_AXIS = "data"


def contract_rows(left_op, right_op):
    return lax.dot_general(left_op, right_op, (((0,), (0,)), ((), ())), preferred_element_type=jnp.float32)


def contract_cols(left_op, right_op):
    return lax.dot_general(left_op, right_op, (((1,), (1,)), ((), ())), preferred_element_type=jnp.float32)


def solution(mesh):
    shards = mesh.shape[DATA_AXIS]
    row_part = P(DATA_AXIS, None)
    replicated = P()

    def local_step(feat_a, feat_b, w_in, w_mid, w_out, t_in, t_mid, t_out, gain_1, bias_1, gain_2, bias_2, off_weight):
        row_count = feat_a.shape[0] * shards

        def norm_pair(pre_a, pre_b):
            stat_sums = jnp.stack([jnp.sum(pre_a, axis=0), jnp.sum(pre_a * pre_a, axis=0), jnp.sum(pre_b, axis=0), jnp.sum(pre_b * pre_b, axis=0)])
            stat_means = lax.psum(stat_sums, DATA_AXIS) / row_count
            inv_a = lax.rsqrt(stat_means[1] - stat_means[0] * stat_means[0] + NORM_EPS)
            inv_b = lax.rsqrt(stat_means[3] - stat_means[2] * stat_means[2] + NORM_EPS)
            return (pre_a - stat_means[0]) * inv_a, inv_a, (pre_b - stat_means[2]) * inv_b

        def hidden_pair(in_a, in_b, weight_a, weight_b, gain_vec, bias_vec):
            normed_a, inv_a, normed_b = norm_pair(jnp.dot(in_a, weight_a, preferred_element_type=jnp.float32), jnp.dot(in_b, weight_b, preferred_element_type=jnp.float32))
            pre_act = normed_a * gain_vec + bias_vec
            act_a = jnp.maximum(pre_act, 0.0).astype(jnp.bfloat16)
            act_b = jnp.maximum(normed_b * gain_vec + bias_vec, 0.0).astype(jnp.bfloat16)
            return act_a, act_b, normed_a, inv_a, pre_act > 0.0

        def norm_back(grad_n, normed, inv_std):
            stat_means = lax.psum(jnp.stack([jnp.sum(grad_n, axis=0), jnp.sum(grad_n * normed, axis=0)]), DATA_AXIS) / row_count
            return (grad_n - stat_means[0] - normed * stat_means[1]) * inv_std

        def affine_back(grad_pre, normed, inv_std, gain_vec):
            stat_sums = lax.psum(jnp.stack([jnp.sum(grad_pre * normed, axis=0), jnp.sum(grad_pre, axis=0)]), DATA_AXIS)
            grad_u = (grad_pre - stat_sums[1] / row_count - normed * (stat_sums[0] / row_count)) * (gain_vec * inv_std)
            return grad_u.astype(jnp.bfloat16), stat_sums[0], stat_sums[1]

        act_1, teach_1, normed_1, inv_1, mask_1 = hidden_pair(feat_a, feat_b, w_in, t_in, gain_1, bias_1)
        act_2, teach_2, normed_2, inv_2, mask_2 = hidden_pair(act_1, teach_1, w_mid, t_mid, gain_2, bias_2)
        zh_a, inv_z, zh_b = norm_pair(jnp.dot(act_2, w_out, preferred_element_type=jnp.float32), jnp.dot(teach_2, t_out, preferred_element_type=jnp.float32))
        emb_a = zh_a.astype(jnp.bfloat16)
        emb_b = zh_b.astype(jnp.bfloat16)
        corr_mat = lax.psum(contract_rows(emb_a, emb_b), DATA_AXIS) / row_count
        proj_width = corr_mat.shape[0]
        on_diag = lax.broadcasted_iota(jnp.int32, (proj_width, proj_width), 0) == lax.broadcasted_iota(jnp.int32, (proj_width, proj_width), 1)
        loss_value = jnp.sum(jnp.where(on_diag, jnp.square(1.0 - corr_mat), off_weight * jnp.square(corr_mat)))
        grad_c = jnp.where(on_diag, -2.0 * (1.0 - corr_mat), 2.0 * off_weight * corr_mat).astype(jnp.bfloat16)
        grad_emb = contract_cols(emb_b, grad_c) / row_count
        grad_z = norm_back(grad_emb, zh_a, inv_z).astype(jnp.bfloat16)
        grad_w_out = contract_rows(act_2, grad_z)
        grad_pre_2 = jnp.where(mask_2, contract_cols(grad_z, w_out), 0.0)
        grad_u_2, grad_gain_2, grad_bias_2 = affine_back(grad_pre_2, normed_2, inv_2, gain_2)
        grad_w_mid = contract_rows(act_1, grad_u_2)
        grad_pre_1 = jnp.where(mask_1, contract_cols(grad_u_2, w_mid), 0.0)
        grad_u_1, grad_gain_1, grad_bias_1 = affine_back(grad_pre_1, normed_1, inv_1, gain_1)
        grad_w_in = contract_rows(feat_a, grad_u_1)
        weight_grads = lax.psum((grad_w_in, grad_w_mid, grad_w_out), DATA_AXIS)
        return (loss_value, grad_emb, weight_grads[0], weight_grads[1], weight_grads[2], grad_gain_1, grad_bias_1, grad_gain_2, grad_bias_2)

    return jax.shard_map(local_step, mesh=mesh, in_specs=(row_part, row_part) + (replicated,) * 11, out_specs=(replicated, row_part) + (replicated,) * 7, check_vma=False)
```

profile of v0, /device:TPU:0, one launch (start us, length us, event | category | flops | bytes accessed | tf_op | source)
XLA Modules:
  0.0 3445.4 jit_solution(9355714230158222410)
XLA Ops:
  7.2 23.7 fusion.47
  31.0 21.3 fusion.46
  52.3 0.7 pad_maximum_fusion
  53.1 0.3 all-reduce.10.cloned.1.call-start
  53.3 44.7 %all-reduce.8.cloned.1.call-done = f32[4,4096]{1,0:T(4,128)} async-done(((f32[4,4096]{1,0:T(4,128)}), f32[4,4096]{1,0:T(4,128)}) %all-reduce.8.cloned.1.call-update) | async-done | bytes 65552 | tf_op jit(solution)/shard_map/psum | solution.py:28
  98.0 0.9 broadcast_multiply_fusion.2
  98.8 0.7 fusion.48
  99.5 45.7 %fusion.45 = (f32[4096]{0:T(1024)S(1)}, f32[4096]{0:T(1024)S(1)}, f32[1024,4096]{1,0:T(8,128)}) fusion(bf16[4096,4096]{1,0:T(8,128)(2,1)} %param.19, f32[1024,4096]{1,0:T(8,128)} %get-tuple-element.62, f32[4096]{0:T(1024)S(1)} %bitcast.89, f32[4096]{0:T(1024)S(1)} %bitcast.90, f32[4096]{0:T(1024)S(1)} %copy-done.23, f32[4096]{0:T(1024)S(1)} %copy-done.15), kind=kOutput, calls=%fused_computation.94 | convolution fusion | flops 34397478912 | bytes 67207168 | tf_op jit(solution)/shard_map/dot_general | solution.py:34
  145.3 45.9 %fusion.44 = (f32[4096]{0:T(1024)S(1)}, f32[4096]{0:T(1024)S(1)}, f32[1024,4096]{1,0:T(8,128)}) fusion(bf16[4096,4096]{1,0:T(8,128)(2,1)} %param.16, f32[1024,4096]{1,0:T(8,128)} %get-tuple-element.63, f32[4096]{0:T(1024)S(1)} %copy-done.23, f32[4096]{0:T(1024)S(1)} %copy-done.15, f32[4096]{0:T(1024)S(1)} %bitcast.85, f32[4096]{0:T(1024)S(1)} %bitcast.78), kind=kOutput, calls=%fused_computation.93 | convolution fusion | flops 34397478912 | bytes 67207168 | tf_op jit(solution)/shard_map/dot_general | solution.py:34
  191.2 0.7 pad_maximum_fusion.1
  191.9 0.0 all-reduce.12.cloned.1.call-start
  192.0 41.4 %all-reduce.10.cloned.1.call-done = f32[4,4096]{1,0:T(4,128)} async-done(((f32[4,4096]{1,0:T(4,128)}), f32[4,4096]{1,0:T(4,128)}) %all-reduce.10.cloned.1.call-update) | async-done | bytes 65552 | tf_op jit(solution)/shard_map/psum | solution.py:28
  233.4 0.9 broadcast_multiply_fusion.1
  234.3 0.7 fusion.49
  235.0 46.2 %fusion.43 = (f32[4096]{0:T(1024)S(1)}, f32[4096]{0:T(1024)S(1)}, f32[1024,4096]{1,0:T(8,128)}) fusion(bf16[4096,4096]{1,0:T(8,128)(2,1)} %param.20, f32[1024,4096]{1,0:T(8,128)} %get-tuple-element.64, f32[4096]{0:T(1024)S(1)} %bitcast.91, f32[4096]{0:T(1024)S(1)} %bitcast.92, f32[4096]{0:T(1024)S(1)} %copy-done.25, f32[4096]{0:T(1024)S(1)} %copy-done.18), kind=kOutput, calls=%fused_computation.92 | convolution fusion | flops 34397478912 | bytes 67207168 | tf_op jit(solution)/shard_map/dot_general | solution.py:51
  281.1 45.9 %fusion.42 = (f32[4096]{0:T(1024)S(1)}, f32[4096]{0:T(1024)S(1)}, f32[1024,4096]{1,0:T(8,128)}) fusion(bf16[4096,4096]{1,0:T(8,128)(2,1)} %param.17, f32[1024,4096]{1,0:T(8,128)} %get-tuple-element.65, f32[4096]{0:T(1024)S(1)} %copy-done.25, f32[4096]{0:T(1024)S(1)} %copy-done.18, f32[4096]{0:T(1024)S(1)} %bitcast.72, f32[4096]{0:T(1024)S(1)} %bitcast.59), kind=kOutput, calls=%fused_computation.91 | convolution fusion | flops 34397478912 | bytes 67207168 | tf_op jit(solution)/shard_map/dot_general | solution.py:51
  327.0 0.7 pad_maximum_fusion.2
  327.7 0.0 all-reduce.14.cloned.1.call-start
  327.8 41.4 %all-reduce.12.cloned.1.call-done = f32[4,4096]{1,0:T(4,128)} async-done(((f32[4,4096]{1,0:T(4,128)}), f32[4,4096]{1,0:T(4,128)}) %all-reduce.12.cloned.1.call-update) | async-done | bytes 65552 | tf_op jit(solution)/shard_map/psum | solution.py:28
  369.2 0.9 broadcast_multiply_fusion
  370.1 0.1 fusion.50
  370.2 47.1 %fusion.3 = f32[4096,4096]{1,0:T(8,128)} fusion(f32[1024,4096]{1,0:T(8,128)} %get-tuple-element.67, f32[4096]{0:T(1024)S(1)} %bitcast.66, f32[4096]{0:T(1024)S(1)} %bitcast.69, f32[1024,4096]{1,0:T(8,128)} %get-tuple-element.66, f32[4096]{0:T(1024)S(1)} %bitcast.107, f32[4096]{0:T(1024)S(1)} %bitcast.105), kind=kOutput, calls=%fused_computation.31 | convolution fusion | flops 34384904192 | bytes 100728832 | tf_op jit(solution)/shard_map/dot_general | solution.py:11
  417.3 0.0 all-reduce.18.cloned.1.call-start
  418.1 0.6 rsqrt_multiply_fusion
  418.7 0.6 rsqrt_multiply_fusion.1
  419.3 744.3 %all-reduce.14.cloned.1.call-done = f32[4096,4096]{1,0:T(8,128)} async-done(((f32[4096,4096]{1,0:T(8,128)}), f32[4096,4096]{1,0:T(8,128)}) %all-reduce.14.cloned.1.call-update) | async-done | bytes 67108880 | tf_op jit(solution)/shard_map/psum | solution.py:54
  1163.6 48.7 %fusion.41 = (f32[4096]{0:T(1024)S(1)}, f32[4096]{0:T(1024)S(1)}, f32[1024,4096]{1,0:T(8,128)}) fusion(f32[4096]{0:T(1024)S(1)} %bitcast.67, f32[1024,4096]{1,0:T(8,128)} %get-tuple-element.67, f32[4096]{0:T(1024)S(1)} %bitcast.70, f32[4096,4096]{1,0:T(8,128)} %all-reduce.14.cloned.1.call-done, f32[]{:T(128)S(6)} %mul.261, ...), kind=kOutput, calls=%fused_computation.90 | convolution fusion | flops 34514919424 | bytes 117538816 | tf_op jit(solution)/shard_map/dot_general | solution.py:15
  1212.4 22.4 psum.74
  1234.8 15.9 multiply_convert_fusion.2
  1250.8 2.5 copy-done
  1253.3 45.2 %multiply_reduce_fusion.1 = (f32[4096]{0:T(1024)S(1)}, f32[4096]{0:T(1024)S(1)}, f32[1024,4096]{1,0:T(8,128)}) fusion(f32[1024,4096]{1,0:T(8,128)S(1)} %copy-done, f32[4096]{0:T(1024)S(1)} %bitcast.73, f32[4096]{0:T(1024)S(1)} %bitcast.61, bf16[1024,4096]{1,0:T(8,128)(2,1)} %multiply_convert_fusion.2, bf16[4096,4096]{1,0:T(8,128)(2,1)} %param.17, ...), kind=kOutput, calls=%fused_computation.8 | convolution fusion | flops 34397478912 | bytes 75595776 | tf_op jit(solution)/shard_map/dot_general | solution.py:15
  1298.6 24.3 psum.75
  1322.9 0.7 fusion.51
  1323.6 12.2 multiply_convert_fusion.1
  1335.7 3.4 copy-done.1
  1339.1 43.3 %multiply_reduce_fusion = (f32[4096]{0:T(1024)S(1)}, f32[4096]{0:T(1024)S(1)}, f32[1024,4096]{1,0:T(8,128)}) fusion(f32[1024,4096]{1,0:T(8,128)} %get-tuple-element.63, f32[4096]{0:T(1024)S(1)} %bitcast.86, f32[4096]{0:T(1024)S(1)} %bitcast.80, bf16[1024,4096]{1,0:T(8,128)(2,1)S(1)} %multiply_convert_fusion.1, bf16[4096,4096]{1,0:T(8,128)(2,1)} %param.16, ...), kind=kOutput, calls=%fused_computation.6 | convolution fusion | flops 34397478912 | bytes 75595776 | tf_op jit(solution)/shard_map/dot_general | solution.py:15
  1382.5 46.8 %fusion.37 = f32[4096,4096]{1,0:T(8,128)} fusion(bf16[1024,4096]{1,0:T(8,128)(2,1)} %copy-done.1, f32[1024,4096]{1,0:T(8,128)} %get-tuple-element.63, f32[4096]{0:T(1024)S(1)} %copy-done.24, f32[4096]{0:T(1024)S(1)} %copy-done.17, f32[4096]{0:T(1024)S(1)} %bitcast.87, f32[4096]{0:T(1024)S(1)} %bitcast.81), kind=kOutput, calls=%fused_computation.86 | convolution fusion | flops 34384904192 | bytes 92340224 | tf_op jit(solution)/shard_map/dot_general | solution.py:11
  1429.3 23.4 psum.76
  1452.7 0.7 fusion.52
  1453.4 32.6 convolution_bitcast_fusion
  1486.0 0.6 copy-done.3
  1486.7 47.0 %fusion.39 = f32[4096,4096]{1,0:T(8,128)} fusion(bf16[1024,4096]{1,0:T(8,128)(2,1)} %multiply_convert_fusion.2, f32[1024,4096]{1,0:T(8,128)} %get-tuple-element.65, f32[4096]{0:T(1024)S(1)} %copy-done.27, f32[4096]{0:T(1024)S(1)} %copy-done.19, f32[4096]{0:T(1024)S(1)} %bitcast.75, f32[4096]{0:T(1024)S(1)} %bitcast.63), kind=kOutput, calls=%fused_computation.88 | convolution fusion | flops 34384904192 | bytes 92340224 | tf_op jit(solution)/shard_map/dot_general | solution.py:11
  1533.8 22.1 select_reduce_fusion
  1555.9 1042.5 %all-reduce.18.cloned.1.call-done = (f32[2048,4096]{0,1:T(8,128)}, f32[4096,4096]{1,0:T(8,128)}) async-done(((f32[2048,4096]{0,1:T(8,128)}, f32[4096,4096]{1,0:T(8,128)}), (f32[2048,4096]{0,1:T(8,128)}, f32[4096,4096]{1,0:T(8,128)})) %all-reduce.18.cloned.1.call-update) | async-done | bytes 100663312 | tf_op jit(solution)/shard_map/psum | solution.py:68
  2598.3 31.1 copy.22
  2629.4 720.5 %all-reduce.16.cloned.1.call-done = f32[4096,4096]{1,0:T(8,128)} async-done(((f32[4096,4096]{1,0:T(8,128)}), f32[4096,4096]{1,0:T(8,128)}) %all-reduce.16.cloned.1.call-update) | async-done | bytes 67108880 | tf_op jit(solution)/shard_map/psum | solution.py:68
  3350.0 44.1 %copy.31 = f32[4096,4096]{1,0:T(8,128)} copy(f32[4096,4096]{1,0:T(8,128)} %get-tuple-element.74) | data formatting | bytes 134217728
  3394.0 44.1 %copy.32 = f32[4096,4096]{1,0:T(8,128)} copy(f32[4096,4096]{1,0:T(8,128)} %all-reduce.16.cloned.1.call-done) | data formatting | bytes 134217728
  (66 shorter events, 0.5 us)
Async XLA Ops:
  7.2 90.8 %all-reduce.8.cloned.1.call-start = ((), (), s32[]{:S(2)}) async-start(), calls=%async_computation | async-start | bytes 131072 | tf_op jit(solution)/shard_map/psum | solution.py:28
  7.2 23.7 copy-start.21
  7.2 23.7 copy-start.22
  31.0 68.5 %copy-start.15 = (f32[4096]{0:T(1024)S(1)}, f32[4096]{0:T(1024)}, u32[]{:S(2)}) copy-start(f32[4096]{0:T(1024)} %param.21) | copy-start | bytes 49156
  31.0 68.5 %copy-start.23 = (f32[4096]{0:T(1024)S(1)}, f32[4096]{0:T(1024)}, u32[]{:S(2)}) copy-start(f32[4096]{0:T(1024)} %param.22) | copy-start | bytes 49156
  53.1 180.4 %all-reduce.10.cloned.1.call-start = ((), (), s32[]{:S(2)}) async-start(), calls=%async_computation.1 | async-start | bytes 131072 | tf_op jit(solution)/shard_map/psum | solution.py:28
  99.5 45.8 %copy-start.8 = (f32[1,4096]{1,0:T(1,128)}, f32[1,4096]{1,0:T(1,128)S(1)}, u32[]{:S(2)}) copy-start(f32[1,4096]{1,0:T(1,128)S(1)} %get-tuple-element.42) | copy-start | bytes 49156
  99.5 45.8 %copy-start.13 = (f32[1,4096]{1,0:T(1,128)}, f32[1,4096]{1,0:T(1,128)S(1)}, u32[]{:S(2)}) copy-start(f32[1,4096]{1,0:T(1,128)S(1)} %get-tuple-element.39) | copy-start | bytes 49156
  145.3 89.7 %copy-start.18 = (f32[4096]{0:T(1024)S(1)}, f32[4096]{0:T(1024)}, u32[]{:S(2)}) copy-start(f32[4096]{0:T(1024)} %param.23) | copy-start | bytes 49156
  145.3 89.7 %copy-start.25 = (f32[4096]{0:T(1024)S(1)}, f32[4096]{0:T(1024)}, u32[]{:S(2)}) copy-start(f32[4096]{0:T(1024)} %param.24) | copy-start | bytes 49156
  191.9 177.3 %all-reduce.12.cloned.1.call-start = ((), (), s32[]{:S(2)}) async-start(), calls=%async_computation.2 | async-start | bytes 131072 | tf_op jit(solution)/shard_map/psum | solution.py:28
  234.9 46.2 %copy-start.4 = (f32[1,4096]{1,0:T(1,128)}, f32[1,4096]{1,0:T(1,128)S(1)}, u32[]{:S(2)}) copy-start(f32[1,4096]{1,0:T(1,128)S(1)} %get-tuple-element.44) | copy-start | bytes 49156
  234.9 1088.6 %copy-start.2 = (f32[1,4096]{1,0:T(1,128)}, f32[1,4096]{1,0:T(1,128)S(1)}, u32[]{:S(2)}) copy-start(f32[1,4096]{1,0:T(1,128)S(1)} %get-tuple-element.47) | copy-start | bytes 49156
  327.7 835.9 %all-reduce.14.cloned.1.call-start = ((), (), s32[]{:S(2)}) async-start(), calls=%async_computation.3 | async-start | bytes 134217728 | tf_op jit(solution)/shard_map/psum | solution.py:54
  417.3 0.7 copy-start.9
  417.3 0.8 copy-start.11
  417.3 0.8 copy-start.16
  417.3 1.4 copy-start.12
  417.3 2181.0 %all-reduce.18.cloned.1.call-start = ((), (), s32[]{:S(2)}) async-start(), calls=%async_computation.5 | async-start | bytes 201326592 | tf_op jit(solution)/shard_map/psum | solution.py:68
  1234.8 18.5 copy-start
  1234.8 18.5 copy-start.5
  1234.8 18.5 copy-start.26
  1253.3 70.2 %copy-start.7 = (f32[4096]{0:T(1024)S(1)}, f32[4096]{0:T(1024)}, u32[]{:S(2)}) copy-start(f32[4096]{0:T(1024)} %rsqrt_multiply_fusion.1) | copy-start | bytes 49156
  1323.5 15.6 copy-start.10
  1323.5 15.6 copy-start.14
  1323.5 15.6 copy-start.17
  1323.6 15.6 copy-start.24
  1335.7 3.4 copy-start.1
  1382.5 70.9 %copy-start.20 = (f32[4096]{0:T(1024)S(1)}, f32[4096]{0:T(1024)}, u32[]{:S(2)}) copy-start(f32[4096]{0:T(1024)} %rsqrt_multiply_fusion) | copy-start | bytes 49156
  1485.9 0.7 copy-start.3
  1485.9 0.7 copy-start.6
  1485.9 0.7 copy-start.19
  1486.0 0.8 copy-start.27
  1486.0 1864.0 %all-reduce.16.cloned.1.call-start = ((), (), s32[]{:S(2)}) async-start(), calls=%async_computation.4 | async-start | bytes 134217728 | tf_op jit(solution)/shard_map/psum | solution.py:68
Sparse Core Ops, SparseCore 0:
  53.2 44.7 all-reduce.7
  192.0 41.3 all-reduce.9
  327.9 41.3 all-reduce.11
  417.5 746.1 all-reduce.13
  1486.1 1112.1 all-reduce.17
  2602.5 747.3 all-reduce.15
where the time goes:
time: 3450 us
  waiting for transfers between devices  2630 us (76%)
  matrix products  540 us (16%)
  local copies, waits for them, and re-layouts  126 us (4%)
  blocking collectives  70.1 us (2%)
  other arithmetic  58.9 us (2%)
    psum x2, waiting for transfers between devices, local_step(): weight_grads = lax.psum((grad_w_in, grad_w_mid, grad_w_out), DATA_AXIS)  1760 us
    psum x1, waiting for transfers between devices, local_step(): corr_mat = lax.psum(contract_rows(emb_a, emb_b), DATA_AXIS) / row_count  744 us
    dot_general x4, matrix products, contract_rows(): lax.dot_general(left_op, right_op, (((0,), (0,)), ((), ())), preferred_el...  173 us
    dot_general x3, matrix products, contract_cols(): lax.dot_general(left_op, right_op, (((1,), (1,)), ((), ())), preferred_el...  137 us
    psum x3, waiting for transfers between devices, norm_pair(): stat_means = lax.psum(stat_sums, DATA_AXIS) / row_count  128 us
    unnamed x59, local copies, waits for them, and re-layouts  126 us
    dot_general x2, matrix products, hidden_pair(): jnp.dot(in_b, weight_b, preferred_element_type=jnp.float32)  69.5 us
  transfers between devices with their start and end apart: 6, of which 6 were waited for; matrix products, arithmetic and copies ran while one was open for 3% of the time, Pallas kernels for 0%

commit v1 on v0

v1 whole, which is shorter than its diff:
```python
import jax
import jax.numpy as jnp
from jax import lax
from jax.sharding import PartitionSpec as P

NORM_EPS = 1e-5
DATA_AXIS = "data"
F32 = jnp.float32
BF16 = jnp.bfloat16


def dot(left_op, right_op, left_dim, right_dim):
    return lax.dot_general(left_op, right_op, (((left_dim,), (right_dim,)), ((), ())), preferred_element_type=F32)


def solution(mesh):
    shards = mesh.shape[DATA_AXIS]
    chips = shards // 2
    row_part = P(DATA_AXIS, None)
    replicated = P()
    pair_groups = [[2 * i, 2 * i + 1] for i in range(chips)]
    pair_perm = [(i, i ^ 1) for i in range(shards)]

    def local_step(feat_a, feat_b, w_in, w_mid, w_out, t_in, t_mid, t_out, gain_1, bias_1, gain_2, bias_2, off_weight):
        row_count = feat_a.shape[0] * shards
        width = w_mid.shape[0]
        half = width // 2
        block = width // shards
        dev = lax.axis_index(DATA_AXIS)
        core = dev % 2
        chip = dev // 2
        own_start = core * half
        other_start = (1 - core) * half

        def rows_of(array, start, size):
            return lax.dynamic_slice_in_dim(array, start, size, 0)

        def cols_of(array, start, size):
            return lax.dynamic_slice_in_dim(array, start, size, 1)

        def gather(array):
            return lax.all_gather(array, DATA_AXIS, axis=0, tiled=True)

        def pair_gather(array):
            return lax.all_gather(array, DATA_AXIS, axis=0, tiled=True, axis_index_groups=pair_groups)

        def norm_rows(pre):
            sums = lax.all_gather(jnp.stack([jnp.sum(pre, axis=0), jnp.sum(pre * pre, axis=0)]), DATA_AXIS)
            means = jnp.sum(sums, axis=0) / row_count
            inv = lax.rsqrt(jnp.maximum(means[1] - means[0] * means[0], 0.0) + NORM_EPS)
            return (pre - means[0]) * inv

        def teacher_layer(layer_in, weight, gain_vec, bias_vec):
            normed = norm_rows(jnp.dot(layer_in, weight, preferred_element_type=F32))
            return jnp.maximum(normed * gain_vec + bias_vec, 0.0).astype(BF16)

        def stats(pre):
            mean = jnp.sum(pre, axis=1, keepdims=True) / row_count
            square = jnp.sum(pre * pre, axis=1, keepdims=True) / row_count
            return mean, lax.rsqrt(jnp.maximum(square - mean * mean, 0.0) + NORM_EPS)

        def norm_back(grad_n, normed, inv_std):
            mean_g = jnp.sum(grad_n, axis=1, keepdims=True) / row_count
            mean_gn = jnp.sum(grad_n * normed, axis=1, keepdims=True) / row_count
            return (grad_n - mean_g - normed * mean_gn) * inv_std

        def affine_back(grad_pre, normed, inv_std, gain_col):
            sum_gn = jnp.sum(grad_pre * normed, axis=1, keepdims=True)
            sum_g = jnp.sum(grad_pre, axis=1, keepdims=True)
            grad_u = (grad_pre - sum_g / row_count - normed * (sum_gn / row_count)) * (gain_col * inv_std)
            return grad_u.astype(BF16), jnp.concatenate([sum_gn, sum_g], axis=1)

        feat_all = gather(feat_a)
        teach_1 = teacher_layer(feat_b, t_in, gain_1, bias_1)
        teach_2 = teacher_layer(teach_1, t_mid, gain_2, bias_2)
        emb_b = norm_rows(jnp.dot(teach_2, t_out, preferred_element_type=F32)).astype(BF16)
        emb_b_all = gather(emb_b)

        gain_1h, bias_1h, gain_2h, bias_2h = (rows_of(v[:, None], own_start, half) for v in (gain_1, bias_1, gain_2, bias_2))

        pre_1 = dot(cols_of(w_in, own_start, half), feat_all, 0, 1)
        mean_1, inv_1 = stats(pre_1)
        act_1 = jnp.maximum((pre_1 - mean_1) * inv_1 * gain_1h + bias_1h, 0.0).astype(BF16)
        act_1_other = lax.ppermute(act_1, DATA_AXIS, pair_perm)

        w_mid_cols = cols_of(w_mid, own_start, half)
        pre_2 = dot(rows_of(w_mid_cols, own_start, half), act_1, 0, 0) + dot(rows_of(w_mid_cols, other_start, half), act_1_other, 0, 0)
        mean_2, inv_2 = stats(pre_2)
        act_2 = jnp.maximum((pre_2 - mean_2) * inv_2 * gain_2h + bias_2h, 0.0).astype(BF16)
        act_2_other = lax.ppermute(act_2, DATA_AXIS, pair_perm)

        w_out_cols = cols_of(w_out, dev * block, block)
        pre_z = dot(rows_of(w_out_cols, own_start, half), act_2, 0, 0) + dot(rows_of(w_out_cols, other_start, half), act_2_other, 0, 0)
        mean_z, inv_z = stats(pre_z)
        zh_a = (pre_z - mean_z) * inv_z
        emb_a = zh_a.astype(BF16)

        corr_mat = dot(emb_a, emb_b_all, 1, 0) / row_count
        on_diag = lax.broadcasted_iota(jnp.int32, corr_mat.shape, 0) + dev * block == lax.broadcasted_iota(jnp.int32, corr_mat.shape, 1)
        loss_part = jnp.sum(jnp.where(on_diag, jnp.square(1.0 - corr_mat), off_weight * jnp.square(corr_mat)))
        grad_c = jnp.where(on_diag, -2.0 * (1.0 - corr_mat), 2.0 * off_weight * corr_mat).astype(BF16)

        grad_z = norm_back(dot(grad_c, emb_b_all, 1, 1) / row_count, zh_a, inv_z).astype(BF16)
        grad_z_all = gather(grad_z)
        grad_emb = dot(emb_b, gather(grad_c), 1, 1) / row_count

        grad_w_out = pair_gather(dot(act_2, grad_z_all, 1, 1))
        normed_2 = (pre_2 - mean_2) * inv_2
        grad_pre_2 = jnp.where(normed_2 * gain_2h + bias_2h > 0.0, dot(rows_of(w_out, own_start, half), grad_z_all, 1, 0), 0.0)
        grad_u_2, affine_2 = affine_back(grad_pre_2, normed_2, inv_2, gain_2h)
        grad_u_2_all = pair_gather(grad_u_2)

        part_start = chip * block
        normed_1 = (rows_of(pre_1, part_start, block) - rows_of(mean_1, part_start, block)) * rows_of(inv_1, part_start, block)
        gain_1p, bias_1p = rows_of(gain_1h, part_start, block), rows_of(bias_1h, part_start, block)
        grad_pre_1 = jnp.where(normed_1 * gain_1p + bias_1p > 0.0, dot(rows_of(w_mid, own_start + part_start, block), grad_u_2_all, 1, 0), 0.0)
        grad_u_1, affine_1 = affine_back(grad_pre_1, normed_1, rows_of(inv_1, part_start, block), gain_1p)
        grad_w_in_parts = lax.all_gather(dot(feat_all, grad_u_1, 0, 1), DATA_AXIS)
        grad_w_mid = pair_gather(dot(act_1, grad_u_2_all, 1, 1))

        grad_w_in = grad_w_in_parts.reshape(chips, 2, -1, block).transpose(2, 1, 0, 3).reshape(-1, width)
        small = jnp.concatenate([affine_1, rows_of(affine_2, part_start, block)], axis=1).T
        small = jnp.concatenate([small, jnp.full((1, block), loss_part)], axis=0)
        small_all = lax.all_gather(small, DATA_AXIS)
        vectors = small_all.reshape(chips, 2, 5, block).transpose(2, 1, 0, 3).reshape(5, width)
        loss_value = jnp.sum(small_all[:, 4, 0])
        return (loss_value, grad_emb, grad_w_in, grad_w_mid, grad_w_out, vectors[0], vectors[1], vectors[2], vectors[3])

    return jax.shard_map(local_step, mesh=mesh, in_specs=(row_part, row_part) + (replicated,) * 11, out_specs=(replicated, row_part) + (replicated,) * 7, check_vma=False)
```

time: 3450 us -> 1960 us (0.57)
  waiting for transfers between devices: 2630 us -> 375 us
  matrix products: 540 us -> 1130 us
  local copies, waits for them, and re-layouts: 126 us -> 224 us
  other arithmetic: 58.9 us -> 147 us
    psum x6 -> x0, waiting for transfers between devices: 2630 us -> none  [the longest x2 1760 us: local_step(): weight_grads = lax.psum((grad_w_in, grad_w_mid, grad_w_out), DATA_AXIS)]
    dot_general x13 -> x16, matrix products: 540 us -> 1130 us  [the longest x13 1010 us: dot(): lax.dot_general(left_op, right_op, (((left_dim,), (right_dim,)), ((), ())...]
    all_gather x0 -> x8, waiting for transfers between devices: none -> 354 us  [the longest x4 297 us: gather(): return lax.all_gather(array, DATA_AXIS, axis=0, tiled=True)]
    convert_element_type x2 -> x5, other arithmetic: 28.1 us -> 144 us  [the longest x1 52.9 us: affine_back(): return (grad_u.astype(BF16), jnp.concatenate([sum_gn, sum_g], axis=1))]
    reshape x0 -> x3, local copies, waits for them, and re-layouts: none -> 82.4 us  [the longest x2 82.3 us: local_step(): grad_w_in_parts.reshape(chips, 2, -1, block).transpose(2, 1, 0, 3)]
    psum x3 -> x0, blocking collectives: 70.1 us -> none  [the longest x2 47.7 us: affine_back(): lax.psum(jnp.stack([jnp.sum(grad_pre * normed, axis=0), jnp.sum(grad_pre,...]
    all_gather x0 -> x4, blocking collectives: none -> 55.3 us  [the longest x3 43.3 us: norm_rows(): lax.all_gather(jnp.stack([jnp.sum(pre, axis=0), jnp.sum(pre * pre, axis=0...]
    transpose x0 -> x1, local copies, waits for them, and re-layouts: none -> 48.6 us  [local_step(): grad_w_in_parts.reshape(chips, 2, -1, block).transpose(2, 1, 0, 3)]
  transfers between devices with their start and end apart: 6 -> 10, of which waited for: 6 -> 3; matrix products, arithmetic and copies ran while one was open for 3% -> 55% of each run, Pallas kernels for 0% -> 0%
where the time goes in v1:
time: 1960 us; the launch traced here: 1950 us
  matrix products  1130 us (58%)
  waiting for transfers between devices  375 us (19%)
  local copies, waits for them, and re-layouts  224 us (11%)
  other arithmetic  147 us (8%)
  blocking collectives  55.3 us (3%)
    dot_general x13, matrix products, dot(): lax.dot_general(left_op, right_op, (((left_dim,), (right_dim,)), ((), ())...  1010 us
    all_gather x4, waiting for transfers between devices, gather(): return lax.all_gather(array, DATA_AXIS, axis=0, tiled=True)  297 us
    unnamed x62, local copies, waits for them, and re-layouts  91.9 us
    reshape x2, local copies, waits for them, and re-layouts, local_step(): grad_w_in_parts.reshape(chips, 2, -1, block).transpose(2, 1, 0, 3)  82.3 us
    dot_general x2, matrix products, teacher_layer(): normed = norm_rows(jnp.dot(layer_in, weight, preferred_element_type=F32))  69.3 us
    all_gather x1, waiting for transfers between devices, local_step(): grad_w_in_parts = lax.all_gather(dot(feat_all, grad_u_1, 0, 1), DATA_AXIS)  56.5 us
    convert_element_type x1, other arithmetic, affine_back(): return (grad_u.astype(BF16), jnp.concatenate([sum_gn, sum_g], axis=1))  52.9 us
    transpose x1, local copies, waits for them, and re-layouts, local_step(): grad_w_in_parts.reshape(chips, 2, -1, block).transpose(2, 1, 0, 3)  48.6 us
  transfers between devices with their start and end apart: 10, of which 3 were waited for; matrix products, arithmetic and copies ran while one was open for 55% of the time, Pallas kernels for 0%

profile of v1, /device:TPU:0, one launch (start us, length us, event | category | flops | bytes accessed | tf_op | source)
XLA Modules:
  0.0 1945.2 jit_solution(13672914933018558136)
XLA Ops:
  7.2 0.7 all-gather.18.cloned.1.call-update
  8.0 23.6 %fusion.52 = (f32[4096]{0:T(1024)S(1)}, f32[4096]{0:T(1024)S(1)}, f32[1024,4096]{1,0:T(8,128)}) fusion(bf16[1024,2048]{1,0:T(8,128)(2,1)} %param.14, bf16[2048,4096]{1,0:T(8,128)(2,1)} %param.18), kind=kOutput, calls=%fused_computation.116 | convolution fusion | flops 17192443904 | bytes 37781504 | tf_op jit(solution)/shard_map/dot_general | solution.py:54
  31.6 16.2 all-gather.5
  48.1 45.7 %fusion.51 = (f32[4096]{0:T(1024)S(1)}, f32[4096]{0:T(1024)S(1)}, f32[1024,4096]{1,0:T(8,128)}) fusion(bf16[4096,4096]{1,0:T(8,128)(2,1)} %param.19, f32[1024,4096]{1,0:T(8,128)} %get-tuple-element.51, f32[4096]{0:T(1024)S(1)} %copy-done.13, f32[4096]{0:T(1024)S(1)} %copy-done.11, f32[4096]{0:T(1024)S(1)} %bitcast.84, f32[4096]{0:T(1024)S(1)} %bitcast.83), kind=kOutput, calls=%fused_computation.115 | convolution fusion | flops 34397478912 | bytes 67207168 | tf_op jit(solution)/shard_map/dot_general | solution.py:54
  93.8 13.6 all-gather.6
  107.6 45.7 %fusion.50 = (f32[4096]{0:T(1024)S(1)}, f32[4096]{0:T(1024)S(1)}, f32[1024,4096]{1,0:T(8,128)}) fusion(bf16[4096,4096]{1,0:T(8,128)(2,1)} %param.20, f32[1024,4096]{1,0:T(8,128)} %get-tuple-element.52, f32[4096]{0:T(1024)S(1)} %copy-done.25, f32[4096]{0:T(1024)S(1)} %copy-done.23, f32[4096]{0:T(1024)S(1)} %bitcast.86, f32[4096]{0:T(1024)S(1)} %bitcast.85), kind=kOutput, calls=%fused_computation.114 | convolution fusion | flops 34397478912 | bytes 67207168 | tf_op jit(solution)/shard_map/dot_general | solution.py:76
  153.4 13.4 all-gather.7
  167.0 9.7 multiply_convert_fusion.3
  176.7 0.4 all-gather.22.cloned.1.call-start
  177.2 86.1 %fusion.48 = (f32[2048]{0:T(1024)S(1)}, f32[2048]{0:T(1024)S(1)}, f32[2048,8192]{1,0:T(8,128)}) fusion(bf16[8192,2048]{1,0:T(8,128)(2,1)} %all-gather.18.cloned.1.call-done, bf16[2048,4096]{1,0:T(8,128)(2,1)} %param.15, s32[]{:T(128)} %select_n.65), kind=kOutput, calls=%fused_computation.112 | convolution fusion | flops 68769808384 | bytes 109068800 | tf_op jit(solution)/shard_map/dot_general | solution.py:13
  263.4 33.3 %maximum_convert_fusion.1 = bf16[2048,8192]{1,0:T(8,128)(2,1)} fusion(f32[2048,8192]{1,0:T(8,128)} %get-tuple-element.50, f32[2048]{0:T(1024)S(1)} %dynamic-slice-done.1, f32[2048]{0:T(1024)S(1)} %dynamic-slice-done, f32[2048]{0:T(1024)S(1)} %get-tuple-element.47, f32[2048]{0:T(1024)S(1)} %get-tuple-element.46), kind=kLoop, calls=%fused_computation.6 | loop fusion | flops 100663296 | bytes 100696064 | tf_op jit(solution)/shard_map/convert_element_type | solution.py:83
  296.8 0.6 dynamic-slice.27
  297.4 85.2 %fusion.25 = f32[2048,8192]{1,0:T(8,128)} fusion(bf16[2048,8192]{1,0:T(8,128)(2,1)} %maximum_convert_fusion.1, bf16[4096,4096]{1,0:T(8,128)(2,1)} %param.16, s32[]{:T(128)S(6)} %select_n.69), kind=kOutput, calls=%fused_computation.54 | convolution fusion | flops 68719476736 | bytes 109051904 | tf_op jit(solution)/shard_map/dot_general | solution.py:13
  382.7 95.5 %fusion.47 = (f32[2048]{0:T(1024)S(1)}, f32[2048]{0:T(1024)S(1)}, f32[2048,8192]{1,0:T(8,128)}) fusion(f32[2048,8192]{1,0:T(8,128)} %fusion.25, bf16[2048,8192]{1,0:T(8,128)(2,1)} %collective-permute-done, bf16[4096,4096]{1,0:T(8,128)(2,1)} %param.16, s32[]{:T(128)S(6)} %select_n.72, s32[]{:T(128)S(6)} %select_n.69), kind=kOutput, calls=%fused_computation.111 | convolution fusion | flops 68786585600 | bytes 176177152 | tf_op jit(solution)/shard_map/dot_general | solution.py:13
  478.2 0.6 fusion.38
  478.8 33.3 %maximum_convert_fusion = bf16[2048,8192]{1,0:T(8,128)(2,1)} fusion(f32[2048,8192]{1,0:T(8,128)} %get-tuple-element.54, f32[2048]{0:T(1024)S(1)} %copy-done.9, f32[2048]{0:T(1024)S(1)} %get-tuple-element.31, f32[2048]{0:T(1024)S(1)} %get-tuple-element.44, f32[2048]{0:T(1024)S(1)} %get-tuple-element.45), kind=kLoop, calls=%fused_computation.2 | loop fusion | flops 100663296 | bytes 100696064 | tf_op jit(solution)/shard_map/convert_element_type | solution.py:89
  512.2 0.2 collective-permute-start.1
  513.1 28.8 %fusion.33 = f32[512,8192]{1,0:T(8,128)} fusion(bf16[2048,8192]{1,0:T(8,128)(2,1)} %maximum_convert_fusion, bf16[4096,4096]{1,0:T(8,128)(2,1)} %param.17, s32[]{:T(128)S(6)} %select_n.69, s32[]{:T(128)S(6)} %select_n.74), kind=kOutput, calls=%fused_computation.62 | convolution fusion | flops 17179869184 | bytes 52428808 | tf_op jit(solution)/shard_map/dot_general | solution.py:13
  541.8 19.5 %collective-permute-done.1 = bf16[2048,8192]{1,0:T(8,128)(2,1)} collective-permute-done((bf16[2048,8192]{1,0:T(8,128)(2,1)}, bf16[2048,8192]{1,0:T(8,128)(2,1)}, u32[]{:S(2)}, u32[]{:S(2)}) %collective-permute-start.1) | collective-permute-done | bytes 33554464 | tf_op jit(solution)/shard_map/ppermute | solution.py:90
  561.3 30.7 %fusion.49 = (f32[512]{0:T(512)S(1)}, f32[512]{0:T(512)S(1)}, f32[512,8192]{1,0:T(8,128)}) fusion(f32[512,8192]{1,0:T(8,128)} %fusion.33, bf16[2048,8192]{1,0:T(8,128)(2,1)} %collective-permute-done.1, bf16[4096,4096]{1,0:T(8,128)(2,1)} %param.17, s32[]{:T(128)S(6)} %select_n.72, s32[]{:T(128)S(6)} %select_n.74), kind=kOutput, calls=%fused_computation.113 | convolution fusion | flops 17196646400 | bytes 69210120 | tf_op jit(solution)/shard_map/dot_general | solution.py:13
  592.0 49.1 %select_reduce_fusion = (f32[]{:T(128)}, bf16[512,4096]{1,0:T(8,128)(2,1)}) fusion(f32[]{:T(128)S(6)} %copy.35, s32[512]{0:T(512)S(1)} %iota_add_fusion, f32[]{:T(128)S(6)} %mul.314, bf16[8192,4096]{1,0:T(8,128)(2,1)} %all-gather.20.cloned.1.call-done, f32[512,8192]{1,0:T(8,128)} %get-tuple-element.55, f32[512]{0:T(512)S(1)} %get-tuple-element.49, ...), kind=kOutput, calls=%fused_computation.38 | convolution fusion | flops 34397487104 | bytes 88086544 | tf_op jit(solution)/shard_map/dot_general | solution.py:13
  641.2 44.5 %multiply_reduce_fusion.9 = (f32[512]{0:T(512)S(1)}, f32[512]{0:T(512)S(1)}, f32[512,8192]{1,0:T(8,128)}) fusion(f32[512]{0:T(512)S(1)} %get-tuple-element.49, f32[512,8192]{1,0:T(8,128)} %get-tuple-element.55, f32[512]{0:T(512)S(1)} %get-tuple-element.48, bf16[512,4096]{1,0:T(8,128)(2,1)} %get-tuple-element.33, ...), kind=kOutput, calls=%fused_computation.26 | convolution fusion | flops 34384904192 | bytes 104865792 | tf_op jit(solution)/shard_map/dot_general | solution.py:13
  685.7 15.0 multiply_convert_fusion.2
  700.8 297.3 %all-gather.22.cloned.1.call-done = bf16[4096,8192]{1,0:T(8,128)(2,1)} async-done(((bf16[512,8192]{1,0:T(8,128)(2,1)}), bf16[4096,8192]{1,0:T(8,128)(2,1)}) %all-gather.22.cloned.1.call-update) | async-done | bytes 67108880 | tf_op jit(solution)/shard_map/all_gather | solution.py:42
  998.1 168.7 %fusion.46 = (f32[2048]{0:T(1024)S(1)}, f32[2048]{0:T(1024)S(1)}, f32[2048,8192]{1,0:T(8,128)}) fusion(f32[2048]{0:T(1024)S(1)} %copy-done.1, f32[2048,8192]{1,0:T(8,128)} %get-tuple-element.54, f32[2048]{0:T(1024)S(1)} %copy-done.3, bf16[4096,8192]{1,0:T(8,128)(2,1)} %all-gather.22.cloned.1.call-done, bf16[4096,4096]{1,0:T(8,128)(2,1)} %param.17, ...), kind=kOutput, calls=%fused_computation.110 | convolution fusion | flops 137589948416 | bytes 218153472 | tf_op jit(solution)/shard_map/dot_general | solution.py:13
  1166.9 52.9 %multiply_convert_fusion = bf16[2048,8192]{1,0:T(8,128)(2,1)} fusion(f32[2048,8192]{1,0:T(8,128)} %get-tuple-element.57, f32[2048,8192]{1,0:T(8,128)} %get-tuple-element.54, f32[2048]{0:T(1024)S(1)} %copy-done.6, f32[2048]{0:T(1024)S(1)} %broadcast_multiply_fusion.3, f32[2048]{0:T(1024)S(1)} %broadcast_multiply_fusion.4, f32[2048]{0:T(1024)S(1)} %copy-done.1, ...), kind=kLoop, calls=%fused_computation | loop fusion | flops 117440512 | bytes 167813120 | tf_op jit(solution)/shard_map/convert_element_type | solution.py:71
  1219.8 0.5 all-gather.26.cloned.1.call-update
  1220.4 151.4 %fusion.58 = f32[2048,4096]{1,0:T(8,128)} fusion(bf16[2048,8192]{1,0:T(8,128)(2,1)} %maximum_convert_fusion, bf16[4096,8192]{1,0:T(8,128)(2,1)} %all-gather.22.cloned.1.call-done), kind=kOutput, calls=%fused_computation.122 | convolution fusion | flops 137438953472 | bytes 134217728 | tf_op jit(solution)/shard_map/dot_general | solution.py:13
  1371.9 0.6 copy-done.14
  1372.6 0.7 dynamic-slice.21
  1373.3 0.7 fusion.53
  1374.1 49.1 %multiply_reduce_fusion.3 = (f32[512]{0:T(512)S(1)}, f32[512]{0:T(512)S(1)}, f32[512,8192]{1,0:T(8,128)}) fusion(f32[2048,8192]{1,0:T(8,128)} %get-tuple-element.50, s32[]{:T(128)S(6)} %select_n.67, f32[512]{0:T(512)S(1)} %get-tuple-element.29, f32[512]{0:T(512)S(1)} %dynamic-slice.21, bf16[4096,8192]{1,0:T(8,128)(2,1)} %all-gather.24.cloned.1.call-done, ...), kind=kOutput, calls=%fused_computation.11 | convolution fusion | flops 34397487104 | bytes 104869896 | tf_op jit(solution)/shard_map/dot_general | solution.py:13
  1423.2 28.3 %fusion.31 = f32[2048,512]{0,1:T(8,128)} fusion(bf16[8192,2048]{1,0:T(8,128)(2,1)} %all-gather.18.cloned.1.call-done, f32[512,8192]{1,0:T(8,128)} %get-tuple-element.58, f32[2048,8192]{1,0:T(8,128)} %get-tuple-element.50, s32[]{:T(128)S(6)} %select_n.67, f32[512]{0:T(512)S(1)} %get-tuple-element.27, f32[512]{0:T(512)S(1)} %get-tuple-element.29, ...), kind=kOutput, calls=%fused_computation.60 | convolution fusion | flops 17209229312 | bytes 71313408 | tf_op jit(solution)/shard_map/dot_general | solution.py:13
  1451.7 151.3 %fusion.57 = f32[2048,4096]{1,0:T(8,128)} fusion(bf16[2048,8192]{1,0:T(8,128)(2,1)} %maximum_convert_fusion.1, bf16[4096,8192]{1,0:T(8,128)(2,1)} %all-gather.24.cloned.1.call-done), kind=kOutput, calls=%fused_computation.121 | convolution fusion | flops 137438953472 | bytes 134217728 | tf_op jit(solution)/shard_map/dot_general | solution.py:13
  1603.1 43.5 %convolution_multiply_fusion = f32[1024,4096]{1,0:T(8,128)} fusion(bf16[1024,4096]{1,0:T(8,128)(2,1)} %multiply_convert_fusion.3, bf16[4096,4096]{1,0:T(8,128)(2,1)} %all-gather.26.cloned.1.call-done), kind=kOutput, calls=%fused_computation.29 | convolution fusion | flops 34363932672 | bytes 58720256 | tf_op jit(solution)/shard_map/dot_general | solution.py:13
  1646.6 0.5 pad_bitcast_fusion
  1647.2 12.0 all-gather.8
  1659.3 0.6 copy.30
  1659.9 0.6 copy.29
  1660.5 0.6 copy.28
  1661.2 0.6 copy.27
  1661.8 0.6 slice_reduce_fusion
  1662.4 56.5 %all-gather.32.cloned.1.call-done = f32[16384,512]{0,1:T(8,128)} async-done(((f32[2048,512]{0,1:T(8,128)}), f32[16384,512]{0,1:T(8,128)}) %all-gather.32.cloned.1.call-update) | async-done | bytes 33554448 | tf_op jit(solution)/shard_map/all_gather | solution.py:118
  1718.9 42.6 %reshape.168 = f32[4,2,2048,512]{2,1,0,3:T(2,128)} reshape(f32[16384,512]{0,1:T(8,128)} %all-gather.32.cloned.1.call-done) | data formatting | bytes 67108864 | tf_op jit(solution)/shard_map/reshape | solution.py:121
  1761.5 48.6 %copy.25 = f32[2048,2,4,512]{3,2,1,0:T(4,128)} copy(f32[2048,2,4,512]{0,1,2,3:T(2,128)} %bitcast.72) | data formatting | bytes 67108864 | tf_op jit(solution)/shard_map/transpose | solution.py:121
  1810.1 39.7 %reshape.169 = f32[2048,4096]{1,0:T(8,128)} reshape(f32[2048,2,4,512]{3,2,1,0:T(4,128)} %copy.25) | data formatting | bytes 67108864 | tf_op jit(solution)/shard_map/reshape | solution.py:121
  1849.8 44.1 %copy.36 = f32[4096,4096]{1,0:T(8,128)} copy(f32[4096,4096]{1,0:T(8,128)} %all-gather.28.cloned.1.call-done) | data formatting | bytes 134217728
  1893.9 44.1 %copy.37 = f32[4096,4096]{1,0:T(8,128)} copy(f32[4096,4096]{1,0:T(8,128)} %all-gather.30.cloned.1.call-done) | data formatting | bytes 134217728
  (103 shorter events, 1.4 us)
Async XLA Ops:
  7.2 170.0 %all-gather.18.cloned.1.call-start = ((), (), s32[]{:S(2)}) async-start(), calls=%async_computation | async-start | bytes 37748736 | tf_op jit(solution)/shard_map/all_gather | solution.py:42
  7.9 40.1 %copy-start.11 = (f32[4096]{0:T(1024)S(1)}, f32[4096]{0:T(1024)}, u32[]{:S(2)}) copy-start(f32[4096]{0:T(1024)} %param.21) | copy-start | bytes 49156
  7.9 40.1 %copy-start.13 = (f32[4096]{0:T(1024)S(1)}, f32[4096]{0:T(1024)}, u32[]{:S(2)}) copy-start(f32[4096]{0:T(1024)} %param.22) | copy-start | bytes 49156
  7.9 584.1 %all-gather.20.cloned.1.call-start = ((), (), s32[]{:S(2)}) async-start(), calls=%async_computation.1 | async-start | bytes 75497472 | tf_op jit(solution)/shard_map/all_gather | solution.py:42
  48.0 59.6 %copy-start.23 = (f32[4096]{0:T(1024)S(1)}, f32[4096]{0:T(1024)}, u32[]{:S(2)}) copy-start(f32[4096]{0:T(1024)} %param.23) | copy-start | bytes 49156
  48.0 59.6 %copy-start.25 = (f32[4096]{0:T(1024)S(1)}, f32[4096]{0:T(1024)}, u32[]{:S(2)}) copy-start(f32[4096]{0:T(1024)} %param.24) | copy-start | bytes 49156
  176.7 821.4 %all-gather.22.cloned.1.call-start = ((), (), s32[]{:S(2)}) async-start(), calls=%async_computation.2 | async-start | bytes 75497472 | tf_op jit(solution)/shard_map/all_gather | solution.py:42
  177.2 86.1 %dynamic-slice-start = ((f32[4096]{0:T(1024)}, s32[]{:T(128)}), f32[2048]{0:T(1024)S(1)}, s32[]{:S(2)}) async-start(f32[4096]{0:T(1024)} %param.21, s32[]{:T(128)} %select_n.65), calls=%async_computation.8 | async-start | bytes 16896 | tf_op jit(solution)/shard_map/dynamic-slice
  177.2 86.1 %dynamic-slice-start.1 = ((f32[4096]{0:T(1024)}, s32[]{:T(128)}), f32[2048]{0:T(1024)S(1)}, s32[]{:S(2)}) async-start(f32[4096]{0:T(1024)} %param.22, s32[]{:T(128)} %select_n.65), calls=%async_computation.9 | async-start | bytes 16896 | tf_op jit(solution)/shard_map/dynamic-slice.2
  263.3 33.4 %copy-start.4 = (f32[2048]{0:T(1024)}, f32[2048]{0:T(1024)S(1)}, u32[]{:S(2)}) copy-start(f32[2048]{0:T(1024)S(1)} %get-tuple-element.47) | copy-start | bytes 24580
  263.3 33.4 %copy-start.5 = (f32[2048]{0:T(1024)}, f32[2048]{0:T(1024)S(1)}, u32[]{:S(2)}) copy-start(f32[2048]{0:T(1024)S(1)} %get-tuple-element.46) | copy-start | bytes 24580
  263.4 33.4 %copy-start.26 = (f32[4096]{0:T(1024)S(1)}, f32[4096]{0:T(1024)}, u32[]{:S(2)}) copy-start(f32[4096]{0:T(1024)} %param.24) | copy-start | bytes 49156
  296.8 85.9 %collective-permute-start = (bf16[2048,8192]{1,0:T(8,128)(2,1)}, bf16[2048,8192]{1,0:T(8,128)(2,1)}, u32[]{:S(2)}, u32[]{:S(2)}) collective-permute-start(bf16[2048,8192]{1,0:T(8,128)(2,1)} %maximum_convert_fusion.1), channel_id=1, source_target_pairs={{0,1},{1,0},{2,3},{3,2},{4,5},{5,4},{6,7},{7,6}} | collective-permute-start | bytes 100663304 | tf_op jit(solution)/shard_map/ppermute | solution.py:84
  382.7 95.5 %copy-start.24 = (f32[4096]{0:T(1024)S(1)}, f32[4096]{0:T(1024)}, u32[]{:S(2)}) copy-start(f32[4096]{0:T(1024)} %param.23) | copy-start | bytes 49156
  382.7 96.2 %copy-start.9 = (f32[2048]{0:T(1024)S(1)}, f32[2048]{0:T(1024)}, u32[]{:S(2)}) copy-start(f32[2048]{0:T(1024)} %dynamic-slice.27) | copy-start | bytes 24580
  478.8 33.4 %copy-start = (f32[2048]{0:T(1024)}, f32[2048]{0:T(1024)S(1)}, u32[]{:S(2)}) copy-start(f32[2048]{0:T(1024)S(1)} %get-tuple-element.44) | copy-start | bytes 24580
  478.8 33.4 %copy-start.2 = (f32[2048]{0:T(1024)}, f32[2048]{0:T(1024)S(1)}, u32[]{:S(2)}) copy-start(f32[2048]{0:T(1024)S(1)} %get-tuple-element.45) | copy-start | bytes 24580
  478.8 33.4 %copy-start.7 = (f32[2048]{0:T(1024)}, f32[2048]{0:T(1024)S(1)}, u32[]{:S(2)}) copy-start(f32[2048]{0:T(1024)S(1)} %get-tuple-element.31) | copy-start | bytes 24580
  512.2 49.1 %collective-permute-start.1 = (bf16[2048,8192]{1,0:T(8,128)(2,1)}, bf16[2048,8192]{1,0:T(8,128)(2,1)}, u32[]{:S(2)}, u32[]{:S(2)}) collective-permute-start(bf16[2048,8192]{1,0:T(8,128)(2,1)} %maximum_convert_fusion), channel_id=1, source_target_pairs={{0,1},{1,0},{2,3},{3,2},{4,5},{5,4},{6,7},{7,6}} | collective-permute-start | bytes 100663304 | tf_op jit(solution)/shard_map/ppermute | solution.py:90
  685.6 312.5 %copy-start.1 = (f32[2048]{0:T(1024)S(1)}, f32[2048]{0:T(1024)}, u32[]{:S(2)}) copy-start(f32[2048]{0:T(1024)} %copy-done) | copy-start | bytes 24580
  685.6 312.5 %copy-start.3 = (f32[2048]{0:T(1024)S(1)}, f32[2048]{0:T(1024)}, u32[]{:S(2)}) copy-start(f32[2048]{0:T(1024)} %copy-done.2) | copy-start | bytes 24580
  685.7 312.5 %copy-start.8 = (f32[2048]{0:T(1024)S(1)}, f32[2048]{0:T(1024)}, u32[]{:S(2)}) copy-start(f32[2048]{0:T(1024)} %copy-done.7) | copy-start | bytes 24580
  685.7 312.4 %copy-start.10 = (f32[2048]{0:T(1024)S(1)}, f32[2048]{0:T(1024)}, u32[]{:S(2)}) copy-start(f32[2048]{0:T(1024)} %dynamic-slice.27) | copy-start | bytes 24580
  700.7 673.3 %all-gather.24.cloned.1.call-start = ((), (), s32[]{:S(2)}) async-start(), calls=%async_computation.3 | async-start | bytes 100663296 | tf_op jit(solution)/shard_map/all_gather | solution.py:45
  998.1 168.7 %copy-start.6 = (f32[2048]{0:T(1024)S(1)}, f32[2048]{0:T(1024)}, u32[]{:S(2)}) copy-start(f32[2048]{0:T(1024)} %get-tuple-element.30) | copy-start | bytes 24580
  1166.8 52.9 %copy-start.15 = (f32[2048]{0:T(1024)}, f32[2048]{0:T(1024)S(1)}, u32[]{:S(2)}) copy-start(f32[2048]{0:T(1024)S(1)} %get-tuple-element.9) | copy-start | bytes 24580
  1166.8 52.9 %copy-start.17 = (f32[2048]{0:T(1024)}, f32[2048]{0:T(1024)S(1)}, u32[]{:S(2)}) copy-start(f32[2048]{0:T(1024)S(1)} %get-tuple-element.10) | copy-start | bytes 24580
  1219.8 383.3 %all-gather.26.cloned.1.call-start = ((), (), s32[]{:S(2)}) async-start(), calls=%async_computation.4 | async-start | bytes 37748736 | tf_op jit(solution)/shard_map/all_gather | solution.py:42
  1220.4 441.4 %all-gather.30.cloned.1.call-start = ((), (), s32[]{:S(2)}) async-start(), calls=%async_computation.6 | async-start | bytes 100663296 | tf_op jit(solution)/shard_map/all_gather | solution.py:45
  1371.8 0.7 copy-start.14
  1371.8 1.5 copy-start.12
  1371.8 347.1 %all-gather.32.cloned.1.call-start = ((), (), s32[]{:S(2)}) async-start(), calls=%async_computation.7 | async-start | bytes 37748736 | tf_op jit(solution)/shard_map/all_gather | solution.py:118
  1423.2 28.4 %copy-start.19 = (f32[512]{0:T(512)}, f32[512]{0:T(512)S(1)}, u32[]{:S(2)}) copy-start(f32[512]{0:T(512)S(1)} %get-tuple-element.15) | copy-start | bytes 6148
  1423.2 28.4 %copy-start.21 = (f32[512]{0:T(512)}, f32[512]{0:T(512)S(1)}, u32[]{:S(2)}) copy-start(f32[512]{0:T(512)S(1)} %get-tuple-element.16) | copy-start | bytes 6148
  1451.6 398.2 %all-gather.28.cloned.1.call-start = ((), (), s32[]{:S(2)}) async-start(), calls=%async_computation.5 | async-start | bytes 100663296 | tf_op jit(solution)/shard_map/all_gather | solution.py:45
  1603.0 43.5 %copy-start.16 = (f32[2048]{0:T(1024)S(1)}, f32[2048]{0:T(1024)}, u32[]{:S(2)}) copy-start(f32[2048]{0:T(1024)} %copy-done.15) | copy-start | bytes 24580
  1603.0 43.5 %copy-start.18 = (f32[2048]{0:T(1024)S(1)}, f32[2048]{0:T(1024)}, u32[]{:S(2)}) copy-start(f32[2048]{0:T(1024)} %copy-done.17) | copy-start | bytes 24580
  1603.0 43.6 %copy-start.20 = (f32[512]{0:T(512)S(1)}, f32[512]{0:T(512)}, u32[]{:S(2)}) copy-start(f32[512]{0:T(512)} %copy-done.19) | copy-start | bytes 6148
  1603.0 43.6 %copy-start.22 = (f32[512]{0:T(512)S(1)}, f32[512]{0:T(512)}, u32[]{:S(2)}) copy-start(f32[512]{0:T(512)} %copy-done.21) | copy-start | bytes 6148
Sparse Core Ops, SparseCore 0:
  9.8 163.0 all-gather.17
  176.8 297.1 all-gather.19
  700.9 297.1 all-gather.21
  1219.9 90.2 all-gather.23
  1311.8 156.3 all-gather.25
  1469.6 90.1 all-gather.29
  1561.7 157.1 all-gather.31
  1721.0 90.1 all-gather.27

commit v2 on v1

--- a/solution.py
+++ b/solution.py
@@ -1,6 +1,9 @@
 import jax
 import jax.numpy as jnp
 from jax import lax
+from jax.experimental import pallas as pl
+from jax.experimental.layout import Layout, with_layout_constraint
+from jax.experimental.pallas import tpu as pltpu
 from jax.sharding import PartitionSpec as P
 
 NORM_EPS = 1e-5
@@ -9,8 +12,63 @@
 BF16 = jnp.bfloat16
 
 
+barrier = lax.optimization_barrier
+
+
 def dot(left_op, right_op, left_dim, right_dim):
     return lax.dot_general(left_op, right_op, (((left_dim,), (right_dim,)), ((), ())), preferred_element_type=F32)
+
+
+def place_rows(buffer, pieces, starts, row_start, total_rows, total_cols, step=256):
+    rows = pieces[0].shape[0]
+    count = len(pieces)
+
+    def kernel(where_ref, *refs):
+        out_ref = refs[-1]
+        for index in range(count):
+            size = pieces[index].shape[1]
+            if isinstance(starts[index], int):
+                out_ref[:, starts[index]:starts[index] + size] = refs[index][...]
+            else:
+                out_ref[:, pl.ds(pl.multiple_of(where_ref[1 + index] * 128, 128), size)] = refs[index][...]
+
+    where = jnp.stack([jnp.asarray(row_start // step, jnp.int32)] + [jnp.asarray(s // 128, jnp.int32) for s in starts])
+    in_specs = [pl.BlockSpec((step, piece.shape[1]), lambda i, where_ref: (i, 0)) for piece in pieces]
+    operands = list(pieces)
+    aliases = {}
+    if buffer is not None:
+        in_specs.append(pl.BlockSpec(memory_space=pl.ANY))
+        operands.append(buffer)
+        aliases = {1 + count: 0}
+    return pl.pallas_call(
+        kernel,
+        out_shape=jax.ShapeDtypeStruct((total_rows, total_cols), F32),
+        grid_spec=pltpu.PrefetchScalarGridSpec(
+            num_scalar_prefetch=1,
+            grid=(rows // step,),
+            in_specs=in_specs,
+            out_specs=pl.BlockSpec((step, total_cols), lambda i, where_ref: (where_ref[0] + i, 0)),
+        ),
+        input_output_aliases=aliases,
+        cost_estimate=pl.CostEstimate(flops=4 * 10**9, bytes_accessed=8 * rows * total_cols, transcendentals=0),
+        compiler_params=pltpu.CompilerParams(vmem_limit_bytes=40 * 2**20),
+    )(where, *operands)
+
+
+def join_columns(parts, order, step=512):
+    count, rows, cols = parts.shape
+
+    def kernel(in_ref, out_ref):
+        out_ref[...] = in_ref[0]
+
+    return pl.pallas_call(
+        kernel,
+        out_shape=jax.ShapeDtypeStruct((rows, count * cols), F32),
+        grid=(count, rows // step),
+        in_specs=[pl.BlockSpec((1, step, cols), lambda i, j: (i, j, 0))],
+        out_specs=pl.BlockSpec((step, cols), lambda i, j: (j, order(i))),
+        cost_estimate=pl.CostEstimate(flops=4 * 10**9, bytes_accessed=8 * parts.size, transcendentals=0),
+    )(parts)
 
 
 def solution(mesh):
@@ -89,36 +147,75 @@
         act_2 = jnp.maximum((pre_2 - mean_2) * inv_2 * gain_2h + bias_2h, 0.0).astype(BF16)
         act_2_other = lax.ppermute(act_2, DATA_AXIS, pair_perm)
 
-        w_out_cols = cols_of(w_out, dev * block, block)
+        pieces = 2
+        piece = block // pieces
+        span = width // pieces
+        w_out_cols = jnp.concatenate([cols_of(w_out, k * span + dev * piece, piece) for k in range(pieces)], axis=1)
         pre_z = dot(rows_of(w_out_cols, own_start, half), act_2, 0, 0) + dot(rows_of(w_out_cols, other_start, half), act_2_other, 0, 0)
         mean_z, inv_z = stats(pre_z)
-        zh_a = (pre_z - mean_z) * inv_z
-        emb_a = zh_a.astype(BF16)
-
-        corr_mat = dot(emb_a, emb_b_all, 1, 0) / row_count
-        on_diag = lax.broadcasted_iota(jnp.int32, corr_mat.shape, 0) + dev * block == lax.broadcasted_iota(jnp.int32, corr_mat.shape, 1)
-        loss_part = jnp.sum(jnp.where(on_diag, jnp.square(1.0 - corr_mat), off_weight * jnp.square(corr_mat)))
-        grad_c = jnp.where(on_diag, -2.0 * (1.0 - corr_mat), 2.0 * off_weight * corr_mat).astype(BF16)
-
-        grad_z = norm_back(dot(grad_c, emb_b_all, 1, 1) / row_count, zh_a, inv_z).astype(BF16)
-        grad_z_all = gather(grad_z)
-        grad_emb = dot(emb_b, gather(grad_c), 1, 1) / row_count
-
-        grad_w_out = pair_gather(dot(act_2, grad_z_all, 1, 1))
+
+        loss_part = 0.0
+        grad_c_own, grad_z_own = [], []
+        for k in range(pieces):
+            pre_k, mean_k, inv_k = (v[k * piece:(k + 1) * piece] for v in (pre_z, mean_z, inv_z))
+            if k:
+                pre_k, grad_z_own[-1] = barrier((pre_k, grad_z_own[-1]))
+            zh_a = (pre_k - mean_k) * inv_k
+            corr_mat = dot(zh_a.astype(BF16), emb_b_all, 1, 0) / row_count
+            feature = lax.broadcasted_iota(jnp.int32, corr_mat.shape, 0) + (k * span + dev * piece)
+            on_diag = feature == lax.broadcasted_iota(jnp.int32, corr_mat.shape, 1)
+            loss_k = jnp.sum(jnp.where(on_diag, jnp.square(1.0 - corr_mat), off_weight * jnp.square(corr_mat)))
+            grad_c = jnp.where(on_diag, -2.0 * (1.0 - corr_mat), 2.0 * off_weight * corr_mat).astype(BF16)
+            grad_z = norm_back(dot(grad_c, emb_b_all, 1, 1) / row_count, zh_a, inv_k).astype(BF16)
+            loss_k, grad_z = barrier((loss_k, grad_z))
+            loss_part = loss_part + loss_k
+            grad_z_own.append(grad_z)
+            grad_c_own.append(grad_c)
+        grad_c_own[0], grad_c_own[1], grad_z_own[1] = barrier((grad_c_own[0], grad_c_own[1], grad_z_own[1]))
+        grad_z_all = [gather(part) for part in grad_z_own]
+        grad_c_all = [gather(part) for part in grad_c_own]
+
+        w_out_rows = rows_of(w_out, own_start, half)
+        out_own, grad_act_2 = [], None
+        for k in range(pieces):
+            grad_z_k = grad_z_all[k]
+            if k:
+                grad_z_k, grad_act_2 = barrier((grad_z_k, grad_act_2))
+            part = dot(act_2, grad_z_k, 1, 1)
+            part, grad_z_k = barrier((part, grad_z_k))
+            out_own.append(part)
+            part = dot(w_out_rows[:, k * span:(k + 1) * span], grad_z_k, 1, 0)
+            grad_act_2 = part if grad_act_2 is None else grad_act_2 + part
+        out_other = [lax.ppermute(part, DATA_AXIS, pair_perm) for part in out_own]
+        places = [k * span for k in range(pieces)]
+        grad_w_out = place_rows(None, out_own, places, own_start, width, width)
+        grad_w_out = place_rows(grad_w_out, out_other, places, other_start, width, width)
         normed_2 = (pre_2 - mean_2) * inv_2
-        grad_pre_2 = jnp.where(normed_2 * gain_2h + bias_2h > 0.0, dot(rows_of(w_out, own_start, half), grad_z_all, 1, 0), 0.0)
+        grad_pre_2 = jnp.where(normed_2 * gain_2h + bias_2h > 0.0, grad_act_2, 0.0)
         grad_u_2, affine_2 = affine_back(grad_pre_2, normed_2, inv_2, gain_2h)
-        grad_u_2_all = pair_gather(grad_u_2)
+        grad_u_2_other = lax.ppermute(grad_u_2, DATA_AXIS, pair_perm)
+
+        emb_parts = [dot(emb_b, part, 1, 1) / row_count for part in grad_c_all]
+        *emb_parts, grad_u_2_other = barrier((*emb_parts, grad_u_2_other))
+        grad_emb = place_rows(None, emb_parts, places, 0, emb_b.shape[0], width)
 
         part_start = chip * block
+        w_mid_rows = rows_of(w_mid, own_start + part_start, block)
         normed_1 = (rows_of(pre_1, part_start, block) - rows_of(mean_1, part_start, block)) * rows_of(inv_1, part_start, block)
         gain_1p, bias_1p = rows_of(gain_1h, part_start, block), rows_of(bias_1h, part_start, block)
-        grad_pre_1 = jnp.where(normed_1 * gain_1p + bias_1p > 0.0, dot(rows_of(w_mid, own_start + part_start, block), grad_u_2_all, 1, 0), 0.0)
+        grad_act_1 = dot(cols_of(w_mid_rows, own_start, half), grad_u_2, 1, 0) + dot(cols_of(w_mid_rows, other_start, half), grad_u_2_other, 1, 0)
+        grad_pre_1 = jnp.where(normed_1 * gain_1p + bias_1p > 0.0, grad_act_1, 0.0)
         grad_u_1, affine_1 = affine_back(grad_pre_1, normed_1, rows_of(inv_1, part_start, block), gain_1p)
-        grad_w_in_parts = lax.all_gather(dot(feat_all, grad_u_1, 0, 1), DATA_AXIS)
-        grad_w_mid = pair_gather(dot(act_1, grad_u_2_all, 1, 1))
-
-        grad_w_in = grad_w_in_parts.reshape(chips, 2, -1, block).transpose(2, 1, 0, 3).reshape(-1, width)
+        grad_w_in_part = with_layout_constraint(dot(feat_all, grad_u_1, 0, 1), Layout(major_to_minor=(0, 1)))
+        grad_w_in_parts = lax.all_gather(grad_w_in_part, DATA_AXIS)
+        grad_w_in = join_columns(grad_w_in_parts, lambda i: (i % 2) * chips + i // 2)
+
+        act_1, grad_w_in_part = barrier((act_1, grad_w_in_part))
+        mid_own = [dot(act_1, grad_u_2, 1, 1), dot(act_1, grad_u_2_other, 1, 1)]
+        mid_other = [lax.ppermute(part, DATA_AXIS, pair_perm) for part in mid_own]
+        grad_w_mid = place_rows(None, mid_own, [own_start, other_start], own_start, width, width)
+        grad_w_mid = place_rows(grad_w_mid, mid_other, [other_start, own_start], other_start, width, width)
+
         small = jnp.concatenate([affine_1, rows_of(affine_2, part_start, block)], axis=1).T
         small = jnp.concatenate([small, jnp.full((1, block), loss_part)], axis=0)
         small_all = lax.all_gather(small, DATA_AXIS)

time: 1960 us -> 1700 us (0.87)
  waiting for transfers between devices: 375 us -> 102 us
  local copies, waits for them, and re-layouts: 224 us -> 9.12 us
  Pallas kernels: 0 us -> 138 us
  matrix products: 1130 us -> 1210 us
    all_gather x4 -> x6, waiting for transfers between devices: 297 us -> 82.9 us  [gather(): return lax.all_gather(array, DATA_AXIS, axis=0, tiled=True)]
    pallas_call x0 -> x6, Pallas kernels: none -> 138 us  [the longest x5 104 us: place_rows(): pl.pallas_call(kernel, out_shape=jax.ShapeDtypeStruct((total_rows, total_...]
    unnamed x62 -> x70, local copies, waits for them, and re-layouts: 91.9 us -> 3.75 us
    dot_general x13 -> x20, matrix products: 1010 us -> 1100 us  [dot(): lax.dot_general(left_op, right_op, (((left_dim,), (right_dim,)), ((), ())...]
    reshape x2 -> x0, local copies, waits for them, and re-layouts: 82.3 us -> none  [local_step(): grad_w_in_parts.reshape(chips, 2, -1, block).transpose(2, 1, 0, 3)]
    all_gather x4 -> x1, waiting for transfers between devices: 56.5 us -> 0.01 us  [local_step(): grad_w_in_parts = lax.all_gather(grad_w_in_part, DATA_AXIS)]
    transpose x1 -> x0, local copies, waits for them, and re-layouts: 48.6 us -> none  [local_step(): grad_w_in_parts.reshape(chips, 2, -1, block).transpose(2, 1, 0, 3)]
  transfers between devices with their start and end apart: 10 -> 14, of which waited for: 3 -> 2; matrix products, arithmetic and copies ran while one was open for 55% -> 73% of each run, Pallas kernels for 0% -> 6%
where the time goes in v2:
time: 1700 us; the launch traced here: 1690 us
  matrix products  1210 us (71%)
  other arithmetic  156 us (9%)
  Pallas kernels  138 us (8%)
  waiting for transfers between devices  102 us (6%)
  blocking collectives  54.4 us (3%)
  between operations  17.1 us (1%)
    dot_general x20, matrix products, dot(): lax.dot_general(left_op, right_op, (((left_dim,), (right_dim,)), ((), ())...  1100 us
    pallas_call x5, Pallas kernels, place_rows(): pl.pallas_call(kernel, out_shape=jax.ShapeDtypeStruct((total_rows, total_...  104 us
    all_gather x6, waiting for transfers between devices, gather(): return lax.all_gather(array, DATA_AXIS, axis=0, tiled=True)  82.9 us
    dot_general x2, matrix products, teacher_layer(): normed = norm_rows(jnp.dot(layer_in, weight, preferred_element_type=F32))  69.3 us
    convert_element_type x1, other arithmetic, affine_back(): return (grad_u.astype(BF16), jnp.concatenate([sum_gn, sum_g], axis=1))  52.9 us
    dot_general x1, matrix products, local_step(): jnp.dot(teach_2, t_out, preferred_element_type=F32)  45.7 us
    all_gather x3, blocking collectives, norm_rows(): lax.all_gather(jnp.stack([jnp.sum(pre, axis=0), jnp.sum(pre * pre, axis=0...  43.3 us
    pallas_call x1, Pallas kernels, join_columns(): pl.pallas_call(kernel, out_shape=jax.ShapeDtypeStruct((rows, count * cols...  34.4 us
  transfers between devices with their start and end apart: 14, of which 2 were waited for; matrix products, arithmetic and copies ran while one was open for 73% of the time, Pallas kernels for 6%

profile of v2, /device:TPU:0, one launch (start us, length us, event | category | flops | bytes accessed | tf_op | source)
XLA Modules:
  0.0 1692.0 jit_solution(14123820966197580038)
XLA Ops:
  7.2 0.7 all-gather.17.cloned.1.call-update
  8.0 23.6 %fusion.66 = (f32[4096]{0:T(1024)S(1)}, f32[4096]{0:T(1024)S(1)}, f32[1024,4096]{1,0:T(8,128)}) fusion(bf16[1024,2048]{1,0:T(8,128)(2,1)} %param.14, bf16[2048,4096]{1,0:T(8,128)(2,1)} %param.18), kind=kOutput, calls=%fused_computation.151 | convolution fusion | flops 17192443904 | bytes 37781504 | tf_op jit(solution)/shard_map/dot_general | solution.py:112
  31.6 16.2 all-gather.5
  48.1 45.7 %fusion.65 = (f32[4096]{0:T(1024)S(1)}, f32[4096]{0:T(1024)S(1)}, f32[1024,4096]{1,0:T(8,128)}) fusion(bf16[4096,4096]{1,0:T(8,128)(2,1)} %param.19, f32[1024,4096]{1,0:T(8,128)} %get-tuple-element.100, f32[4096]{0:T(1024)S(1)} %copy-done.14, f32[4096]{0:T(1024)S(1)} %copy-done.16, f32[4096]{0:T(1024)S(1)} %bitcast.100, f32[4096]{0:T(1024)S(1)} %bitcast.99), kind=kOutput, calls=%fused_computation.150 | convolution fusion | flops 34397478912 | bytes 67207168 | tf_op jit(solution)/shard_map/dot_general | solution.py:112
  93.8 13.6 all-gather.6
  107.6 45.7 %fusion.64 = (f32[4096]{0:T(1024)S(1)}, f32[4096]{0:T(1024)S(1)}, f32[1024,4096]{1,0:T(8,128)}) fusion(bf16[4096,4096]{1,0:T(8,128)(2,1)} %param.20, f32[1024,4096]{1,0:T(8,128)} %get-tuple-element.101, f32[4096]{0:T(1024)S(1)} %copy-done.28, f32[4096]{0:T(1024)S(1)} %copy-done.26, f32[4096]{0:T(1024)S(1)} %bitcast.102, f32[4096]{0:T(1024)S(1)} %bitcast.101), kind=kOutput, calls=%fused_computation.149 | convolution fusion | flops 34397478912 | bytes 67207168 | tf_op jit(solution)/shard_map/dot_general | solution.py:134
  153.4 13.4 all-gather.7
  167.0 9.8 multiply_convert_fusion.2
  177.4 86.1 %fusion.62 = (f32[2048]{0:T(1024)S(1)}, f32[2048]{0:T(1024)S(1)}, f32[2048,8192]{1,0:T(8,128)}) fusion(bf16[8192,2048]{1,0:T(8,128)(2,1)} %all-gather.17.cloned.1.call-done, bf16[2048,4096]{1,0:T(8,128)(2,1)} %param.15, s32[]{:T(128)} %select_n.92), kind=kOutput, calls=%fused_computation.147 | convolution fusion | flops 68769808384 | bytes 109068800 | tf_op jit(solution)/shard_map/dot_general | solution.py:19
  263.5 33.3 %maximum_convert_fusion.1 = bf16[2048,8192]{1,0:T(8,128)(2,1)} fusion(f32[2048,8192]{1,0:T(8,128)} %get-tuple-element.103, f32[2048]{0:T(1024)S(1)} %dynamic-slice-done, f32[2048]{0:T(1024)S(1)} %dynamic-slice-done.1, f32[2048]{0:T(1024)S(1)} %get-tuple-element.93, f32[2048]{0:T(1024)S(1)} %get-tuple-element.92), kind=kLoop, calls=%fused_computation.7 | loop fusion | flops 100663296 | bytes 100696064 | tf_op jit(solution)/shard_map/convert_element_type | solution.py:141
  297.5 85.2 %fusion.22 = f32[2048,8192]{1,0:T(8,128)} fusion(bf16[2048,8192]{1,0:T(8,128)(2,1)} %maximum_convert_fusion.1, bf16[4096,4096]{1,0:T(8,128)(2,1)} %param.16, s32[]{:T(128)S(6)} %select_n.96), kind=kOutput, calls=%fused_computation.53 | convolution fusion | flops 68719476736 | bytes 109051904 | tf_op jit(solution)/shard_map/dot_general | solution.py:19
  382.8 95.5 %fusion.61 = (f32[2048]{0:T(1024)S(1)}, f32[2048]{0:T(1024)S(1)}, f32[2048,8192]{1,0:T(8,128)}) fusion(f32[2048,8192]{1,0:T(8,128)} %fusion.22, bf16[2048,8192]{1,0:T(8,128)(2,1)} %collective-permute-done, bf16[4096,4096]{1,0:T(8,128)(2,1)} %param.16, s32[]{:T(128)S(6)} %select_n.100, s32[]{:T(128)S(6)} %select_n.96), kind=kOutput, calls=%fused_computation.146 | convolution fusion | flops 68786585600 | bytes 176177152 | tf_op jit(solution)/shard_map/dot_general | solution.py:19
  478.3 0.6 fusion.49
  478.9 33.7 %maximum_convert_fusion = bf16[2048,8192]{1,0:T(8,128)(2,1)} fusion(f32[2048,8192]{1,0:T(8,128)} %get-tuple-element.104, f32[2048]{0:T(1024)S(1)} %copy-done.12, f32[2048]{0:T(1024)S(1)} %get-tuple-element.71, f32[2048]{0:T(1024)S(1)} %get-tuple-element.90, f32[2048]{0:T(1024)S(1)} %get-tuple-element.91), kind=kLoop, calls=%fused_computation.3 | loop fusion | flops 100663296 | bytes 100696064 | tf_op jit(solution)/shard_map/convert_element_type | solution.py:147
  513.5 3.8 constant_dynamic-slice_fusion
  517.4 27.4 %fusion.41 = f32[512,8192]{1,0:T(8,128)} fusion(bf16[2048,8192]{1,0:T(8,128)(2,1)} %maximum_convert_fusion, s32[]{:T(128)} %select_n.92, bf16[4096,256]{1,0:T(8,128)(2,1)} %get-tuple-element.73, bf16[4096,256]{1,0:T(8,128)(2,1)S(1)} %get-tuple-element.72), kind=kOutput, calls=%fused_computation.81 | convolution fusion | flops 17184063488 | bytes 54525956 | tf_op jit(solution)/shard_map/dot_general | solution.py:19
  544.8 17.0 %collective-permute-done.1 = bf16[2048,8192]{1,0:T(8,128)(2,1)} collective-permute-done((bf16[2048,8192]{1,0:T(8,128)(2,1)}, bf16[2048,8192]{1,0:T(8,128)(2,1)}, u32[]{:S(2)}, u32[]{:S(2)}) %collective-permute-start.1) | collective-permute-done | bytes 33554464 | tf_op jit(solution)/shard_map/ppermute | solution.py:148
  561.8 29.7 %fusion.63 = (f32[512]{0:T(512)S(1)}, f32[512]{0:T(512)S(1)}, f32[512,8192]{1,0:T(8,128)}) fusion(f32[512,8192]{1,0:T(8,128)} %fusion.41, bf16[2048,8192]{1,0:T(8,128)(2,1)} %collective-permute-done.1, s32[]{:T(128)S(6)} %select_n.99, bf16[4096,256]{1,0:T(8,128)(2,1)} %get-tuple-element.73, bf16[4096,256]{1,0:T(8,128)(2,1)S(1)} %get-tuple-element.72), kind=kOutput, calls=%fused_computation.148 | convolution fusion | flops 17200840704 | bytes 71307264 | tf_op jit(solution)/shard_map/dot_general | solution.py:19
  591.6 29.5 %select_reduce_fusion.1 = (f32[]{:T(128)}, bf16[256,4096]{1,0:T(8,128)(2,1)S(1)}) fusion(f32[]{:T(128)S(6)} %copy.34, s32[256]{0:T(256)S(1)} %iota_add_fusion.1, f32[]{:T(128)S(6)} %mul.359, bf16[8192,4096]{1,0:T(8,128)(2,1)} %all-gather.19.cloned.1.call-done, f32[512,8192]{1,0:T(8,128)} %get-tuple-element.105, f32[256]{0:T(256)S(1)} %get-tuple-element.112, ...), kind=kOutput, calls=%fused_computation.73 | convolution fusion | flops 17198743552 | bytes 77597712 | tf_op jit(solution)/shard_map/dot_general | solution.py:19
  621.1 32.3 %fusion.68 = (f32[256]{0:T(256)S(1)}, f32[256]{0:T(256)S(1)}, f32[256,8192]{1,0:T(8,128)}) fusion(f32[256]{0:T(256)S(1)} %get-tuple-element.112, f32[256]{0:T(256)S(1)} %get-tuple-element.95, f32[512,8192]{1,0:T(8,128)} %get-tuple-element.105, bf16[256,4096]{1,0:T(8,128)(2,1)S(1)} %get-tuple-element.37, bf16[8192,4096]{1,0:T(8,128)(2,1)} %all-gather.19.cloned.1.call-done), kind=kOutput, calls=%fused_computation.153 | convolution fusion | flops 17192452096 | bytes 85987328 | tf_op jit(solution)/shard_map/dot_general | solution.py:19
  653.4 14.7 multiply_convert_fusion.5
  668.2 29.6 %select_reduce_fusion = (f32[]{:T(128)}, bf16[256,4096]{1,0:T(8,128)(2,1)S(1)}) fusion(f32[]{:T(128)S(6)} %copy.34, s32[256]{0:T(256)S(1)} %iota_add_fusion, f32[]{:T(128)S(6)} %mul.359, bf16[8192,4096]{1,0:T(8,128)(2,1)} %all-gather.19.cloned.1.call-done, f32[256,8192]{1,0:T(8,128)} %get-tuple-element.29, f32[256]{0:T(256)S(1)} %get-tuple-element.113, ...), kind=kOutput, calls=%fused_computation.70 | convolution fusion | flops 17198743552 | bytes 77597712 | tf_op jit(solution)/shard_map/dot_general | solution.py:19
  697.8 33.0 %fusion.67 = (f32[256]{0:T(256)S(1)}, f32[256]{0:T(256)S(1)}, f32[256,8192]{1,0:T(8,128)}) fusion(f32[256]{0:T(256)S(1)} %get-tuple-element.113, f32[256,8192]{1,0:T(8,128)} %get-tuple-element.29, f32[256]{0:T(256)S(1)} %get-tuple-element.94, bf16[256,4096]{1,0:T(8,128)(2,1)S(1)} %get-tuple-element.38, bf16[8192,4096]{1,0:T(8,128)(2,1)} %all-gather.19.cloned.1.call-done), kind=kOutput, calls=%fused_computation.152 | convolution fusion | flops 17192452096 | bytes 85987328 | tf_op jit(solution)/shard_map/dot_general | solution.py:19
  730.8 8.6 multiply_convert_fusion.4
  740.6 82.9 %all-gather.23.cloned.1.call-done = bf16[2048,8192]{1,0:T(8,128)(2,1)} async-done(((bf16[256,8192]{1,0:T(8,128)(2,1)}), bf16[2048,8192]{1,0:T(8,128)(2,1)}) %all-gather.23.cloned.1.call-update) | async-done | bytes 33554448 | tf_op jit(solution)/shard_map/all_gather | solution.py:100
  823.5 79.9 %fusion.75.refs_0_ = f32[2048,2048]{1,0:T(8,128)} fusion(bf16[2048,8192]{1,0:T(8,128)(2,1)} %maximum_convert_fusion, bf16[2048,8192]{1,0:T(8,128)(2,1)} %all-gather.23.cloned.1.call-done), kind=kOutput, calls=%fused_computation.160 | convolution fusion | flops 68719476736 | bytes 83886080 | tf_op jit(solution)/shard_map/dot_general | solution.py:19
  903.4 79.3 %fusion.4 = f32[2048,8192]{1,0:T(8,128)} fusion(bf16[2048,8192]{1,0:T(8,128)(2,1)} %all-gather.23.cloned.1.call-done, bf16[4096,4096]{1,0:T(8,128)(2,1)} %param.17, s32[]{:T(128)} %select_n.92), kind=kOutput, calls=%fused_computation.29 | convolution fusion | flops 68719476736 | bytes 109052416 | tf_op jit(solution)/shard_map/dot_general | solution.py:19
  982.8 79.7 %fusion.76.refs_1_ = f32[2048,2048]{1,0:T(8,128)} fusion(bf16[2048,8192]{1,0:T(8,128)(2,1)} %maximum_convert_fusion, bf16[2048,8192]{1,0:T(8,128)(2,1)} %all-gather.21.cloned.1.call-done), kind=kOutput, calls=%fused_computation.161 | convolution fusion | flops 68719476736 | bytes 83886080 | tf_op jit(solution)/shard_map/dot_general | solution.py:19
  1062.5 113.1 %fusion.60 = (f32[2048]{0:T(1024)S(1)}, f32[2048]{0:T(1024)S(1)}, f32[2048,8192]{1,0:T(8,128)}) fusion(f32[2048]{0:T(1024)S(1)} %copy-done.4, f32[2048,8192]{1,0:T(8,128)} %get-tuple-element.104, f32[2048]{0:T(1024)S(1)} %copy-done.6, f32[2048,8192]{1,0:T(8,128)} %fusion.4, bf16[2048,8192]{1,0:T(8,128)(2,1)} %all-gather.21.cloned.1.call-done, ...), kind=kOutput, calls=%fused_computation.145 | convolution fusion | flops 68887248896 | bytes 243319296 | tf_op jit(solution)/shard_map/dot_general | solution.py:19
  1176.3 52.9 %multiply_convert_fusion = bf16[2048,8192]{1,0:T(8,128)(2,1)} fusion(f32[2048,8192]{1,0:T(8,128)} %get-tuple-element.108, f32[2048,8192]{1,0:T(8,128)} %get-tuple-element.104, f32[2048]{0:T(1024)S(1)} %copy-done.9, f32[2048]{0:T(1024)S(1)} %broadcast_multiply_fusion.3, f32[2048]{0:T(1024)S(1)} %broadcast_multiply_fusion.4, f32[2048]{0:T(1024)S(1)} %copy-done.4, ...), kind=kLoop, calls=%fused_computation | loop fusion | flops 117440512 | bytes 167813120 | tf_op jit(solution)/shard_map/convert_element_type | solution.py:129
  1229.5 0.8 dynamic-slice.21
  1230.2 0.8 fusion.69
  1231.0 24.7 %convolution_multiply_fusion.3.refs_0_ = f32[1024,2048]{1,0:T(8,128)} fusion(bf16[1024,4096]{1,0:T(8,128)(2,1)} %multiply_convert_fusion.2, bf16[2048,4096]{1,0:T(8,128)(2,1)} %all-gather.25.cloned.1.call-done), kind=kOutput, calls=%fused_computation.61 | convolution fusion | flops 17181966336 | bytes 33554432 | tf_op jit(solution)/shard_map/dot_general | solution.py:19
  1255.7 24.2 %convolution_multiply_fusion.2.refs_1_ = f32[1024,2048]{1,0:T(8,128)} fusion(bf16[1024,4096]{1,0:T(8,128)(2,1)} %multiply_convert_fusion.2, bf16[2048,4096]{1,0:T(8,128)(2,1)} %all-gather.27.cloned.1.call-done), kind=kOutput, calls=%fused_computation.60 | convolution fusion | flops 17181966336 | bytes 33554432 | tf_op jit(solution)/shard_map/dot_general | solution.py:19
  1279.9 27.7 %fusion.44 = f32[512,8192]{1,0:T(8,128)} fusion(bf16[2048,8192]{1,0:T(8,128)(2,1)} %multiply_convert_fusion, bf16[4096,4096]{1,0:T(8,128)(2,1)} %param.16, s32[]{:T(128)S(6)} %select_n.98, s32[]{:T(128)S(6)} %select_n.96), kind=kOutput, calls=%fused_computation.83 | convolution fusion | flops 17179869184 | bytes 52428808 | tf_op jit(solution)/shard_map/dot_general | solution.py:19
  1307.6 32.5 %multiply_reduce_fusion.3 = (f32[512]{0:T(512)S(1)}, f32[512]{0:T(512)S(1)}, f32[512,8192]{1,0:T(8,128)}) fusion(f32[2048,8192]{1,0:T(8,128)} %get-tuple-element.103, s32[]{:T(128)S(6)} %select_n.94, f32[512]{0:T(512)S(1)} %get-tuple-element.69, f32[512]{0:T(512)S(1)} %dynamic-slice.21, f32[512,8192]{1,0:T(8,128)} %fusion.44, ...), kind=kOutput, calls=%fused_computation.11 | convolution fusion | flops 17221812224 | bytes 85995536 | tf_op jit(solution)/shard_map/dot_general | solution.py:19
  1340.7 29.3 %fusion.37 = f32[2048,512]{1,0:T(8,128)} fusion(bf16[8192,2048]{1,0:T(8,128)(2,1)} %all-gather.17.cloned.1.call-done, f32[512,8192]{1,0:T(8,128)} %get-tuple-element.109, f32[2048,8192]{1,0:T(8,128)} %get-tuple-element.103, s32[]{:T(128)S(6)} %select_n.94, f32[512]{0:T(512)S(1)} %get-tuple-element.67, f32[512]{0:T(512)S(1)} %get-tuple-element.69, ...), kind=kOutput, calls=%fused_computation.78 | convolution fusion | flops 17209229312 | bytes 71313408 | tf_op jit(solution)/shard_map/dot_general | solution.py:19
  1370.6 79.7 %fusion.77.refs_0_ = f32[2048,2048]{1,0:T(8,128)} fusion(bf16[2048,8192]{1,0:T(8,128)(2,1)} %maximum_convert_fusion.1, bf16[2048,8192]{1,0:T(8,128)(2,1)} %multiply_convert_fusion), kind=kOutput, calls=%fused_computation.162 | convolution fusion | flops 68719476736 | bytes 83886080 | tf_op jit(solution)/shard_map/dot_general | solution.py:19
  1450.3 79.7 %fusion.78.refs_1_ = f32[2048,2048]{1,0:T(8,128)} fusion(bf16[2048,8192]{1,0:T(8,128)(2,1)} %maximum_convert_fusion.1, bf16[2048,8192]{1,0:T(8,128)(2,1)} %collective-permute-done.2), kind=kOutput, calls=%fused_computation.163 | convolution fusion | flops 68719476736 | bytes 83886080 | tf_op jit(solution)/shard_map/dot_general | solution.py:19
  1532.2 23.6 %shard_map.200.refs_2_ = f32[4096,4096]{1,0:T(8,128)} custom-call(s32[3]{0:T(128)S(1)} %pad_add_fusion.where_ref, f32[2048,2048]{1,0:T(8,128)} %fusion.75.refs_0_, f32[2048,2048]{1,0:T(8,128)} %fusion.76.refs_1_), custom_call_target="tpu_custom_call" | custom-call | flops 4000000000 | bytes 67108864 | tf_op jit(solution)/shard_map/pallas_call | solution.py:43
  1555.8 23.6 %shard_map.201 = f32[4096,4096]{1,0:T(8,128)} custom-call(s32[3]{0:T(128)S(1)} %get-tuple-element.110.where_ref, f32[2048,2048]{1,0:T(8,128)} %collective-permute-done.5.refs_0_, f32[2048,2048]{1,0:T(8,128)} %collective-permute-done.6.refs_1_, f32[4096,4096]{1,0:T(8,128)} %shard_map.200.refs_2_), custom_call_target="tpu_custom_call", output_to_operand_aliasing={{}: (3, {})} | custom-call | flops 4000000000 | bytes 67108864 | tf_op jit(solution)/shard_map/pallas_call | solution.py:43
  1579.4 11.1 all-gather.8
  1590.6 0.6 copy.26
  1591.2 0.6 copy.27
  1593.6 23.2 %shard_map.198.refs_2_ = f32[4096,4096]{1,0:T(8,128)} custom-call(s32[3]{0:T(128)S(1)} %pad_add_fusion.5.where_ref, f32[2048,2048]{1,0:T(8,128)} %fusion.77.refs_0_, f32[2048,2048]{1,0:T(8,128)} %fusion.78.refs_1_), custom_call_target="tpu_custom_call" | custom-call | flops 4000000000 | bytes 67108864 | tf_op jit(solution)/shard_map/pallas_call | solution.py:43
  1616.9 10.1 shard_map.196
  1627.0 23.2 %shard_map.199 = f32[4096,4096]{1,0:T(8,128)} custom-call(s32[3]{0:T(128)S(1)} %get-tuple-element.111.where_ref, f32[2048,2048]{1,0:T(8,128)} %collective-permute-done.3.refs_0_, f32[2048,2048]{1,0:T(8,128)} %collective-permute-done.4.refs_1_, f32[4096,4096]{1,0:T(8,128)} %shard_map.198.refs_2_), custom_call_target="tpu_custom_call", output_to_operand_aliasing={{}: (3, {})} | custom-call | flops 4000000000 | bytes 67108864 | tf_op jit(solution)/shard_map/pallas_call | solution.py:43
  1650.3 34.4 %shard_map.197 = f32[2048,4096]{1,0:T(8,128)} custom-call(f32[8,2048,512]{2,1,0:T(8,128)} %bitcast.88), custom_call_target="tpu_custom_call" | custom-call | flops 4000000000 | bytes 67108864 | tf_op jit(solution)/shard_map/pallas_call | solution.py:64
  (139 shorter events, 8.2 us)
Async XLA Ops:
  7.2 170.1 %all-gather.17.cloned.1.call-start = ((), (), s32[]{:S(2)}) async-start(), calls=%async_computation | async-start | bytes 37748736 | tf_op jit(solution)/shard_map/all_gather | solution.py:100
  7.9 40.1 %copy-start.14 = (f32[4096]{0:T(1024)S(1)}, f32[4096]{0:T(1024)}, u32[]{:S(2)}) copy-start(f32[4096]{0:T(1024)} %param.22) | copy-start | bytes 49156
  7.9 40.1 %copy-start.16 = (f32[4096]{0:T(1024)S(1)}, f32[4096]{0:T(1024)}, u32[]{:S(2)}) copy-start(f32[4096]{0:T(1024)} %param.21) | copy-start | bytes 49156
  7.9 583.7 %all-gather.19.cloned.1.call-start = ((), (), s32[]{:S(2)}) async-start(), calls=%async_computation.1 | async-start | bytes 75497472 | tf_op jit(solution)/shard_map/all_gather | solution.py:100
  48.0 59.6 %copy-start.26 = (f32[4096]{0:T(1024)S(1)}, f32[4096]{0:T(1024)}, u32[]{:S(2)}) copy-start(f32[4096]{0:T(1024)} %param.23) | copy-start | bytes 49156
  48.0 59.6 %copy-start.28 = (f32[4096]{0:T(1024)S(1)}, f32[4096]{0:T(1024)}, u32[]{:S(2)}) copy-start(f32[4096]{0:T(1024)} %param.24) | copy-start | bytes 49156
  176.8 646.7 %all-gather.23.cloned.1.call-start = ((), (), s32[]{:S(2)}) async-start(), calls=%async_computation.3 | async-start | bytes 37748736 | tf_op jit(solution)/shard_map/all_gather | solution.py:100
  177.3 86.1 %dynamic-slice-start = ((f32[4096]{0:T(1024)}, s32[]{:T(128)}), f32[2048]{0:T(1024)S(1)}, s32[]{:S(2)}) async-start(f32[4096]{0:T(1024)} %param.22, s32[]{:T(128)} %select_n.92), calls=%async_computation.9 | async-start | bytes 16896 | tf_op jit(solution)/shard_map/dynamic-slice.2
  177.3 86.1 %dynamic-slice-start.1 = ((f32[4096]{0:T(1024)}, s32[]{:T(128)}), f32[2048]{0:T(1024)S(1)}, s32[]{:S(2)}) async-start(f32[4096]{0:T(1024)} %param.21, s32[]{:T(128)} %select_n.92), calls=%async_computation.10 | async-start | bytes 16896 | tf_op jit(solution)/shard_map/dynamic-slice
  263.4 33.4 %copy-start.7 = (f32[2048]{0:T(1024)}, f32[2048]{0:T(1024)S(1)}, u32[]{:S(2)}) copy-start(f32[2048]{0:T(1024)S(1)} %get-tuple-element.93) | copy-start | bytes 24580
  263.5 33.4 %copy-start.8 = (f32[2048]{0:T(1024)}, f32[2048]{0:T(1024)S(1)}, u32[]{:S(2)}) copy-start(f32[2048]{0:T(1024)S(1)} %get-tuple-element.92) | copy-start | bytes 24580
  263.5 33.4 %copy-start.29 = (f32[4096]{0:T(1024)S(1)}, f32[4096]{0:T(1024)}, u32[]{:S(2)}) copy-start(f32[4096]{0:T(1024)} %param.24) | copy-start | bytes 49156
  296.9 85.9 %collective-permute-start = (bf16[2048,8192]{1,0:T(8,128)(2,1)}, bf16[2048,8192]{1,0:T(8,128)(2,1)}, u32[]{:S(2)}, u32[]{:S(2)}) collective-permute-start(bf16[2048,8192]{1,0:T(8,128)(2,1)} %maximum_convert_fusion.1), channel_id=1, source_target_pairs={{0,1},{1,0},{2,3},{3,2},{4,5},{5,4},{6,7},{7,6}} | collective-permute-start | bytes 100663304 | tf_op jit(solution)/shard_map/ppermute | solution.py:142
  382.8 95.5 %copy-start.27 = (f32[4096]{0:T(1024)S(1)}, f32[4096]{0:T(1024)}, u32[]{:S(2)}) copy-start(f32[4096]{0:T(1024)} %param.23) | copy-start | bytes 49156
  382.8 96.2 %copy-start.12 = (f32[2048]{0:T(1024)S(1)}, f32[2048]{0:T(1024)}, u32[]{:S(2)}) copy-start(f32[2048]{0:T(1024)} %dynamic-slice.27) | copy-start | bytes 24580
  478.9 33.7 %copy-start.3 = (f32[2048]{0:T(1024)}, f32[2048]{0:T(1024)S(1)}, u32[]{:S(2)}) copy-start(f32[2048]{0:T(1024)S(1)} %get-tuple-element.90) | copy-start | bytes 24580
  478.9 33.7 %copy-start.5 = (f32[2048]{0:T(1024)}, f32[2048]{0:T(1024)S(1)}, u32[]{:S(2)}) copy-start(f32[2048]{0:T(1024)S(1)} %get-tuple-element.91) | copy-start | bytes 24580
  478.9 33.7 %copy-start.10 = (f32[2048]{0:T(1024)}, f32[2048]{0:T(1024)S(1)}, u32[]{:S(2)}) copy-start(f32[2048]{0:T(1024)S(1)} %get-tuple-element.71) | copy-start | bytes 24580
  512.7 49.1 %collective-permute-start.1 = (bf16[2048,8192]{1,0:T(8,128)(2,1)}, bf16[2048,8192]{1,0:T(8,128)(2,1)}, u32[]{:S(2)}, u32[]{:S(2)}) collective-permute-start(bf16[2048,8192]{1,0:T(8,128)(2,1)} %maximum_convert_fusion), channel_id=1, source_target_pairs={{0,1},{1,0},{2,3},{3,2},{4,5},{5,4},{6,7},{7,6}} | collective-permute-start | bytes 100663304 | tf_op jit(solution)/shard_map/ppermute | solution.py:148
  621.1 32.3 %copy-start.1 = (bf16[256,4096]{1,0:T(8,128)(2,1)}, bf16[256,4096]{1,0:T(8,128)(2,1)S(1)}, u32[]{:S(2)}) copy-start(bf16[256,4096]{1,0:T(8,128)(2,1)S(1)} %get-tuple-element.37) | copy-start | bytes 6291460
  668.1 314.6 %all-gather.21.cloned.1.call-start = ((), (), s32[]{:S(2)}) async-start(), calls=%async_computation.2 | async-start | bytes 37748736 | tf_op jit(solution)/shard_map/all_gather | solution.py:100
  697.8 33.0 %copy-start.2 = (bf16[256,4096]{1,0:T(8,128)(2,1)}, bf16[256,4096]{1,0:T(8,128)(2,1)S(1)}, u32[]{:S(2)}) copy-start(bf16[256,4096]{1,0:T(8,128)(2,1)S(1)} %get-tuple-element.38) | copy-start | bytes 6291460
  739.4 491.6 %all-gather.25.cloned.1.call-start = ((), (), s32[]{:S(2)}) async-start(), calls=%async_computation.4 | async-start | bytes 18874368 | tf_op jit(solution)/shard_map/all_gather | solution.py:100
  740.0 515.7 %all-gather.27.cloned.1.call-start = ((), (), s32[]{:S(2)}) async-start(), calls=%async_computation.5 | async-start | bytes 18874368 | tf_op jit(solution)/shard_map/all_gather | solution.py:100
  740.6 909.7 %all-gather.29.cloned.1.call-start = ((), (), s32[]{:S(2)}) async-start(), calls=%async_computation.6 | async-start | bytes 37748736 | tf_op jit(solution)/shard_map/all_gather | solution.py:210
  982.7 79.8 %copy-start.4 = (f32[2048]{0:T(1024)S(1)}, f32[2048]{0:T(1024)}, u32[]{:S(2)}) copy-start(f32[2048]{0:T(1024)} %copy-done.3) | copy-start | bytes 24580
  982.7 79.8 %copy-start.6 = (f32[2048]{0:T(1024)S(1)}, f32[2048]{0:T(1024)}, u32[]{:S(2)}) copy-start(f32[2048]{0:T(1024)} %copy-done.5) | copy-start | bytes 24580
  982.7 79.8 %copy-start.11 = (f32[2048]{0:T(1024)S(1)}, f32[2048]{0:T(1024)}, u32[]{:S(2)}) copy-start(f32[2048]{0:T(1024)} %copy-done.10) | copy-start | bytes 24580
  982.7 79.8 %copy-start.13 = (f32[2048]{0:T(1024)S(1)}, f32[2048]{0:T(1024)}, u32[]{:S(2)}) copy-start(f32[2048]{0:T(1024)} %dynamic-slice.27) | copy-start | bytes 24580
  1062.5 113.8 %copy-start.9 = (f32[2048]{0:T(1024)S(1)}, f32[2048]{0:T(1024)}, u32[]{:S(2)}) copy-start(f32[2048]{0:T(1024)} %get-tuple-element.70) | copy-start | bytes 24580
  1175.7 0.6 copy-start.18
  1175.7 0.6 copy-start.20
  1176.3 53.1 %copy-start.15 = (f32[4096]{0:T(1024)S(1)}, f32[4096]{0:T(1024)}, u32[]{:S(2)}) copy-start(f32[4096]{0:T(1024)} %param.22) | copy-start | bytes 49156
  1176.3 54.0 %copy-start.17 = (f32[4096]{0:T(1024)S(1)}, f32[4096]{0:T(1024)}, u32[]{:S(2)}) copy-start(f32[4096]{0:T(1024)} %param.21) | copy-start | bytes 49156
  1229.1 78.5 %collective-permute-start.2 = (bf16[2048,8192]{1,0:T(8,128)(2,1)}, bf16[2048,8192]{1,0:T(8,128)(2,1)}, u32[]{:S(2)}, u32[]{:S(2)}) collective-permute-start(bf16[2048,8192]{1,0:T(8,128)(2,1)} %multiply_convert_fusion), channel_id=1, source_target_pairs={{0,1},{1,0},{2,3},{3,2},{4,5},{5,4},{6,7},{7,6}} | collective-permute-start | bytes 100663304 | tf_op jit(solution)/shard_map/ppermute | solution.py:196
  1340.1 0.6 copy-start.22
  1340.1 0.6 copy-start.24
  1370.0 185.7 %collective-permute-start.5 = (f32[2048,2048]{1,0:T(8,128)}, f32[2048,2048]{1,0:T(8,128)}, u32[]{:S(2)}, u32[]{:S(2)}) collective-permute-start(f32[2048,2048]{1,0:T(8,128)} %fusion.75.refs_0_), channel_id=1, source_target_pairs={{0,1},{1,0},{2,3},{3,2},{4,5},{5,4},{6,7},{7,6}} | collective-permute-start | bytes 50331656 | tf_op jit(solution)/shard_map/ppermute | solution.py:189
  1370.3 185.4 %collective-permute-start.6 = (f32[2048,2048]{1,0:T(8,128)}, f32[2048,2048]{1,0:T(8,128)}, u32[]{:S(2)}, u32[]{:S(2)}) collective-permute-start(f32[2048,2048]{1,0:T(8,128)} %fusion.76.refs_1_), channel_id=1, source_target_pairs={{0,1},{1,0},{2,3},{3,2},{4,5},{5,4},{6,7},{7,6}} | collective-permute-start | bytes 50331656 | tf_op jit(solution)/shard_map/ppermute | solution.py:189
  1450.3 81.8 %copy-start.19 = (f32[2048]{0:T(1024)S(1)}, f32[2048]{0:T(1024)}, u32[]{:S(2)}) copy-start(f32[2048]{0:T(1024)} %copy-done.18) | copy-start | bytes 24580
  1450.3 81.8 %copy-start.21 = (f32[2048]{0:T(1024)S(1)}, f32[2048]{0:T(1024)}, u32[]{:S(2)}) copy-start(f32[2048]{0:T(1024)} %copy-done.20) | copy-start | bytes 24580
  1530.1 97.0 %collective-permute-start.3 = (f32[2048,2048]{1,0:T(8,128)}, f32[2048,2048]{1,0:T(8,128)}, u32[]{:S(2)}, u32[]{:S(2)}) collective-permute-start(f32[2048,2048]{1,0:T(8,128)} %fusion.77.refs_0_), channel_id=1, source_target_pairs={{0,1},{1,0},{2,3},{3,2},{4,5},{5,4},{6,7},{7,6}} | collective-permute-start | bytes 50331656 | tf_op jit(solution)/shard_map/ppermute | solution.py:215
  1530.3 96.7 %collective-permute-start.4 = (f32[2048,2048]{1,0:T(8,128)}, f32[2048,2048]{1,0:T(8,128)}, u32[]{:S(2)}, u32[]{:S(2)}) collective-permute-start(f32[2048,2048]{1,0:T(8,128)} %fusion.78.refs_1_), channel_id=1, source_target_pairs={{0,1},{1,0},{2,3},{3,2},{4,5},{5,4},{6,7},{7,6}} | collective-permute-start | bytes 50331656 | tf_op jit(solution)/shard_map/ppermute | solution.py:215
  1532.2 84.7 %slice-start = ((s8[8388608]{0:T(1024)(128)(4,1)}), s8[4194304]{0:T(1024)(128)(4,1)S(1)}, s32[]{:S(2)}) async-start(s8[8388608]{0:T(1024)(128)(4,1)} %bitcast.86), calls=%async_computation.7 | async-start | bytes 8388608
  1555.8 23.6 %copy-start.23 = (f32[512]{0:T(512)S(1)}, f32[512]{0:T(512)}, u32[]{:S(2)}) copy-start(f32[512]{0:T(512)} %copy-done.22) | copy-start | bytes 6148
  1555.8 23.6 %copy-start.25 = (f32[512]{0:T(512)S(1)}, f32[512]{0:T(512)}, u32[]{:S(2)}) copy-start(f32[512]{0:T(512)} %copy-done.24) | copy-start | bytes 6148
  1555.8 61.1 %slice-start.1 = ((s8[8388608]{0:T(1024)(128)(4,1)}), s8[4194304]{0:T(1024)(128)(4,1)S(1)}, s32[]{:S(2)}) async-start(s8[8388608]{0:T(1024)(128)(4,1)} %bitcast.86), calls=%async_computation.8 | async-start | bytes 8388608
  1593.6 23.3 %copy-start = (s32[3]{0:T(128)S(1)}, s32[3]{0:T(128)}, u32[]{:S(2)}) copy-start(s32[3]{0:T(128)} %constant.183.clone.1.where_ref) | copy-start | bytes 40
Sparse Core Ops, SparseCore 0:
  9.8 163.0 all-gather.16
  176.9 297.1 all-gather.18
  668.2 155.2 all-gather.22
  825.2 155.2 all-gather.20
  982.1 84.0 all-gather.24
  1067.9 84.0 all-gather.26
  1370.2 155.2 all-gather.28

commit v3 on v2

--- a/solution.py
+++ b/solution.py
@@ -55,20 +55,83 @@
     )(where, *operands)
 
 
-def join_columns(parts, order, step=512):
-    count, rows, cols = parts.shape
+def join_columns(parts, rows, order, step=256):
+    count, _, cols = parts.shape
 
     def kernel(in_ref, out_ref):
-        out_ref[...] = in_ref[0]
+        for i in range(count):
+            out_ref[:, order(i) * cols:(order(i) + 1) * cols] = in_ref[i]
 
     return pl.pallas_call(
         kernel,
         out_shape=jax.ShapeDtypeStruct((rows, count * cols), F32),
-        grid=(count, rows // step),
-        in_specs=[pl.BlockSpec((1, step, cols), lambda i, j: (i, j, 0))],
-        out_specs=pl.BlockSpec((step, cols), lambda i, j: (j, order(i))),
+        grid=(rows // step,),
+        in_specs=[pl.BlockSpec((count, step, cols), lambda i: (0, i, 0))],
+        out_specs=pl.BlockSpec((step, count * cols), lambda i: (i, 0)),
         cost_estimate=pl.CostEstimate(flops=4 * 10**9, bytes_accessed=8 * parts.size, transcendentals=0),
+        compiler_params=pltpu.CompilerParams(vmem_limit_bytes=40 * 2**20),
     )(parts)
+
+
+def split_columns(array, core, blocks, step=256):
+    width = array.shape[1]
+    half, piece = width // 2, width // blocks // 2
+
+    def kernel(core_ref, in_ref, first_ref, second_ref):
+        for i in range(blocks):
+            low = 2 * i * piece
+            first_ref[:, i * piece:(i + 1) * piece] = in_ref[:, low:low + piece]
+            second_ref[:, i * piece:(i + 1) * piece] = in_ref[:, low + piece:low + 2 * piece]
+
+    out_spec = pl.BlockSpec((step, half), lambda i, core_ref: (i, 0))
+    return pl.pallas_call(
+        kernel,
+        out_shape=[jax.ShapeDtypeStruct((half, half), array.dtype)] * 2,
+        grid_spec=pltpu.PrefetchScalarGridSpec(
+            num_scalar_prefetch=1,
+            grid=(half // step,),
+            in_specs=[pl.BlockSpec((step, width), lambda i, core_ref: (core_ref[0] * (half // step) + i, 0))],
+            out_specs=[out_spec, out_spec],
+        ),
+        cost_estimate=pl.CostEstimate(flops=2 * 10**9, bytes_accessed=4 * half * width, transcendentals=0),
+    )(jnp.asarray(core, jnp.int32)[None], array)
+
+
+def place_pieces(buffer, first, second, core, blocks, step=256):
+    half, width = first.shape[0], 2 * first.shape[1]
+    piece = width // blocks // 2
+    per_block = second.shape[1] // step
+
+    def kernel(core_ref, first_ref, second_ref, *rest):
+        out_ref = rest[-1]
+        for i in range(blocks):
+            low = 2 * i * piece
+            out_ref[:, low:low + piece] = first_ref[:, i * piece:(i + 1) * piece]
+            out_ref[:, low + piece:low + 2 * piece] = second_ref[0, :, i * piece:(i + 1) * piece]
+
+    in_specs = [
+        pl.BlockSpec((step, half), lambda i, core_ref: (i, 0)),
+        pl.BlockSpec((1, step, half), lambda i, core_ref: (2 * (i // per_block) + core_ref[0], i % per_block, 0)),
+    ]
+    operands = [first, second]
+    aliases = {}
+    if buffer is not None:
+        in_specs.append(pl.BlockSpec(memory_space=pl.ANY))
+        operands.append(buffer)
+        aliases = {3: 0}
+    return pl.pallas_call(
+        kernel,
+        out_shape=jax.ShapeDtypeStruct((width, width), F32),
+        grid_spec=pltpu.PrefetchScalarGridSpec(
+            num_scalar_prefetch=1,
+            grid=(half // step,),
+            in_specs=in_specs,
+            out_specs=pl.BlockSpec((step, width), lambda i, core_ref: (core_ref[0] * (half // step) + i, 0)),
+        ),
+        input_output_aliases=aliases,
+        cost_estimate=pl.CostEstimate(flops=4 * 10**9, bytes_accessed=8 * half * width, transcendentals=0),
+        compiler_params=pltpu.CompilerParams(vmem_limit_bytes=40 * 2**20),
+    )(jnp.asarray(core, jnp.int32)[None], *operands)
 
 
 def solution(mesh):
@@ -149,20 +212,23 @@
 
         pieces = 2
         piece = block // pieces
-        span = width // pieces
-        w_out_cols = jnp.concatenate([cols_of(w_out, k * span + dev * piece, piece) for k in range(pieces)], axis=1)
-        pre_z = dot(rows_of(w_out_cols, own_start, half), act_2, 0, 0) + dot(rows_of(w_out_cols, other_start, half), act_2_other, 0, 0)
-        mean_z, inv_z = stats(pre_z)
+        w_out_cols = cols_of(w_out, dev * block, block)
+        w_out_other = rows_of(w_out_cols, other_start, half)
+        pre_z_own = dot(rows_of(w_out_cols, own_start, half), act_2, 0, 0)
+        w_out_pieces = list(split_columns(w_out, core, shards))
+        act_2_other, w_out_pieces[0] = barrier((act_2_other, w_out_pieces[0]))
 
         loss_part = 0.0
         grad_c_own, grad_z_own = [], []
         for k in range(pieces):
-            pre_k, mean_k, inv_k = (v[k * piece:(k + 1) * piece] for v in (pre_z, mean_z, inv_z))
+            w_k, pre_k = w_out_other[:, k * piece:(k + 1) * piece], pre_z_own[k * piece:(k + 1) * piece]
             if k:
-                pre_k, grad_z_own[-1] = barrier((pre_k, grad_z_own[-1]))
+                w_k, pre_k, grad_z_own[-1] = barrier((w_k, pre_k, grad_z_own[-1]))
+            pre_k = pre_k + dot(w_k, act_2_other, 0, 0)
+            mean_k, inv_k = stats(pre_k)
             zh_a = (pre_k - mean_k) * inv_k
             corr_mat = dot(zh_a.astype(BF16), emb_b_all, 1, 0) / row_count
-            feature = lax.broadcasted_iota(jnp.int32, corr_mat.shape, 0) + (k * span + dev * piece)
+            feature = lax.broadcasted_iota(jnp.int32, corr_mat.shape, 0) + (dev * block + k * piece)
             on_diag = feature == lax.broadcasted_iota(jnp.int32, corr_mat.shape, 1)
             loss_k = jnp.sum(jnp.where(on_diag, jnp.square(1.0 - corr_mat), off_weight * jnp.square(corr_mat)))
             grad_c = jnp.where(on_diag, -2.0 * (1.0 - corr_mat), 2.0 * off_weight * corr_mat).astype(BF16)
@@ -173,33 +239,28 @@
             grad_c_own.append(grad_c)
         grad_c_own[0], grad_c_own[1], grad_z_own[1] = barrier((grad_c_own[0], grad_c_own[1], grad_z_own[1]))
         grad_z_all = [gather(part) for part in grad_z_own]
-        grad_c_all = [gather(part) for part in grad_c_own]
-
-        w_out_rows = rows_of(w_out, own_start, half)
-        out_own, grad_act_2 = [], None
-        for k in range(pieces):
-            grad_z_k = grad_z_all[k]
-            if k:
-                grad_z_k, grad_act_2 = barrier((grad_z_k, grad_act_2))
-            part = dot(act_2, grad_z_k, 1, 1)
-            part, grad_z_k = barrier((part, grad_z_k))
-            out_own.append(part)
-            part = dot(w_out_rows[:, k * span:(k + 1) * span], grad_z_k, 1, 0)
-            grad_act_2 = part if grad_act_2 is None else grad_act_2 + part
-        out_other = [lax.ppermute(part, DATA_AXIS, pair_perm) for part in out_own]
-        places = [k * span for k in range(pieces)]
-        grad_w_out = place_rows(None, out_own, places, own_start, width, width)
-        grad_w_out = place_rows(grad_w_out, out_other, places, other_start, width, width)
+        grad_c_all = gather(jnp.concatenate(grad_c_own, axis=0))
+
+        part_start = chip * block
+        out_first = dot(act_2, grad_z_all[0], 1, 1)
+        out_first, grad_z_first = barrier((out_first, grad_z_all[0]))
+        grad_act_2 = dot(w_out_pieces[0], grad_z_first, 1, 0)
+        grad_act_2, grad_z_second = barrier((grad_act_2, grad_z_all[1]))
+        out_second = dot(rows_of(act_2, part_start, block), grad_z_second, 1, 1)
+        out_second, grad_z_second = barrier((out_second, grad_z_second))
+        grad_act_2 = grad_act_2 + dot(w_out_pieces[1], grad_z_second, 1, 0)
+        out_first_other = lax.ppermute(out_first, DATA_AXIS, pair_perm)
+        out_second_all = lax.all_gather(out_second, DATA_AXIS)
+        grad_w_out = place_pieces(None, out_first, out_second_all, core, shards)
+        grad_w_out = place_pieces(grad_w_out, out_first_other, out_second_all, 1 - core, shards)
         normed_2 = (pre_2 - mean_2) * inv_2
         grad_pre_2 = jnp.where(normed_2 * gain_2h + bias_2h > 0.0, grad_act_2, 0.0)
         grad_u_2, affine_2 = affine_back(grad_pre_2, normed_2, inv_2, gain_2h)
         grad_u_2_other = lax.ppermute(grad_u_2, DATA_AXIS, pair_perm)
 
-        emb_parts = [dot(emb_b, part, 1, 1) / row_count for part in grad_c_all]
-        *emb_parts, grad_u_2_other = barrier((*emb_parts, grad_u_2_other))
-        grad_emb = place_rows(None, emb_parts, places, 0, emb_b.shape[0], width)
-
-        part_start = chip * block
+        grad_emb = dot(emb_b, grad_c_all, 1, 1) / row_count
+        grad_emb, grad_u_2_other = barrier((grad_emb, grad_u_2_other))
+
         w_mid_rows = rows_of(w_mid, own_start + part_start, block)
         normed_1 = (rows_of(pre_1, part_start, block) - rows_of(mean_1, part_start, block)) * rows_of(inv_1, part_start, block)
         gain_1p, bias_1p = rows_of(gain_1h, part_start, block), rows_of(bias_1h, part_start, block)
@@ -207,20 +268,22 @@
         grad_pre_1 = jnp.where(normed_1 * gain_1p + bias_1p > 0.0, grad_act_1, 0.0)
         grad_u_1, affine_1 = affine_back(grad_pre_1, normed_1, rows_of(inv_1, part_start, block), gain_1p)
         grad_w_in_part = with_layout_constraint(dot(feat_all, grad_u_1, 0, 1), Layout(major_to_minor=(0, 1)))
-        grad_w_in_parts = lax.all_gather(grad_w_in_part, DATA_AXIS)
-        grad_w_in = join_columns(grad_w_in_parts, lambda i: (i % 2) * chips + i // 2)
+        small = jnp.concatenate([affine_1, rows_of(affine_2, part_start, block)], axis=1).T
+        small = jnp.concatenate([small, jnp.full((4, block), loss_part)], axis=0)
+        gathered = lax.all_gather(jnp.concatenate([grad_w_in_part, small], axis=0), DATA_AXIS)
+        features = grad_w_in_part.shape[0]
+        grad_w_in = join_columns(gathered, features, lambda i: (i % 2) * chips + i // 2)
+        small_all = gathered[:, features:features + 5]
+        vectors = small_all.reshape(chips, 2, 5, block).transpose(2, 1, 0, 3).reshape(5, width)
+        loss_value = jnp.sum(small_all[:, 4, 0])
 
         act_1, grad_w_in_part = barrier((act_1, grad_w_in_part))
         mid_own = [dot(act_1, grad_u_2, 1, 1), dot(act_1, grad_u_2_other, 1, 1)]
         mid_other = [lax.ppermute(part, DATA_AXIS, pair_perm) for part in mid_own]
         grad_w_mid = place_rows(None, mid_own, [own_start, other_start], own_start, width, width)
+        mid_other[0], mid_other[1], grad_w_out = barrier((mid_other[0], mid_other[1], grad_w_out))
         grad_w_mid = place_rows(grad_w_mid, mid_other, [other_start, own_start], other_start, width, width)
 
-        small = jnp.concatenate([affine_1, rows_of(affine_2, part_start, block)], axis=1).T
-        small = jnp.concatenate([small, jnp.full((1, block), loss_part)], axis=0)
-        small_all = lax.all_gather(small, DATA_AXIS)
-        vectors = small_all.reshape(chips, 2, 5, block).transpose(2, 1, 0, 3).reshape(5, width)
-        loss_value = jnp.sum(small_all[:, 4, 0])
         return (loss_value, grad_emb, grad_w_in, grad_w_mid, grad_w_out, vectors[0], vectors[1], vectors[2], vectors[3])
 
     return jax.shard_map(local_step, mesh=mesh, in_specs=(row_part, row_part) + (replicated,) * 11, out_specs=(replicated, row_part) + (replicated,) * 7, check_vma=False)

time: 1700 us -> 1600 us (0.941)
  waiting for transfers between devices: 102 us -> 60.1 us
  matrix products: 1210 us -> 1170 us
    pallas_call x0 -> x3, Pallas kernels: none -> 60 us  [the longest x2 45.8 us: place_pieces(): pl.pallas_call(kernel, out_shape=jax.ShapeDtypeStruct((width, width), F32...]
    pallas_call x5 -> x2, Pallas kernels: 104 us -> 46.5 us  [place_rows(): pl.pallas_call(kernel, out_shape=jax.ShapeDtypeStruct((total_rows, total_...]
    dot_general x20, matrix products: 1100 us -> 1050 us  [dot(): lax.dot_general(left_op, right_op, (((left_dim,), (right_dim,)), ((), ())...]
    all_gather x6 -> x5, waiting for transfers between devices: 82.9 us -> 59.3 us  [gather(): return lax.all_gather(array, DATA_AXIS, axis=0, tiled=True)]
  transfers between devices with their start and end apart: 14 -> 13, of which waited for: 2 -> 1; matrix products, arithmetic and copies ran while one was open for 73% -> 80% of each run, Pallas kernels for 6% -> 7%
where the time goes in v3:
time: 1600 us
  matrix products  1170 us (73%)
  other arithmetic  154 us (10%)
  Pallas kernels  129 us (8%)
  waiting for transfers between devices  60.1 us (4%)
  blocking collectives  43.2 us (3%)
  local copies, waits for them, and re-layouts  25.3 us (2%)
  between operations  17 us (1%)
    dot_general x20, matrix products, dot(): lax.dot_general(left_op, right_op, (((left_dim,), (right_dim,)), ((), ())...  1050 us
    dot_general x2, matrix products, teacher_layer(): normed = norm_rows(jnp.dot(layer_in, weight, preferred_element_type=F32))  69.3 us
    all_gather x5, waiting for transfers between devices, gather(): return lax.all_gather(array, DATA_AXIS, axis=0, tiled=True)  59.3 us
    convert_element_type x1, other arithmetic, affine_back(): return (grad_u.astype(BF16), jnp.concatenate([sum_gn, sum_g], axis=1))  52.9 us
    pallas_call x2, Pallas kernels, place_rows(): pl.pallas_call(kernel, out_shape=jax.ShapeDtypeStruct((total_rows, total_...  46.5 us
    pallas_call x2, Pallas kernels, place_pieces(): pl.pallas_call(kernel, out_shape=jax.ShapeDtypeStruct((width, width), F32...  45.8 us
    dot_general x1, matrix products, local_step(): jnp.dot(teach_2, t_out, preferred_element_type=F32)  45.7 us
    all_gather x3, blocking collectives, norm_rows(): lax.all_gather(jnp.stack([jnp.sum(pre, axis=0), jnp.sum(pre * pre, axis=0...  43.2 us
  transfers between devices with their start and end apart: 13, of which 1 were waited for; matrix products, arithmetic and copies ran while one was open for 80% of the time, Pallas kernels for 7%

profile of v3, /device:TPU:0, one launch (start us, length us, event | category | flops | bytes accessed | tf_op | source)
XLA Modules:
  0.0 1595.7 jit_solution(3933241681859998486)
XLA Ops:
  7.2 0.7 all-gather.16.cloned.1.call-update
  8.0 23.6 %fusion.58 = (f32[4096]{0:T(1024)S(1)}, f32[4096]{0:T(1024)S(1)}, f32[1024,4096]{1,0:T(8,128)}) fusion(bf16[1024,2048]{1,0:T(8,128)(2,1)} %param.14, bf16[2048,4096]{1,0:T(8,128)(2,1)} %param.18), kind=kOutput, calls=%fused_computation.138 | convolution fusion | flops 17192443904 | bytes 37781504 | tf_op jit(solution)/shard_map/dot_general | solution.py:175
  31.6 16.2 %all-gather.5 = f32[8,2,4096]{2,1,0:T(2,128)S(1)} all-gather(f32[1,2,4096]{2,1,0:T(2,128)S(1)} %maximum_bitcast_fusion), channel_id=2, replica_groups=mesh['data'=8] {'data'}, dimensions={0}, use_global_device_ids=true | all-gather | bytes 294912 | tf_op jit(solution)/shard_map/all_gather | solution.py:169
  48.1 45.7 %fusion.57 = (f32[4096]{0:T(1024)S(1)}, f32[4096]{0:T(1024)S(1)}, f32[1024,4096]{1,0:T(8,128)}) fusion(bf16[4096,4096]{1,0:T(8,128)(2,1)} %param.19, f32[1024,4096]{1,0:T(8,128)} %get-tuple-element.112, f32[4096]{0:T(1024)S(1)} %copy-done.13, f32[4096]{0:T(1024)S(1)} %copy-done.11, f32[4096]{0:T(1024)S(1)} %bitcast.102, f32[4096]{0:T(1024)S(1)} %bitcast.101), kind=kOutput, calls=%fused_computation.137 | convolution fusion | flops 34397478912 | bytes 67207168 | tf_op jit(solution)/shard_map/dot_general | solution.py:175
  93.8 13.6 all-gather.6
  107.6 45.7 %fusion.56 = (f32[4096]{0:T(1024)S(1)}, f32[4096]{0:T(1024)S(1)}, f32[1024,4096]{1,0:T(8,128)}) fusion(bf16[4096,4096]{1,0:T(8,128)(2,1)} %param.20, f32[1024,4096]{1,0:T(8,128)} %get-tuple-element.113, f32[4096]{0:T(1024)S(1)} %copy-done.17, f32[4096]{0:T(1024)S(1)} %copy-done.15, f32[4096]{0:T(1024)S(1)} %bitcast.104, f32[4096]{0:T(1024)S(1)} %bitcast.103), kind=kOutput, calls=%fused_computation.136 | convolution fusion | flops 34397478912 | bytes 67207168 | tf_op jit(solution)/shard_map/dot_general | solution.py:197
  153.4 13.4 all-gather.7
  167.0 9.7 multiply_convert_fusion.2
  177.0 86.1 %fusion.54 = (f32[2048]{0:T(1024)S(1)}, f32[2048]{0:T(1024)S(1)}, f32[2048,8192]{1,0:T(8,128)}) fusion(bf16[8192,2048]{1,0:T(8,128)(2,1)} %all-gather.16.cloned.1.call-done, bf16[2048,4096]{1,0:T(8,128)(2,1)} %param.15, s32[]{:T(128)} %select_n.89), kind=kOutput, calls=%fused_computation.134 | convolution fusion | flops 68769808384 | bytes 109068800 | tf_op jit(solution)/shard_map/dot_general | solution.py:19
  263.2 33.3 %maximum_convert_fusion.1 = bf16[2048,8192]{1,0:T(8,128)(2,1)} fusion(f32[2048,8192]{1,0:T(8,128)} %get-tuple-element.110, f32[2048]{0:T(1024)S(1)} %dynamic-slice-done.1, f32[2048]{0:T(1024)S(1)} %dynamic-slice-done, f32[2048]{0:T(1024)S(1)} %get-tuple-element.105, f32[2048]{0:T(1024)S(1)} %get-tuple-element.104), kind=kLoop, calls=%fused_computation.7 | loop fusion | flops 100663296 | bytes 100696064 | tf_op jit(solution)/shard_map/convert_element_type | solution.py:204
  297.2 85.5 %fusion.20 = f32[2048,8192]{1,0:T(8,128)} fusion(bf16[2048,8192]{1,0:T(8,128)(2,1)} %maximum_convert_fusion.1, bf16[4096,4096]{1,0:T(8,128)(2,1)} %param.16, s32[]{:T(128)S(6)} %select_n.93), kind=kOutput, calls=%fused_computation.54 | convolution fusion | flops 68719476736 | bytes 109051904 | tf_op jit(solution)/shard_map/dot_general | solution.py:19
  382.7 95.5 %fusion.53 = (f32[2048]{0:T(1024)S(1)}, f32[2048]{0:T(1024)S(1)}, f32[2048,8192]{1,0:T(8,128)}) fusion(f32[2048,8192]{1,0:T(8,128)} %fusion.20, bf16[2048,8192]{1,0:T(8,128)(2,1)} %collective-permute-done, bf16[4096,4096]{1,0:T(8,128)(2,1)} %param.16, s32[]{:T(128)S(6)} %select_n.97, s32[]{:T(128)S(6)} %select_n.93), kind=kOutput, calls=%fused_computation.133 | convolution fusion | flops 68786585600 | bytes 176177152 | tf_op jit(solution)/shard_map/dot_general | solution.py:19
  478.8 33.5 %maximum_convert_fusion = bf16[2048,8192]{1,0:T(8,128)(2,1)} fusion(f32[2048,8192]{1,0:T(8,128)} %get-tuple-element.111, f32[2048]{0:T(1024)S(1)} %copy-done.9, f32[2048]{0:T(1024)S(1)} %get-tuple-element.87, f32[2048]{0:T(1024)S(1)} %get-tuple-element.102, f32[2048]{0:T(1024)S(1)} %get-tuple-element.103), kind=kLoop, calls=%fused_computation.3 | loop fusion | flops 100663296 | bytes 100696064 | tf_op jit(solution)/shard_map/convert_element_type | solution.py:210
  513.2 2.0 dynamic-slice.29
  515.2 14.2 shard_map.196
  529.5 28.3 %fusion.37 = f32[512,8192]{1,0:T(8,128)} fusion(bf16[2048,8192]{1,0:T(8,128)(2,1)} %maximum_convert_fusion, bf16[4096,4096]{1,0:T(8,128)(2,1)} %in_ref.1, s32[]{:T(128)S(6)} %select_n.93, s32[]{:T(128)S(6)} %select_n.99), kind=kOutput, calls=%fused_computation.76 | convolution fusion | flops 17179869184 | bytes 52428808 | tf_op jit(solution)/shard_map/dot_general | solution.py:19
  557.8 7.6 slice.75
  565.4 21.0 %fusion.62 = (f32[256]{0:T(256)S(1)}, f32[256]{0:T(256)S(1)}, f32[256,8192]{1,0:T(8,128)}) fusion(bf16[2048,8192]{1,0:T(8,128)(2,1)} %collective-permute-done.1, bf16[4096,4096]{1,0:T(8,128)(2,1)} %in_ref.1, s32[]{:T(128)S(6)} %select_n.97, s32[]{:T(128)S(6)} %select_n.99, f32[512,8192]{1,0:T(8,128)} %fusion.37), kind=kOutput, calls=%fused_computation.142 | convolution fusion | flops 8598323200 | bytes 51382280 | tf_op jit(solution)/shard_map/dot_general | solution.py:19
  586.4 29.5 %select_convert_fusion.1 = (bf16[256,4096]{1,0:T(8,128)(2,1)S(1)}, f32[]{:T(128)}) fusion(f32[]{:T(128)S(6)} %mul.362, s32[256]{0:T(256)S(1)} %iota_add_fusion.1, f32[]{:T(128)S(6)} %copy.34, bf16[8192,4096]{1,0:T(8,128)(2,1)} %all-gather.18.cloned.1.call-done, f32[256,8192]{1,0:T(8,128)} %get-tuple-element.115, f32[256]{0:T(256)S(1)} %get-tuple-element.109, ...), kind=kOutput, calls=%fused_computation.69 | convolution fusion | flops 17198743552 | bytes 77597712 | tf_op jit(solution)/shard_map/dot_general | solution.py:19
  616.0 32.4 %fusion.61 = (f32[256]{0:T(256)S(1)}, f32[256]{0:T(256)S(1)}, f32[256,8192]{1,0:T(8,128)}) fusion(f32[256]{0:T(256)S(1)} %get-tuple-element.109, f32[256,8192]{1,0:T(8,128)} %get-tuple-element.115, f32[256]{0:T(256)S(1)} %get-tuple-element.108, bf16[256,4096]{1,0:T(8,128)(2,1)S(1)} %get-tuple-element.49, bf16[8192,4096]{1,0:T(8,128)(2,1)} %all-gather.18.cloned.1.call-done), kind=kOutput, calls=%fused_computation.141 | convolution fusion | flops 17192452096 | bytes 85987328 | tf_op jit(solution)/shard_map/dot_general | solution.py:19
  648.4 8.6 multiply_convert_fusion.5
  657.1 20.0 %fusion.60 = (f32[256]{0:T(256)S(1)}, f32[256]{0:T(256)S(1)}, f32[256,8192]{1,0:T(8,128)}) fusion(f32[256,8192]{1,0:T(8,128)} %slice.75, bf16[2048,256]{1,0:T(8,128)(2,1)S(1)} %dynamic-slice.29, bf16[2048,8192]{1,0:T(8,128)(2,1)} %collective-permute-done.1), kind=kOutput, calls=%fused_computation.140 | convolution fusion | flops 8598323200 | bytes 51382272 | tf_op jit(solution)/shard_map/dot_general | solution.py:19
  677.0 30.5 %select_reduce_fusion = (f32[]{:T(128)}, bf16[256,4096]{1,0:T(8,128)(2,1)}) fusion(s32[256]{0:T(256)S(1)} %iota_add_fusion, f32[]{:T(128)S(6)} %copy.34, f32[]{:T(128)S(6)} %mul.362, bf16[8192,4096]{1,0:T(8,128)(2,1)} %all-gather.18.cloned.1.call-done, f32[256,8192]{1,0:T(8,128)} %get-tuple-element.117, f32[256]{0:T(256)S(1)} %get-tuple-element.107, ...), kind=kOutput, calls=%fused_computation.64 | convolution fusion | flops 17198743552 | bytes 77597712 | tf_op jit(solution)/shard_map/dot_general | solution.py:19
  707.5 32.8 %fusion.59 = (f32[256]{0:T(256)S(1)}, f32[256]{0:T(256)S(1)}, f32[256,8192]{1,0:T(8,128)}) fusion(f32[256]{0:T(256)S(1)} %get-tuple-element.107, f32[256,8192]{1,0:T(8,128)} %get-tuple-element.117, f32[256]{0:T(256)S(1)} %get-tuple-element.106, bf16[256,4096]{1,0:T(8,128)(2,1)} %get-tuple-element.50, bf16[8192,4096]{1,0:T(8,128)(2,1)} %all-gather.18.cloned.1.call-done), kind=kOutput, calls=%fused_computation.139 | convolution fusion | flops 17192452096 | bytes 85987328 | tf_op jit(solution)/shard_map/dot_general | solution.py:19
  740.4 8.6 multiply_convert_fusion.4
  749.1 4.0 pad_maximum_fusion
  753.2 59.2 %all-gather.20.cloned.1.call-done = bf16[2048,8192]{1,0:T(8,128)(2,1)} async-done(((bf16[256,8192]{1,0:T(8,128)(2,1)}), bf16[2048,8192]{1,0:T(8,128)(2,1)}) %all-gather.20.cloned.1.call-update) | async-done | bytes 33554448 | tf_op jit(solution)/shard_map/all_gather | solution.py:163
  812.4 79.4 %fusion.67.first_ref = f32[2048,2048]{1,0:T(8,128)} fusion(bf16[2048,8192]{1,0:T(8,128)(2,1)} %maximum_convert_fusion, bf16[2048,8192]{1,0:T(8,128)(2,1)} %all-gather.20.cloned.1.call-done), kind=kOutput, calls=%fused_computation.147 | convolution fusion | flops 68719476736 | bytes 83886080 | tf_op jit(solution)/shard_map/dot_general | solution.py:19
  891.7 79.2 %fusion.68 = f32[2048,8192]{1,0:T(8,128)} fusion(bf16[2048,2048]{1,0:T(8,128)(2,1)} %get-tuple-element.36, bf16[2048,8192]{1,0:T(8,128)(2,1)} %all-gather.20.cloned.1.call-done), kind=kOutput, calls=%fused_computation.148 | convolution fusion | flops 68719476736 | bytes 109051904 | tf_op jit(solution)/shard_map/dot_general | solution.py:19
  971.0 25.3 %fusion.7 = f32[512,2048]{1,0:T(8,128)} fusion(bf16[2048,8192]{1,0:T(8,128)(2,1)} %all-gather.22.cloned.1.call-done, bf16[2048,8192]{1,0:T(8,128)(2,1)} %maximum_convert_fusion, s32[]{:T(128)S(6)} %select_n.91), kind=kOutput, calls=%fused_computation.33 | convolution fusion | flops 17179869184 | bytes 46137348 | tf_op jit(solution)/shard_map/dot_general | solution.py:19
  996.4 112.9 %fusion.52 = (f32[2048]{0:T(1024)S(1)}, f32[2048]{0:T(1024)S(1)}, f32[2048,8192]{1,0:T(8,128)}) fusion(f32[2048]{0:T(1024)S(1)} %copy-done.1, f32[2048,8192]{1,0:T(8,128)} %get-tuple-element.111, f32[2048]{0:T(1024)S(1)} %copy-done.3, f32[2048,8192]{1,0:T(8,128)} %fusion.68, bf16[2048,2048]{1,0:T(8,128)(2,1)} %get-tuple-element.46, ...), kind=kOutput, calls=%fused_computation.132 | convolution fusion | flops 68887248896 | bytes 243318784 | tf_op jit(solution)/shard_map/dot_general | solution.py:19
  1109.4 52.9 %multiply_convert_fusion = bf16[2048,8192]{1,0:T(8,128)(2,1)} fusion(f32[2048,8192]{1,0:T(8,128)} %get-tuple-element.119, f32[2048,8192]{1,0:T(8,128)} %get-tuple-element.111, f32[2048]{0:T(1024)S(1)} %copy-done.6, f32[2048]{0:T(1024)S(1)} %broadcast_multiply_fusion.3, f32[2048]{0:T(1024)S(1)} %broadcast_multiply_fusion.4, f32[2048]{0:T(1024)S(1)} %copy-done.1, ...), kind=kLoop, calls=%fused_computation | loop fusion | flops 117440512 | bytes 167813120 | tf_op jit(solution)/shard_map/convert_element_type | solution.py:192
  1162.6 0.8 dynamic-slice.21
  1163.4 0.8 fusion.63
  1165.5 27.6 %fusion.39 = f32[512,8192]{1,0:T(8,128)} fusion(bf16[2048,8192]{1,0:T(8,128)(2,1)} %multiply_convert_fusion, bf16[4096,4096]{1,0:T(8,128)(2,1)} %param.16, s32[]{:T(128)S(6)} %select_n.95, s32[]{:T(128)S(6)} %select_n.93), kind=kOutput, calls=%fused_computation.78 | convolution fusion | flops 17179869184 | bytes 52428808 | tf_op jit(solution)/shard_map/dot_general | solution.py:19
  1193.0 43.3 %convolution_multiply_fusion.2 = f32[1024,4096]{1,0:T(8,128)} fusion(bf16[1024,4096]{1,0:T(8,128)(2,1)} %multiply_convert_fusion.2, bf16[4096,4096]{1,0:T(8,128)(2,1)} %all-gather.24.cloned.1.call-done), kind=kOutput, calls=%fused_computation.25 | convolution fusion | flops 34363932672 | bytes 58720256 | tf_op jit(solution)/shard_map/dot_general | solution.py:19
  1236.4 32.5 %fusion.55 = (f32[512]{0:T(512)S(1)}, f32[512]{0:T(512)S(1)}, f32[512,8192]{1,0:T(8,128)}) fusion(f32[512]{0:T(512)S(1)} %get-tuple-element.85, f32[512]{0:T(512)S(1)} %dynamic-slice.21, f32[2048,8192]{1,0:T(8,128)} %get-tuple-element.110, s32[]{:T(128)S(6)} %select_n.91, f32[512,8192]{1,0:T(8,128)} %fusion.39, ...), kind=kOutput, calls=%fused_computation.135 | convolution fusion | flops 17221812224 | bytes 85995536 | tf_op jit(solution)/shard_map/dot_general | solution.py:19
  1268.9 29.3 %fusion.35 = f32[2048,512]{1,0:T(8,128)} fusion(bf16[8192,2048]{1,0:T(8,128)(2,1)} %all-gather.16.cloned.1.call-done, f32[512,8192]{1,0:T(8,128)} %get-tuple-element.120, f32[2048,8192]{1,0:T(8,128)} %get-tuple-element.110, s32[]{:T(128)S(6)} %select_n.91, f32[512]{0:T(512)S(1)} %get-tuple-element.83, f32[512]{0:T(512)S(1)} %get-tuple-element.85, ...), kind=kOutput, calls=%fused_computation.74 | convolution fusion | flops 17209229312 | bytes 71313408 | tf_op jit(solution)/shard_map/dot_general | solution.py:19
  1298.2 10.7 concatenate.15
  1309.2 79.3 %fusion.70.refs_1_ = f32[2048,2048]{1,0:T(8,128)} fusion(bf16[2048,8192]{1,0:T(8,128)(2,1)} %maximum_convert_fusion.1, bf16[2048,8192]{1,0:T(8,128)(2,1)} %collective-permute-done.2), kind=kOutput, calls=%fused_computation.150 | convolution fusion | flops 68719476736 | bytes 83886080 | tf_op jit(solution)/shard_map/dot_general | solution.py:19
  1388.6 79.6 %fusion.69.refs_0_ = f32[2048,2048]{1,0:T(8,128)} fusion(bf16[2048,8192]{1,0:T(8,128)(2,1)} %maximum_convert_fusion.1, bf16[2048,8192]{1,0:T(8,128)(2,1)} %multiply_convert_fusion), kind=kOutput, calls=%fused_computation.149 | convolution fusion | flops 68719476736 | bytes 83886080 | tf_op jit(solution)/shard_map/dot_general | solution.py:19
  1468.8 23.3 %shard_map.200.refs_2_ = f32[4096,4096]{1,0:T(8,128)} custom-call(s32[3]{0:T(128)S(1)} %pad_add_fusion.1.where_ref, f32[2048,2048]{1,0:T(8,128)} %fusion.69.refs_0_, f32[2048,2048]{1,0:T(8,128)} %fusion.70.refs_1_), custom_call_target="tpu_custom_call" | custom-call | flops 4000000000 | bytes 67108864 | tf_op jit(solution)/shard_map/pallas_call | solution.py:43
  1492.1 22.9 %shard_map.198.rest_0_ = f32[4096,4096]{1,0:T(8,128)} custom-call(s32[1]{0:T(128)} %bitcast.core_ref, f32[2048,2048]{1,0:T(8,128)} %fusion.67.first_ref, f32[8,512,2048]{2,1,0:T(8,128)} %bitcast.86), custom_call_target="tpu_custom_call" | custom-call | flops 4000000000 | bytes 67108864 | tf_op jit(solution)/shard_map/pallas_call | solution.py:122
  1515.0 22.9 %shard_map.199 = f32[4096,4096]{1,0:T(8,128)} custom-call(s32[1]{0:T(128)} %bitcast.26.core_ref, f32[2048,2048]{1,0:T(8,128)} %collective-permute-done.5.first_ref, f32[8,512,2048]{2,1,0:T(8,128)} %bitcast.87, f32[4096,4096]{1,0:T(8,128)} %shard_map.198.rest_0_), custom_call_target="tpu_custom_call", output_to_operand_aliasing={{}: (3, {})} | custom-call | flops 4000000000 | bytes 67108864 | tf_op jit(solution)/shard_map/pallas_call | solution.py:122
  1537.8 23.3 %shard_map.201 = f32[4096,4096]{1,0:T(8,128)} custom-call(s32[3]{0:T(128)S(1)} %pad_add_fusion.where_ref, f32[2048,2048]{1,0:T(8,128)} %collective-permute-done.3.refs_0_, f32[2048,2048]{1,0:T(8,128)} %collective-permute-done.4.refs_1_, f32[4096,4096]{1,0:T(8,128)} %shard_map.200.refs_2_), custom_call_target="tpu_custom_call", output_to_operand_aliasing={{}: (3, {})} | custom-call | flops 4000000000 | bytes 67108864 | tf_op jit(solution)/shard_map/pallas_call | solution.py:43
  1561.1 22.5 %shard_map.197 = f32[2048,4096]{1,0:T(8,128)} custom-call(f32[8,2056,512]{2,1,0:T(8,128)} %bitcast.88), custom_call_target="tpu_custom_call" | custom-call | flops 4000000000 | bytes 67371008 | tf_op jit(solution)/shard_map/pallas_call | solution.py:65
  1583.7 0.9 slice.84
  1584.6 1.4 slice_reduce_fusion
  (111 shorter events, 6.7 us)
Async XLA Ops:
  7.2 169.8 %all-gather.16.cloned.1.call-start = ((), (), s32[]{:S(2)}) async-start(), calls=%async_computation | async-start | bytes 37748736 | tf_op jit(solution)/shard_map/all_gather | solution.py:163
  7.9 40.1 %copy-start.11 = (f32[4096]{0:T(1024)S(1)}, f32[4096]{0:T(1024)}, u32[]{:S(2)}) copy-start(f32[4096]{0:T(1024)} %param.21) | copy-start | bytes 49156
  7.9 40.1 %copy-start.13 = (f32[4096]{0:T(1024)S(1)}, f32[4096]{0:T(1024)}, u32[]{:S(2)}) copy-start(f32[4096]{0:T(1024)} %param.22) | copy-start | bytes 49156
  7.9 578.5 %all-gather.18.cloned.1.call-start = ((), (), s32[]{:S(2)}) async-start(), calls=%async_computation.1 | async-start | bytes 75497472 | tf_op jit(solution)/shard_map/all_gather | solution.py:163
  48.0 59.6 %copy-start.15 = (f32[4096]{0:T(1024)S(1)}, f32[4096]{0:T(1024)}, u32[]{:S(2)}) copy-start(f32[4096]{0:T(1024)} %param.23) | copy-start | bytes 49156
  48.0 59.6 %copy-start.17 = (f32[4096]{0:T(1024)S(1)}, f32[4096]{0:T(1024)}, u32[]{:S(2)}) copy-start(f32[4096]{0:T(1024)} %param.24) | copy-start | bytes 49156
  176.7 635.7 %all-gather.20.cloned.1.call-start = ((), (), s32[]{:S(2)}) async-start(), calls=%async_computation.2 | async-start | bytes 37748736 | tf_op jit(solution)/shard_map/all_gather | solution.py:163
  177.0 86.1 %dynamic-slice-start = ((f32[4096]{0:T(1024)}, s32[]{:T(128)}), f32[2048]{0:T(1024)S(1)}, s32[]{:S(2)}) async-start(f32[4096]{0:T(1024)} %param.21, s32[]{:T(128)} %select_n.89), calls=%async_computation.7 | async-start | bytes 16896 | tf_op jit(solution)/shard_map/dynamic-slice
  177.0 86.1 %dynamic-slice-start.1 = ((f32[4096]{0:T(1024)}, s32[]{:T(128)}), f32[2048]{0:T(1024)S(1)}, s32[]{:S(2)}) async-start(f32[4096]{0:T(1024)} %param.22, s32[]{:T(128)} %select_n.89), calls=%async_computation.8 | async-start | bytes 16896 | tf_op jit(solution)/shard_map/dynamic-slice.2
  263.1 33.4 %copy-start.4 = (f32[2048]{0:T(1024)}, f32[2048]{0:T(1024)S(1)}, u32[]{:S(2)}) copy-start(f32[2048]{0:T(1024)S(1)} %get-tuple-element.105) | copy-start | bytes 24580
  263.1 33.4 %copy-start.5 = (f32[2048]{0:T(1024)}, f32[2048]{0:T(1024)S(1)}, u32[]{:S(2)}) copy-start(f32[2048]{0:T(1024)S(1)} %get-tuple-element.104) | copy-start | bytes 24580
  263.1 33.4 %copy-start.18 = (f32[4096]{0:T(1024)S(1)}, f32[4096]{0:T(1024)}, u32[]{:S(2)}) copy-start(f32[4096]{0:T(1024)} %param.24) | copy-start | bytes 49156
  296.5 86.1 %collective-permute-start = (bf16[2048,8192]{1,0:T(8,128)(2,1)}, bf16[2048,8192]{1,0:T(8,128)(2,1)}, u32[]{:S(2)}, u32[]{:S(2)}) collective-permute-start(bf16[2048,8192]{1,0:T(8,128)(2,1)} %maximum_convert_fusion.1), channel_id=1, source_target_pairs={{0,1},{1,0},{2,3},{3,2},{4,5},{5,4},{6,7},{7,6}} | collective-permute-start | bytes 100663304 | tf_op jit(solution)/shard_map/ppermute | solution.py:205
  382.7 95.5 %copy-start.16 = (f32[4096]{0:T(1024)S(1)}, f32[4096]{0:T(1024)}, u32[]{:S(2)}) copy-start(f32[4096]{0:T(1024)} %param.23) | copy-start | bytes 49156
  382.7 96.1 %copy-start.9 = (f32[2048]{0:T(1024)S(1)}, f32[2048]{0:T(1024)}, u32[]{:S(2)}) copy-start(f32[2048]{0:T(1024)} %dynamic-slice.27) | copy-start | bytes 24580
  478.8 33.5 %copy-start = (f32[2048]{0:T(1024)}, f32[2048]{0:T(1024)S(1)}, u32[]{:S(2)}) copy-start(f32[2048]{0:T(1024)S(1)} %get-tuple-element.102) | copy-start | bytes 24580
  478.8 33.5 %copy-start.2 = (f32[2048]{0:T(1024)}, f32[2048]{0:T(1024)S(1)}, u32[]{:S(2)}) copy-start(f32[2048]{0:T(1024)S(1)} %get-tuple-element.103) | copy-start | bytes 24580
  478.8 33.5 %copy-start.7 = (f32[2048]{0:T(1024)}, f32[2048]{0:T(1024)S(1)}, u32[]{:S(2)}) copy-start(f32[2048]{0:T(1024)S(1)} %get-tuple-element.87) | copy-start | bytes 24580
  512.3 53.0 %collective-permute-start.1 = (bf16[2048,8192]{1,0:T(8,128)(2,1)}, bf16[2048,8192]{1,0:T(8,128)(2,1)}, u32[]{:S(2)}, u32[]{:S(2)}) collective-permute-start(bf16[2048,8192]{1,0:T(8,128)(2,1)} %maximum_convert_fusion), channel_id=1, source_target_pairs={{0,1},{1,0},{2,3},{3,2},{4,5},{5,4},{6,7},{7,6}} | collective-permute-start | bytes 100663304 | tf_op jit(solution)/shard_map/ppermute | solution.py:211
  657.0 314.0 %all-gather.22.cloned.1.call-start = ((), (), s32[]{:S(2)}) async-start(), calls=%async_computation.3 | async-start | bytes 37748736 | tf_op jit(solution)/shard_map/all_gather | solution.py:163
  749.0 444.0 %all-gather.24.cloned.1.call-start = ((), (), s32[]{:S(2)}) async-start(), calls=%async_computation.4 | async-start | bytes 37748736 | tf_op jit(solution)/shard_map/all_gather | solution.py:163
  753.1 739.0 %all-gather.28.cloned.1.call-start = ((), (), s32[]{:S(2)}) async-start(), calls=%async_computation.6 | async-start | bytes 37748736 | tf_op jit(solution)/shard_map/all_gather | solution.py:253
  970.9 25.4 %copy-start.1 = (f32[2048]{0:T(1024)S(1)}, f32[2048]{0:T(1024)}, u32[]{:S(2)}) copy-start(f32[2048]{0:T(1024)} %copy-done) | copy-start | bytes 24580
  970.9 25.4 %copy-start.3 = (f32[2048]{0:T(1024)S(1)}, f32[2048]{0:T(1024)}, u32[]{:S(2)}) copy-start(f32[2048]{0:T(1024)} %copy-done.2) | copy-start | bytes 24580
  971.0 25.4 %copy-start.8 = (f32[2048]{0:T(1024)S(1)}, f32[2048]{0:T(1024)}, u32[]{:S(2)}) copy-start(f32[2048]{0:T(1024)} %copy-done.7) | copy-start | bytes 24580
  971.0 25.4 %copy-start.10 = (f32[2048]{0:T(1024)S(1)}, f32[2048]{0:T(1024)}, u32[]{:S(2)}) copy-start(f32[2048]{0:T(1024)} %dynamic-slice.27) | copy-start | bytes 24580
  996.3 564.8 %all-gather.26.cloned.1.call-start = ((), (), s32[]{:S(2)}) async-start(), calls=%async_computation.5 | async-start | bytes 37896192 | tf_op jit(solution)/shard_map/all_gather | solution.py:273
  996.4 112.9 %copy-start.6 = (f32[2048]{0:T(1024)S(1)}, f32[2048]{0:T(1024)}, u32[]{:S(2)}) copy-start(f32[2048]{0:T(1024)} %get-tuple-element.86) | copy-start | bytes 24580
  1109.3 53.2 %copy-start.14 = (f32[4096]{0:T(1024)S(1)}, f32[4096]{0:T(1024)}, u32[]{:S(2)}) copy-start(f32[4096]{0:T(1024)} %param.22) | copy-start | bytes 49156
  1109.4 54.0 %copy-start.12 = (f32[4096]{0:T(1024)S(1)}, f32[4096]{0:T(1024)}, u32[]{:S(2)}) copy-start(f32[4096]{0:T(1024)} %param.21) | copy-start | bytes 49156
  1162.3 74.1 %collective-permute-start.2 = (bf16[2048,8192]{1,0:T(8,128)(2,1)}, bf16[2048,8192]{1,0:T(8,128)(2,1)}, u32[]{:S(2)}, u32[]{:S(2)}) collective-permute-start(bf16[2048,8192]{1,0:T(8,128)(2,1)} %multiply_convert_fusion), channel_id=1, source_target_pairs={{0,1},{1,0},{2,3},{3,2},{4,5},{5,4},{6,7},{7,6}} | collective-permute-start | bytes 100663304 | tf_op jit(solution)/shard_map/ppermute | solution.py:259
  1308.9 206.0 %collective-permute-start.5 = (f32[2048,2048]{1,0:T(8,128)}, f32[2048,2048]{1,0:T(8,128)}, u32[]{:S(2)}, u32[]{:S(2)}) collective-permute-start(f32[2048,2048]{1,0:T(8,128)} %fusion.67.first_ref), channel_id=1, source_target_pairs={{0,1},{1,0},{2,3},{3,2},{4,5},{5,4},{6,7},{7,6}} | collective-permute-start | bytes 50331656 | tf_op jit(solution)/shard_map/ppermute | solution.py:252
  1468.2 69.7 %collective-permute-start.4 = (f32[2048,2048]{1,0:T(8,128)}, f32[2048,2048]{1,0:T(8,128)}, u32[]{:S(2)}, u32[]{:S(2)}) collective-permute-start(f32[2048,2048]{1,0:T(8,128)} %fusion.70.refs_1_), channel_id=1, source_target_pairs={{0,1},{1,0},{2,3},{3,2},{4,5},{5,4},{6,7},{7,6}} | collective-permute-start | bytes 50331656 | tf_op jit(solution)/shard_map/ppermute | solution.py:282
  1468.4 69.4 %collective-permute-start.3 = (f32[2048,2048]{1,0:T(8,128)}, f32[2048,2048]{1,0:T(8,128)}, u32[]{:S(2)}, u32[]{:S(2)}) collective-permute-start(f32[2048,2048]{1,0:T(8,128)} %fusion.69.refs_0_), channel_id=1, source_target_pairs={{0,1},{1,0},{2,3},{3,2},{4,5},{5,4},{6,7},{7,6}} | collective-permute-start | bytes 50331656 | tf_op jit(solution)/shard_map/ppermute | solution.py:282
Sparse Core Ops, SparseCore 0:
  9.8 163.0 all-gather.15
  176.8 297.1 all-gather.17
  657.1 155.2 all-gather.19
  814.0 155.2 all-gather.21
  971.5 155.1 all-gather.23
  1128.4 155.2 all-gather.27
  1309.1 157.0 all-gather.25

commit v4 on v3

--- a/solution.py
+++ b/solution.py
@@ -19,40 +19,40 @@
     return lax.dot_general(left_op, right_op, (((left_dim,), (right_dim,)), ((), ())), preferred_element_type=F32)
 
 
-def place_rows(buffer, pieces, starts, row_start, total_rows, total_cols, step=256):
-    rows = pieces[0].shape[0]
-    count = len(pieces)
-
-    def kernel(where_ref, *refs):
-        out_ref = refs[-1]
-        for index in range(count):
-            size = pieces[index].shape[1]
-            if isinstance(starts[index], int):
-                out_ref[:, starts[index]:starts[index] + size] = refs[index][...]
-            else:
-                out_ref[:, pl.ds(pl.multiple_of(where_ref[1 + index] * 128, 128), size)] = refs[index][...]
-
-    where = jnp.stack([jnp.asarray(row_start // step, jnp.int32)] + [jnp.asarray(s // 128, jnp.int32) for s in starts])
-    in_specs = [pl.BlockSpec((step, piece.shape[1]), lambda i, where_ref: (i, 0)) for piece in pieces]
-    operands = list(pieces)
+def place_rows(buffer, pieces, gathered, core, other_core, total, step=256):
+    half = total // 2
+    part = gathered.shape[2] // 2
+    per_block = gathered.shape[1] // step
+
+    def kernel(core_ref, own_ref, other_ref, gathered_ref, *rest):
+        out_ref = rest[-1]
+        for k, piece_ref in ((0, own_ref), (1, other_ref)):
+            low = core_ref[k] * half
+            out_ref[:, pl.ds(pl.multiple_of(low, 128), part)] = gathered_ref[0, :, k * part:(k + 1) * part]
+            out_ref[:, pl.ds(pl.multiple_of(low + part, 128), half - part)] = piece_ref[...]
+
+    cores = jnp.stack([jnp.asarray(core, jnp.int32), jnp.asarray(other_core, jnp.int32)])
+    in_specs = [pl.BlockSpec((step, half - part), lambda i, core_ref: (i, 0))] * 2
+    in_specs.append(pl.BlockSpec((1, step, 2 * part), lambda i, core_ref: (2 * (i // per_block) + core_ref[0], i % per_block, 0)))
+    operands = [*pieces, gathered]
     aliases = {}
     if buffer is not None:
         in_specs.append(pl.BlockSpec(memory_space=pl.ANY))
         operands.append(buffer)
-        aliases = {1 + count: 0}
-    return pl.pallas_call(
-        kernel,
-        out_shape=jax.ShapeDtypeStruct((total_rows, total_cols), F32),
+        aliases = {4: 0}
+    return pl.pallas_call(
+        kernel,
+        out_shape=jax.ShapeDtypeStruct((total, total), F32),
         grid_spec=pltpu.PrefetchScalarGridSpec(
             num_scalar_prefetch=1,
-            grid=(rows // step,),
+            grid=(half // step,),
             in_specs=in_specs,
-            out_specs=pl.BlockSpec((step, total_cols), lambda i, where_ref: (where_ref[0] + i, 0)),
+            out_specs=pl.BlockSpec((step, total), lambda i, core_ref: (core_ref[0] * (half // step) + i, 0)),
         ),
         input_output_aliases=aliases,
-        cost_estimate=pl.CostEstimate(flops=4 * 10**9, bytes_accessed=8 * rows * total_cols, transcendentals=0),
+        cost_estimate=pl.CostEstimate(flops=4 * 10**9, bytes_accessed=8 * half * total, transcendentals=0),
         compiler_params=pltpu.CompilerParams(vmem_limit_bytes=40 * 2**20),
-    )(where, *operands)
+    )(cores, *operands)
 
 
 def join_columns(parts, rows, order, step=256):
@@ -261,6 +261,12 @@
         grad_emb = dot(emb_b, grad_c_all, 1, 1) / row_count
         grad_emb, grad_u_2_other = barrier((grad_emb, grad_u_2_other))
 
+        act_1_part = rows_of(act_1, part_start, block)
+        mid_part = jnp.concatenate([dot(act_1_part, grad_u_2[:block], 1, 1), dot(act_1_part, grad_u_2_other[:block], 1, 1)], axis=1)
+        mid_part = with_layout_constraint(mid_part, Layout(major_to_minor=(0, 1)))
+        mid_gathered = lax.all_gather(mid_part, DATA_AXIS)
+        mid_part, grad_u_2_other = barrier((mid_part, grad_u_2_other))
+
         w_mid_rows = rows_of(w_mid, own_start + part_start, block)
         normed_1 = (rows_of(pre_1, part_start, block) - rows_of(mean_1, part_start, block)) * rows_of(inv_1, part_start, block)
         gain_1p, bias_1p = rows_of(gain_1h, part_start, block), rows_of(bias_1h, part_start, block)
@@ -278,11 +284,11 @@
         loss_value = jnp.sum(small_all[:, 4, 0])
 
         act_1, grad_w_in_part = barrier((act_1, grad_w_in_part))
-        mid_own = [dot(act_1, grad_u_2, 1, 1), dot(act_1, grad_u_2_other, 1, 1)]
+        mid_own = [dot(act_1, grad_u_2[block:], 1, 1), dot(act_1, grad_u_2_other[block:], 1, 1)]
         mid_other = [lax.ppermute(part, DATA_AXIS, pair_perm) for part in mid_own]
-        grad_w_mid = place_rows(None, mid_own, [own_start, other_start], own_start, width, width)
+        grad_w_mid = place_rows(None, mid_own, mid_gathered, core, 1 - core, width)
         mid_other[0], mid_other[1], grad_w_out = barrier((mid_other[0], mid_other[1], grad_w_out))
-        grad_w_mid = place_rows(grad_w_mid, mid_other, [other_start, own_start], other_start, width, width)
+        grad_w_mid = place_rows(grad_w_mid, mid_other, mid_gathered, 1 - core, core, width)
 
         return (loss_value, grad_emb, grad_w_in, grad_w_mid, grad_w_out, vectors[0], vectors[1], vectors[2], vectors[3])
 

time: 1600 us -> 1600 us (level)
  matrix products: 1170 us -> 1150 us
    dot_general x20 -> x22, matrix products: 1050 us -> 1030 us  [dot(): lax.dot_general(left_op, right_op, (((left_dim,), (right_dim,)), ((), ())...]
  transfers between devices with their start and end apart: 13 -> 14, of which waited for: 1 -> 2; matrix products, arithmetic and copies ran while one was open for 80% -> 79% of each run, Pallas kernels for 7% -> 6%
where the time goes in v4:
time: 1600 us; the launch traced here: 1590 us
  matrix products  1150 us (72%)
  other arithmetic  156 us (10%)
  Pallas kernels  126 us (8%)
  waiting for transfers between devices  72 us (4%)
  blocking collectives  43.5 us (3%)
  local copies, waits for them, and re-layouts  29.9 us (2%)
  between operations  16.8 us (1%)
    dot_general x22, matrix products, dot(): lax.dot_general(left_op, right_op, (((left_dim,), (right_dim,)), ((), ())...  1030 us
    dot_general x2, matrix products, teacher_layer(): normed = norm_rows(jnp.dot(layer_in, weight, preferred_element_type=F32))  69.3 us
    all_gather x5, waiting for transfers between devices, gather(): return lax.all_gather(array, DATA_AXIS, axis=0, tiled=True)  59.5 us
    convert_element_type x1, other arithmetic, affine_back(): return (grad_u.astype(BF16), jnp.concatenate([sum_gn, sum_g], axis=1))  52.9 us
    pallas_call x2, Pallas kernels, place_pieces(): pl.pallas_call(kernel, out_shape=jax.ShapeDtypeStruct((width, width), F32...  45.7 us
    dot_general x1, matrix products, local_step(): jnp.dot(teach_2, t_out, preferred_element_type=F32)  45.7 us
    all_gather x3, blocking collectives, norm_rows(): lax.all_gather(jnp.stack([jnp.sum(pre, axis=0), jnp.sum(pre * pre, axis=0...  43.5 us
    pallas_call x2, Pallas kernels, place_rows(): pl.pallas_call(kernel, out_shape=jax.ShapeDtypeStruct((total, total), F32...  43 us
  transfers between devices with their start and end apart: 14, of which 2 were waited for; matrix products, arithmetic and copies ran while one was open for 79% of the time, Pallas kernels for 6%

profile of v4, /device:TPU:0, one launch (start us, length us, event | category | flops | bytes accessed | tf_op | source)
XLA Modules:
  0.0 1592.6 jit_solution(13450998454298260441)
XLA Ops:
  8.0 23.6 %fusion.70 = (f32[4096]{0:T(1024)S(1)}, f32[4096]{0:T(1024)S(1)}, f32[1024,4096]{1,0:T(8,128)}) fusion(bf16[1024,2048]{1,0:T(8,128)(2,1)} %param.14, bf16[2048,4096]{1,0:T(8,128)(2,1)} %param.18), kind=kOutput, calls=%fused_computation.151 | convolution fusion | flops 17192443904 | bytes 37781504 | tf_op jit(solution)/shard_map/dot_general | solution.py:175
  31.6 16.2 %all-gather.6 = f32[8,2,4096]{2,1,0:T(2,128)S(1)} all-gather(f32[1,2,4096]{2,1,0:T(2,128)S(1)} %maximum_bitcast_fusion), channel_id=2, replica_groups=mesh['data'=8] {'data'}, dimensions={0}, use_global_device_ids=true | all-gather | bytes 294912 | tf_op jit(solution)/shard_map/all_gather | solution.py:169
  48.1 45.7 %fusion.69 = (f32[4096]{0:T(1024)S(1)}, f32[4096]{0:T(1024)S(1)}, f32[1024,4096]{1,0:T(8,128)}) fusion(bf16[4096,4096]{1,0:T(8,128)(2,1)} %param.19, f32[1024,4096]{1,0:T(8,128)} %get-tuple-element.114, f32[4096]{0:T(1024)S(1)} %copy-done.14, f32[4096]{0:T(1024)S(1)} %copy-done.12, f32[4096]{0:T(1024)S(1)} %bitcast.100, f32[4096]{0:T(1024)S(1)} %bitcast.99), kind=kOutput, calls=%fused_computation.150 | convolution fusion | flops 34397478912 | bytes 67207168 | tf_op jit(solution)/shard_map/dot_general | solution.py:175
  93.8 13.9 all-gather.7
  107.9 45.7 %fusion.68 = (f32[4096]{0:T(1024)S(1)}, f32[4096]{0:T(1024)S(1)}, f32[1024,4096]{1,0:T(8,128)}) fusion(bf16[4096,4096]{1,0:T(8,128)(2,1)} %param.20, f32[1024,4096]{1,0:T(8,128)} %get-tuple-element.115, f32[4096]{0:T(1024)S(1)} %copy-done.18, f32[4096]{0:T(1024)S(1)} %copy-done.16, f32[4096]{0:T(1024)S(1)} %bitcast.102, f32[4096]{0:T(1024)S(1)} %bitcast.101), kind=kOutput, calls=%fused_computation.149 | convolution fusion | flops 34397478912 | bytes 67207168 | tf_op jit(solution)/shard_map/dot_general | solution.py:197
  153.7 13.4 all-gather.8
  167.3 9.7 multiply_convert_fusion.2
  177.3 86.1 %fusion.66 = (f32[2048]{0:T(1024)S(1)}, f32[2048]{0:T(1024)S(1)}, f32[2048,8192]{1,0:T(8,128)}) fusion(bf16[8192,2048]{1,0:T(8,128)(2,1)} %all-gather.18.cloned.1.call-done, bf16[2048,4096]{1,0:T(8,128)(2,1)} %param.15, s32[]{:T(128)} %select_n.76), kind=kOutput, calls=%fused_computation.147 | convolution fusion | flops 68769808384 | bytes 109068800 | tf_op jit(solution)/shard_map/dot_general | solution.py:19
  263.4 33.3 %maximum_convert_fusion.1 = bf16[2048,8192]{1,0:T(8,128)(2,1)} fusion(f32[2048,8192]{1,0:T(8,128)} %get-tuple-element.112, f32[2048]{0:T(1024)S(1)} %dynamic-slice-done.1, f32[2048]{0:T(1024)S(1)} %dynamic-slice-done, f32[2048]{0:T(1024)S(1)} %get-tuple-element.107, f32[2048]{0:T(1024)S(1)} %get-tuple-element.106), kind=kLoop, calls=%fused_computation.7 | loop fusion | flops 100663296 | bytes 100696064 | tf_op jit(solution)/shard_map/convert_element_type | solution.py:204
  297.4 85.3 %fusion.28 = f32[2048,8192]{1,0:T(8,128)} fusion(bf16[2048,8192]{1,0:T(8,128)(2,1)} %maximum_convert_fusion.1, bf16[4096,4096]{1,0:T(8,128)(2,1)} %param.16, s32[]{:T(128)S(6)} %select_n.80), kind=kOutput, calls=%fused_computation.62 | convolution fusion | flops 68719476736 | bytes 109051904 | tf_op jit(solution)/shard_map/dot_general | solution.py:19
  382.7 95.7 %fusion.65 = (f32[2048]{0:T(1024)S(1)}, f32[2048]{0:T(1024)S(1)}, f32[2048,8192]{1,0:T(8,128)}) fusion(f32[2048,8192]{1,0:T(8,128)} %fusion.28, bf16[2048,8192]{1,0:T(8,128)(2,1)} %collective-permute-done, bf16[4096,4096]{1,0:T(8,128)(2,1)} %param.16, s32[]{:T(128)S(6)} %select_n.84, s32[]{:T(128)S(6)} %select_n.80), kind=kOutput, calls=%fused_computation.146 | convolution fusion | flops 68786585600 | bytes 176177152 | tf_op jit(solution)/shard_map/dot_general | solution.py:19
  479.1 33.5 %maximum_convert_fusion = bf16[2048,8192]{1,0:T(8,128)(2,1)} fusion(f32[2048,8192]{1,0:T(8,128)} %get-tuple-element.113, f32[2048]{0:T(1024)S(1)} %copy-done.10, f32[2048]{0:T(1024)S(1)} %get-tuple-element.89, f32[2048]{0:T(1024)S(1)} %get-tuple-element.104, f32[2048]{0:T(1024)S(1)} %get-tuple-element.105), kind=kLoop, calls=%fused_computation.3 | loop fusion | flops 100663296 | bytes 100696064 | tf_op jit(solution)/shard_map/convert_element_type | solution.py:210
  513.4 2.0 dynamic-slice.29
  515.5 14.2 shard_map.196
  529.7 28.3 %fusion.47 = f32[512,8192]{1,0:T(8,128)} fusion(bf16[2048,8192]{1,0:T(8,128)(2,1)} %maximum_convert_fusion, bf16[4096,4096]{1,0:T(8,128)(2,1)} %in_ref.1, s32[]{:T(128)S(6)} %select_n.80, s32[]{:T(128)S(6)} %select_n.86), kind=kOutput, calls=%fused_computation.87 | convolution fusion | flops 17179869184 | bytes 52428808 | tf_op jit(solution)/shard_map/dot_general | solution.py:19
  558.1 7.6 slice.91
  565.7 20.8 %fusion.74 = (f32[256]{0:T(256)S(1)}, f32[256]{0:T(256)S(1)}, f32[256,8192]{1,0:T(8,128)}) fusion(bf16[2048,8192]{1,0:T(8,128)(2,1)} %collective-permute-done.1, bf16[4096,4096]{1,0:T(8,128)(2,1)} %in_ref.1, s32[]{:T(128)S(6)} %select_n.84, s32[]{:T(128)S(6)} %select_n.86, f32[512,8192]{1,0:T(8,128)} %fusion.47), kind=kOutput, calls=%fused_computation.155 | convolution fusion | flops 8598323200 | bytes 51382280 | tf_op jit(solution)/shard_map/dot_general | solution.py:19
  586.5 29.5 %select_convert_fusion.1 = (bf16[256,4096]{1,0:T(8,128)(2,1)S(1)}, f32[]{:T(128)}) fusion(f32[]{:T(128)S(6)} %mul.362, s32[256]{0:T(256)S(1)} %iota_add_fusion.1, f32[]{:T(128)S(6)} %copy.42, bf16[8192,4096]{1,0:T(8,128)(2,1)} %all-gather.20.cloned.1.call-done, f32[256,8192]{1,0:T(8,128)} %get-tuple-element.117, f32[256]{0:T(256)S(1)} %get-tuple-element.111, ...), kind=kOutput, calls=%fused_computation.79 | convolution fusion | flops 17198743552 | bytes 77597712 | tf_op jit(solution)/shard_map/dot_general | solution.py:19
  616.1 32.7 %fusion.73 = (f32[256]{0:T(256)S(1)}, f32[256]{0:T(256)S(1)}, f32[256,8192]{1,0:T(8,128)}) fusion(f32[256]{0:T(256)S(1)} %get-tuple-element.111, f32[256,8192]{1,0:T(8,128)} %get-tuple-element.117, f32[256]{0:T(256)S(1)} %get-tuple-element.110, bf16[256,4096]{1,0:T(8,128)(2,1)S(1)} %get-tuple-element.50, bf16[8192,4096]{1,0:T(8,128)(2,1)} %all-gather.20.cloned.1.call-done), kind=kOutput, calls=%fused_computation.154 | convolution fusion | flops 17192452096 | bytes 85987328 | tf_op jit(solution)/shard_map/dot_general | solution.py:19
  648.8 8.6 multiply_convert_fusion.5
  657.4 20.0 %fusion.72 = (f32[256]{0:T(256)S(1)}, f32[256]{0:T(256)S(1)}, f32[256,8192]{1,0:T(8,128)}) fusion(f32[256,8192]{1,0:T(8,128)} %slice.91, bf16[2048,256]{1,0:T(8,128)(2,1)S(1)} %dynamic-slice.29, bf16[2048,8192]{1,0:T(8,128)(2,1)} %collective-permute-done.1), kind=kOutput, calls=%fused_computation.153 | convolution fusion | flops 8598323200 | bytes 51382272 | tf_op jit(solution)/shard_map/dot_general | solution.py:19
  677.4 30.5 %select_reduce_fusion = (f32[]{:T(128)}, bf16[256,4096]{1,0:T(8,128)(2,1)}) fusion(s32[256]{0:T(256)S(1)} %iota_add_fusion, f32[]{:T(128)S(6)} %copy.42, f32[]{:T(128)S(6)} %mul.362, bf16[8192,4096]{1,0:T(8,128)(2,1)} %all-gather.20.cloned.1.call-done, f32[256,8192]{1,0:T(8,128)} %get-tuple-element.119, f32[256]{0:T(256)S(1)} %get-tuple-element.109, ...), kind=kOutput, calls=%fused_computation.74 | convolution fusion | flops 17198743552 | bytes 77597712 | tf_op jit(solution)/shard_map/dot_general | solution.py:19
  707.9 32.6 %fusion.71 = (f32[256]{0:T(256)S(1)}, f32[256]{0:T(256)S(1)}, f32[256,8192]{1,0:T(8,128)}) fusion(f32[256]{0:T(256)S(1)} %get-tuple-element.109, f32[256,8192]{1,0:T(8,128)} %get-tuple-element.119, f32[256]{0:T(256)S(1)} %get-tuple-element.108, bf16[256,4096]{1,0:T(8,128)(2,1)} %get-tuple-element.51, bf16[8192,4096]{1,0:T(8,128)(2,1)} %all-gather.20.cloned.1.call-done), kind=kOutput, calls=%fused_computation.152 | convolution fusion | flops 17192452096 | bytes 85987328 | tf_op jit(solution)/shard_map/dot_general | solution.py:19
  740.5 8.6 multiply_convert_fusion.4
  749.2 4.0 pad_maximum_fusion
  753.3 59.4 %all-gather.22.cloned.1.call-done = bf16[2048,8192]{1,0:T(8,128)(2,1)} async-done(((bf16[256,8192]{1,0:T(8,128)(2,1)}), bf16[2048,8192]{1,0:T(8,128)(2,1)}) %all-gather.22.cloned.1.call-update) | async-done | bytes 33554448 | tf_op jit(solution)/shard_map/all_gather | solution.py:163
  812.7 79.4 %fusion.79.first_ref = f32[2048,2048]{1,0:T(8,128)} fusion(bf16[2048,8192]{1,0:T(8,128)(2,1)} %maximum_convert_fusion, bf16[2048,8192]{1,0:T(8,128)(2,1)} %all-gather.22.cloned.1.call-done), kind=kOutput, calls=%fused_computation.160 | convolution fusion | flops 68719476736 | bytes 83886080 | tf_op jit(solution)/shard_map/dot_general | solution.py:19
  892.1 79.3 %fusion.80 = f32[2048,8192]{1,0:T(8,128)} fusion(bf16[2048,2048]{1,0:T(8,128)(2,1)} %get-tuple-element.37, bf16[2048,8192]{1,0:T(8,128)(2,1)} %all-gather.22.cloned.1.call-done), kind=kOutput, calls=%fused_computation.161 | convolution fusion | flops 68719476736 | bytes 109051904 | tf_op jit(solution)/shard_map/dot_general | solution.py:19
  971.4 25.3 %fusion.15 = f32[512,2048]{1,0:T(8,128)} fusion(bf16[2048,8192]{1,0:T(8,128)(2,1)} %all-gather.24.cloned.1.call-done, bf16[2048,8192]{1,0:T(8,128)(2,1)} %maximum_convert_fusion, s32[]{:T(128)S(6)} %select_n.78), kind=kOutput, calls=%fused_computation.41 | convolution fusion | flops 17179869184 | bytes 46137348 | tf_op jit(solution)/shard_map/dot_general | solution.py:19
  996.8 112.9 %fusion.64 = (f32[2048]{0:T(1024)S(1)}, f32[2048]{0:T(1024)S(1)}, f32[2048,8192]{1,0:T(8,128)}) fusion(f32[2048]{0:T(1024)S(1)} %copy-done.2, f32[2048,8192]{1,0:T(8,128)} %get-tuple-element.113, f32[2048]{0:T(1024)S(1)} %copy-done.4, f32[2048,8192]{1,0:T(8,128)} %fusion.80, bf16[2048,2048]{1,0:T(8,128)(2,1)} %get-tuple-element.47, ...), kind=kOutput, calls=%fused_computation.145 | convolution fusion | flops 68887248896 | bytes 243318784 | tf_op jit(solution)/shard_map/dot_general | solution.py:19
  1109.8 52.9 %multiply_convert_fusion = bf16[2048,8192]{1,0:T(8,128)(2,1)} fusion(f32[2048,8192]{1,0:T(8,128)} %get-tuple-element.121, f32[2048,8192]{1,0:T(8,128)} %get-tuple-element.113, f32[2048]{0:T(1024)S(1)} %copy-done.7, f32[2048]{0:T(1024)S(1)} %broadcast_multiply_fusion.3, f32[2048]{0:T(1024)S(1)} %broadcast_multiply_fusion.4, f32[2048]{0:T(1024)S(1)} %copy-done.2, ...), kind=kLoop, calls=%fused_computation | loop fusion | flops 117440512 | bytes 167813120 | tf_op jit(solution)/shard_map/convert_element_type | solution.py:192
  1162.9 9.5 fusion.7
  1172.4 43.4 %convolution_multiply_fusion.2 = f32[1024,4096]{1,0:T(8,128)} fusion(bf16[1024,4096]{1,0:T(8,128)(2,1)} %multiply_convert_fusion.2, bf16[4096,4096]{1,0:T(8,128)(2,1)} %all-gather.26.cloned.1.call-done), kind=kOutput, calls=%fused_computation.29 | convolution fusion | flops 34363932672 | bytes 58720256 | tf_op jit(solution)/shard_map/dot_general | solution.py:19
  1215.8 11.7 collective-permute-done.2
  1227.5 9.5 fusion.13
  1237.0 1.6 pad_maximum_fusion.1
  1241.6 27.8 %fusion.49 = f32[512,8192]{1,0:T(8,128)} fusion(bf16[2048,8192]{1,0:T(8,128)(2,1)} %multiply_convert_fusion, bf16[4096,4096]{1,0:T(8,128)(2,1)} %param.16, s32[]{:T(128)S(6)} %select_n.82, s32[]{:T(128)S(6)} %select_n.80), kind=kOutput, calls=%fused_computation.89 | convolution fusion | flops 17179869184 | bytes 52428808 | tf_op jit(solution)/shard_map/dot_general | solution.py:19
  1269.4 32.5 %fusion.67 = (f32[512]{0:T(512)S(1)}, f32[512]{0:T(512)S(1)}, f32[512,8192]{1,0:T(8,128)}) fusion(f32[512]{0:T(512)S(1)} %get-tuple-element.87, f32[512]{0:T(512)S(1)} %dynamic-slice.21, f32[2048,8192]{1,0:T(8,128)} %get-tuple-element.112, s32[]{:T(128)S(6)} %select_n.78, f32[512,8192]{1,0:T(8,128)} %fusion.49, ...), kind=kOutput, calls=%fused_computation.148 | convolution fusion | flops 17221812224 | bytes 85995536 | tf_op jit(solution)/shard_map/dot_general | solution.py:19
  1301.9 29.6 %fusion.45 = f32[2048,512]{1,0:T(8,128)} fusion(bf16[8192,2048]{1,0:T(8,128)(2,1)} %all-gather.18.cloned.1.call-done, f32[512,8192]{1,0:T(8,128)} %get-tuple-element.122, f32[2048,8192]{1,0:T(8,128)} %get-tuple-element.112, s32[]{:T(128)S(6)} %select_n.78, f32[512]{0:T(512)S(1)} %get-tuple-element.85, f32[512]{0:T(512)S(1)} %get-tuple-element.87, ...), kind=kOutput, calls=%fused_computation.84 | convolution fusion | flops 17209229312 | bytes 71313408 | tf_op jit(solution)/shard_map/dot_general | solution.py:19
  1331.5 10.7 concatenate.19
  1342.5 60.7 %fusion.2.other_ref = f32[2048,1536]{1,0:T(8,128)} fusion(bf16[2048,8192]{1,0:T(8,128)(2,1)} %maximum_convert_fusion.1, bf16[2048,8192]{1,0:T(8,128)(2,1)} %collective-permute-done.2), kind=kOutput, calls=%fused_computation.12 | convolution fusion | flops 51539607552 | bytes 71303168 | tf_op jit(solution)/shard_map/dot_general | solution.py:19
  1403.2 60.9 %fusion.own_ref = f32[2048,1536]{1,0:T(8,128)} fusion(bf16[2048,8192]{1,0:T(8,128)(2,1)} %maximum_convert_fusion.1, bf16[2048,8192]{1,0:T(8,128)(2,1)} %multiply_convert_fusion), kind=kOutput, calls=%fused_computation.10 | convolution fusion | flops 51539607552 | bytes 71303168 | tf_op jit(solution)/shard_map/dot_general | solution.py:19
  1464.8 22.9 %shard_map.198.rest_0_ = f32[4096,4096]{1,0:T(8,128)} custom-call(s32[1]{0:T(128)} %bitcast.core_ref, f32[2048,2048]{1,0:T(8,128)} %fusion.79.first_ref, f32[8,512,2048]{2,1,0:T(8,128)} %bitcast.82), custom_call_target="tpu_custom_call" | custom-call | flops 4000000000 | bytes 67108864 | tf_op jit(solution)/shard_map/pallas_call | solution.py:122
  1487.7 22.9 %shard_map.199 = f32[4096,4096]{1,0:T(8,128)} custom-call(s32[1]{0:T(128)} %bitcast.23.core_ref, f32[2048,2048]{1,0:T(8,128)} %collective-permute-done.5.first_ref, f32[8,512,2048]{2,1,0:T(8,128)} %bitcast.83, f32[4096,4096]{1,0:T(8,128)} %shard_map.198.rest_0_), custom_call_target="tpu_custom_call", output_to_operand_aliasing={{}: (3, {})} | custom-call | flops 4000000000 | bytes 67108864 | tf_op jit(solution)/shard_map/pallas_call | solution.py:122
  1510.6 4.6 copy-done
  1515.2 20.0 %shard_map.200.rest_0_ = f32[4096,4096]{1,0:T(8,128)} custom-call(s32[2]{0:T(128)S(1)} %pad_add_fusion.1.core_ref, f32[2048,1536]{1,0:T(8,128)S(1)} %copy-done, f32[2048,1536]{1,0:T(8,128)} %fusion.2.other_ref, f32[8,512,1024]{2,1,0:T(8,128)} %bitcast.84), custom_call_target="tpu_custom_call" | custom-call | flops 4000000000 | bytes 67108864 | tf_op jit(solution)/shard_map/pallas_call | solution.py:43
  1535.2 23.0 %shard_map.201 = f32[4096,4096]{1,0:T(8,128)} custom-call(s32[2]{0:T(128)S(1)} %pad_add_fusion.core_ref, f32[2048,1536]{1,0:T(8,128)} %collective-permute-done.3.own_ref, f32[2048,1536]{1,0:T(8,128)} %collective-permute-done.4.other_ref, f32[8,512,1024]{2,1,0:T(8,128)} %bitcast.85, f32[4096,4096]{1,0:T(8,128)} %shard_map.200.rest_0_), custom_call_target="tpu_custom_call", output_to_operand_aliasing={{}: (4, {})} | custom-call | flops 4000000000 | bytes 67108864 | tf_op jit(solution)/shard_map/pallas_call | solution.py:43
  1558.2 22.5 %shard_map.197 = f32[2048,4096]{1,0:T(8,128)} custom-call(f32[8,2056,512]{2,1,0:T(8,128)} %bitcast.86), custom_call_target="tpu_custom_call" | custom-call | flops 4000000000 | bytes 67371008 | tf_op jit(solution)/shard_map/pallas_call | solution.py:65
  (119 shorter events, 11.2 us)
Async XLA Ops:
  7.2 170.0 %all-gather.18.cloned.1.call-start = ((), (), s32[]{:S(2)}) async-start(), calls=%async_computation | async-start | bytes 37748736 | tf_op jit(solution)/shard_map/all_gather | solution.py:163
  7.9 40.1 %copy-start.12 = (f32[4096]{0:T(1024)S(1)}, f32[4096]{0:T(1024)}, u32[]{:S(2)}) copy-start(f32[4096]{0:T(1024)} %param.21) | copy-start | bytes 49156
  7.9 40.1 %copy-start.14 = (f32[4096]{0:T(1024)S(1)}, f32[4096]{0:T(1024)}, u32[]{:S(2)}) copy-start(f32[4096]{0:T(1024)} %param.22) | copy-start | bytes 49156
  7.9 578.6 %all-gather.20.cloned.1.call-start = ((), (), s32[]{:S(2)}) async-start(), calls=%async_computation.1 | async-start | bytes 75497472 | tf_op jit(solution)/shard_map/all_gather | solution.py:163
  48.0 59.8 %copy-start.16 = (f32[4096]{0:T(1024)S(1)}, f32[4096]{0:T(1024)}, u32[]{:S(2)}) copy-start(f32[4096]{0:T(1024)} %param.23) | copy-start | bytes 49156
  48.1 59.8 %copy-start.18 = (f32[4096]{0:T(1024)S(1)}, f32[4096]{0:T(1024)}, u32[]{:S(2)}) copy-start(f32[4096]{0:T(1024)} %param.24) | copy-start | bytes 49156
  177.0 635.8 %all-gather.22.cloned.1.call-start = ((), (), s32[]{:S(2)}) async-start(), calls=%async_computation.2 | async-start | bytes 37748736 | tf_op jit(solution)/shard_map/all_gather | solution.py:163
  177.2 86.1 %dynamic-slice-start = ((f32[4096]{0:T(1024)}, s32[]{:T(128)}), f32[2048]{0:T(1024)S(1)}, s32[]{:S(2)}) async-start(f32[4096]{0:T(1024)} %param.21, s32[]{:T(128)} %select_n.76), calls=%async_computation.8 | async-start | bytes 16896 | tf_op jit(solution)/shard_map/dynamic-slice
  177.2 86.1 %dynamic-slice-start.1 = ((f32[4096]{0:T(1024)}, s32[]{:T(128)}), f32[2048]{0:T(1024)S(1)}, s32[]{:S(2)}) async-start(f32[4096]{0:T(1024)} %param.22, s32[]{:T(128)} %select_n.76), calls=%async_computation.9 | async-start | bytes 16896 | tf_op jit(solution)/shard_map/dynamic-slice.2
  263.4 33.4 %copy-start.5 = (f32[2048]{0:T(1024)}, f32[2048]{0:T(1024)S(1)}, u32[]{:S(2)}) copy-start(f32[2048]{0:T(1024)S(1)} %get-tuple-element.107) | copy-start | bytes 24580
  263.4 33.4 %copy-start.6 = (f32[2048]{0:T(1024)}, f32[2048]{0:T(1024)S(1)}, u32[]{:S(2)}) copy-start(f32[2048]{0:T(1024)S(1)} %get-tuple-element.106) | copy-start | bytes 24580
  263.4 33.4 %copy-start.19 = (f32[4096]{0:T(1024)S(1)}, f32[4096]{0:T(1024)}, u32[]{:S(2)}) copy-start(f32[4096]{0:T(1024)} %param.24) | copy-start | bytes 49156
  296.8 86.0 %collective-permute-start = (bf16[2048,8192]{1,0:T(8,128)(2,1)}, bf16[2048,8192]{1,0:T(8,128)(2,1)}, u32[]{:S(2)}, u32[]{:S(2)}) collective-permute-start(bf16[2048,8192]{1,0:T(8,128)(2,1)} %maximum_convert_fusion.1), channel_id=1, source_target_pairs={{0,1},{1,0},{2,3},{3,2},{4,5},{5,4},{6,7},{7,6}} | collective-permute-start | bytes 100663304 | tf_op jit(solution)/shard_map/ppermute | solution.py:205
  382.7 95.7 %copy-start.17 = (f32[4096]{0:T(1024)S(1)}, f32[4096]{0:T(1024)}, u32[]{:S(2)}) copy-start(f32[4096]{0:T(1024)} %param.23) | copy-start | bytes 49156
  382.7 96.3 %copy-start.10 = (f32[2048]{0:T(1024)S(1)}, f32[2048]{0:T(1024)}, u32[]{:S(2)}) copy-start(f32[2048]{0:T(1024)} %dynamic-slice.27) | copy-start | bytes 24580
  479.1 33.5 %copy-start.1 = (f32[2048]{0:T(1024)}, f32[2048]{0:T(1024)S(1)}, u32[]{:S(2)}) copy-start(f32[2048]{0:T(1024)S(1)} %get-tuple-element.104) | copy-start | bytes 24580
  479.1 33.5 %copy-start.3 = (f32[2048]{0:T(1024)}, f32[2048]{0:T(1024)S(1)}, u32[]{:S(2)}) copy-start(f32[2048]{0:T(1024)S(1)} %get-tuple-element.105) | copy-start | bytes 24580
  479.1 33.5 %copy-start.8 = (f32[2048]{0:T(1024)}, f32[2048]{0:T(1024)S(1)}, u32[]{:S(2)}) copy-start(f32[2048]{0:T(1024)S(1)} %get-tuple-element.89) | copy-start | bytes 24580
  512.6 53.1 %collective-permute-start.1 = (bf16[2048,8192]{1,0:T(8,128)(2,1)}, bf16[2048,8192]{1,0:T(8,128)(2,1)}, u32[]{:S(2)}, u32[]{:S(2)}) collective-permute-start(bf16[2048,8192]{1,0:T(8,128)(2,1)} %maximum_convert_fusion), channel_id=1, source_target_pairs={{0,1},{1,0},{2,3},{3,2},{4,5},{5,4},{6,7},{7,6}} | collective-permute-start | bytes 100663304 | tf_op jit(solution)/shard_map/ppermute | solution.py:211
  657.4 314.0 %all-gather.24.cloned.1.call-start = ((), (), s32[]{:S(2)}) async-start(), calls=%async_computation.3 | async-start | bytes 37748736 | tf_op jit(solution)/shard_map/all_gather | solution.py:163
  749.2 423.3 %all-gather.26.cloned.1.call-start = ((), (), s32[]{:S(2)}) async-start(), calls=%async_computation.4 | async-start | bytes 37748736 | tf_op jit(solution)/shard_map/all_gather | solution.py:163
  753.2 711.6 %all-gather.30.cloned.1.call-start = ((), (), s32[]{:S(2)}) async-start(), calls=%async_computation.6 | async-start | bytes 37748736 | tf_op jit(solution)/shard_map/all_gather | solution.py:253
  971.4 25.4 %copy-start.2 = (f32[2048]{0:T(1024)S(1)}, f32[2048]{0:T(1024)}, u32[]{:S(2)}) copy-start(f32[2048]{0:T(1024)} %copy-done.1) | copy-start | bytes 24580
  971.4 25.4 %copy-start.4 = (f32[2048]{0:T(1024)S(1)}, f32[2048]{0:T(1024)}, u32[]{:S(2)}) copy-start(f32[2048]{0:T(1024)} %copy-done.3) | copy-start | bytes 24580
  971.4 25.4 %copy-start.9 = (f32[2048]{0:T(1024)S(1)}, f32[2048]{0:T(1024)}, u32[]{:S(2)}) copy-start(f32[2048]{0:T(1024)} %copy-done.8) | copy-start | bytes 24580
  971.4 25.4 %copy-start.11 = (f32[2048]{0:T(1024)S(1)}, f32[2048]{0:T(1024)}, u32[]{:S(2)}) copy-start(f32[2048]{0:T(1024)} %dynamic-slice.27) | copy-start | bytes 24580
  996.7 513.9 %all-gather.32.cloned.1.call-start = ((), (), s32[]{:S(2)}) async-start(), calls=%async_computation.7 | async-start | bytes 18874368 | tf_op jit(solution)/shard_map/all_gather | solution.py:267
  996.8 112.9 %copy-start.7 = (f32[2048]{0:T(1024)S(1)}, f32[2048]{0:T(1024)}, u32[]{:S(2)}) copy-start(f32[2048]{0:T(1024)} %get-tuple-element.88) | copy-start | bytes 24580
  1162.7 64.8 %collective-permute-start.2 = (bf16[2048,8192]{1,0:T(8,128)(2,1)}, bf16[2048,8192]{1,0:T(8,128)(2,1)}, u32[]{:S(2)}, u32[]{:S(2)}) collective-permute-start(bf16[2048,8192]{1,0:T(8,128)(2,1)} %multiply_convert_fusion), channel_id=1, source_target_pairs={{0,1},{1,0},{2,3},{3,2},{4,5},{5,4},{6,7},{7,6}} | collective-permute-start | bytes 100663304 | tf_op jit(solution)/shard_map/ppermute | solution.py:259
  1215.8 22.8 %copy-start.15 = (f32[4096]{0:T(1024)S(1)}, f32[4096]{0:T(1024)}, u32[]{:S(2)}) copy-start(f32[4096]{0:T(1024)} %param.22) | copy-start | bytes 49156
  1215.8 23.7 %copy-start.13 = (f32[4096]{0:T(1024)S(1)}, f32[4096]{0:T(1024)}, u32[]{:S(2)}) copy-start(f32[4096]{0:T(1024)} %param.21) | copy-start | bytes 49156
  1238.6 319.6 %all-gather.28.cloned.1.call-start = ((), (), s32[]{:S(2)}) async-start(), calls=%async_computation.5 | async-start | bytes 37896192 | tf_op jit(solution)/shard_map/all_gather | solution.py:279
  1342.2 145.4 %collective-permute-start.5 = (f32[2048,2048]{1,0:T(8,128)}, f32[2048,2048]{1,0:T(8,128)}, u32[]{:S(2)}, u32[]{:S(2)}) collective-permute-start(f32[2048,2048]{1,0:T(8,128)} %fusion.79.first_ref), channel_id=1, source_target_pairs={{0,1},{1,0},{2,3},{3,2},{4,5},{5,4},{6,7},{7,6}} | collective-permute-start | bytes 50331656 | tf_op jit(solution)/shard_map/ppermute | solution.py:252
  1464.1 46.4 %collective-permute-start.4 = (f32[2048,1536]{1,0:T(8,128)}, f32[2048,1536]{1,0:T(8,128)}, u32[]{:S(2)}, u32[]{:S(2)}) collective-permute-start(f32[2048,1536]{1,0:T(8,128)} %fusion.2.other_ref), channel_id=1, source_target_pairs={{0,1},{1,0},{2,3},{3,2},{4,5},{5,4},{6,7},{7,6}} | collective-permute-start | bytes 37748744 | tf_op jit(solution)/shard_map/ppermute | solution.py:288
  1464.4 46.1 %collective-permute-start.3 = (f32[2048,1536]{1,0:T(8,128)}, f32[2048,1536]{1,0:T(8,128)}, u32[]{:S(2)}, u32[]{:S(2)}) collective-permute-start(f32[2048,1536]{1,0:T(8,128)} %fusion.own_ref), channel_id=1, source_target_pairs={{0,1},{1,0},{2,3},{3,2},{4,5},{5,4},{6,7},{7,6}} | collective-permute-start | bytes 37748744 | tf_op jit(solution)/shard_map/ppermute | solution.py:288
  1510.6 4.6 copy-start
Sparse Core Ops, SparseCore 0:
  9.8 163.0 all-gather.17
  177.1 297.1 all-gather.19
  657.5 155.1 all-gather.21
  814.4 155.2 all-gather.23
  971.9 155.1 all-gather.25
  1128.8 155.2 all-gather.29
  1285.9 85.1 all-gather.31
  1373.0 157.0 all-gather.27
